TPU v7x, 256 devices: a whole 4x4x8 slice. The times are simulated.
256 devices in a mesh: grp: 32 (over z, x), mem: 8 (over y, core).
Axes of the slice: x: 4, y: 4, z: 8, core: 2. Of those that a mesh axis runs over, the one named last changes fastest.
Arguments:
- right_side: float32 [32, 524288], P(None, ('grp', 'mem')), may hold values from -6 to 6
- fine_tiles: float32 [4096, 3, 128, 128], P(('grp', 'mem')), may hold values from -0.13492627 to 6.130239
- fine_columns: int32 [4096, 3], P(('grp', 'mem')), may hold values from 0 to 19, as said below
- fine_sends: int32 [512, 256], P(('grp', 'mem')), may hold values from 0 to 2047, as said below
- fine_weights: float32 [524288], P(('grp', 'mem')), may hold values from 0.5 to 2
- fine_groups: int32 [524288], P(('grp', 'mem')), may hold values from 0 to 255, as said below
- group_tiles: float32 [512, 3, 128, 128], P('grp'), may hold values from -1.0794102 to 49.0419102
- group_columns: int32 [512, 3], P('grp'), may hold values from 0 to 17, as said below
- group_sends: int32 [64, 128], P('grp'), may hold values from 0 to 2047, as said below
- group_weights: float32 [65536], P('grp'), may hold values from 0.5 to 2
- group_groups: int32 [65536], P('grp'), may hold values from 0 to 63, as said below
- coarse_tiles: float32 [16, 3, 128, 128], replicated, may hold values from -2.1588203 to 98.08382034355964
- coarse_columns: int32 [16, 3], replicated, may hold values from 0 to 15, as said below
Outputs:
- solution: float32 [32, 524288], P(None, ('grp', 'mem'))
- residual: float32 [32, 524288], P(None, ('grp', 'mem'))
Inputs may be any that keep to these rules, and one draw needn't show every extreme that they name: `fine_columns`: fine tiles: within each owner's 16 tile rows, entry 0 is the tile row's own index; entries 1 each name a distinct block of the extended vector (16 own blocks, then 2 from the lower neighbour, then 2 from the higher), and so do entries 2; every halo block is named by entries 2. `fine_sends`: each list holds 256 distinct rows of its owner; list 2 o goes to owner o - 1, list 2 o + 1 to owner o + 1. `fine_groups`: each aggregate of an owner takes exactly 8 of its rows. `group_columns`: as for fine_columns, per group, with 16 tile rows and 2 halo blocks. `group_sends`: each list holds 128 distinct rows of its group. `group_groups`: each aggregate of a group takes exactly 32 of its rows. `coarse_columns`: entry 0 is the tile row's own index; entries 1 name each block once, and so do entries 2.
All inputs are finite; a program needn't handle non-finite values.
Results may differ from a plain program's by a relative error of at most 0.0003.
Values sent between devices are 32-bit elements; how exact they have to be, the bound alone decides.
No kernel may reach another device: no remote copies, remote signals or barrier semaphores. Data moves between devices by JAX's collectives and lax.ppermute only.
A program may use at most 128 MiB of HBM per device.

v0:
```python
import jax
import jax.numpy as jnp
from jax import lax
from jax.sharding import Mesh
from jax.sharding import PartitionSpec as P

AGG1 = 8
AGG2 = 32
ITERS = 2
GRP_MEM = ("grp_0", "grp_1", "mem_0", "mem_1")
GRP = ("grp_0", "grp_1")
MEM = ("mem_0", "mem_1")


RELAXATION = 0.7


def padded(shard, sides, width):
    edges = {}
    for axis, dim in sides:
        count, length = (lax.axis_size(axis), shard.shape[dim])
        up = [(i, (i + 1) % count) for i in range(count - 1)]
        last = lax.slice_in_dim(shard, length - width, length, axis=dim)
        leading = lax.slice_in_dim(shard, 0, width, axis=dim)
        edges[dim] = (
            lax.ppermute(last, axis, up),
            lax.ppermute(leading, axis, [(b, a) for a, b in up]),
        )
    done = []
    for _, dim in sides:
        low, high = edges[dim]
        around = [(width, width) if d in done else (0, 0) for d in range(shard.ndim)]
        shard = jnp.concatenate([jnp.pad(low, around), shard, jnp.pad(high, around)], axis=dim)
        done.append(dim)
    return shard


def with_halo(shard, sides, width):
    for axis, dim in sides:
        count, length = (lax.axis_size(axis), shard.shape[dim])
        up = [(i, (i + 1) % count) for i in range(count - 1)]
        down = [(j, i) for i, j in up]
        last = lax.slice_in_dim(shard, length - width, length, axis=dim)
        leading = lax.slice_in_dim(shard, 0, width, axis=dim)
        before = lax.ppermute(last, axis, up)
        after = lax.ppermute(leading, axis, down)
        shard = jnp.concatenate([before, shard, after], axis=dim)
    return shard


def over_axes(shard, axes):
    for axis in axes:
        shard = lax.psum(shard, axis)
    return shard


def joined_along(parts, dim):
    dims = list(parts.shape[1:])
    dims[dim] *= parts.shape[0]
    return jnp.moveaxis(parts, 0, dim).reshape(dims)


def copy_for_each(shard, axis):
    copies = jnp.broadcast_to(shard, (lax.axis_size(axis), *shard.shape))
    return lax.all_to_all(copies, axis, split_axis=0, concat_axis=0, tiled=True)


def gathered_copies(shard, axis, dim):
    return joined_along(copy_for_each(shard, axis), dim)


def tile_apply(tile_set, tile_cols, extended):
    tile_width = tile_set.shape[2]
    blocks = extended.reshape(extended.shape[0], -1, tile_width)
    picked = blocks[:, tile_cols, :]
    result = jnp.einsum("bkij,nbkj->nbi", tile_set, picked, precision=lax.Precision.HIGHEST)
    return result.reshape(extended.shape[0], -1)


def scaled_inverse(tile_set, tile_cols):
    block_count = tile_set.shape[0]
    own_mask = (tile_cols == jnp.arange(block_count, dtype=jnp.int32)[:, None]).astype(
        tile_set.dtype
    )
    diagonal = jnp.sum(own_mask[:, :, None] * jnp.diagonal(tile_set, axis1=2, axis2=3), axis=1)
    return (RELAXATION / diagonal).reshape(-1)


def aggregate_table(agg_map, coarse_count):
    return (agg_map[:, None] == jnp.arange(coarse_count, dtype=jnp.int32)[None, :]).astype(
        jnp.float32
    )


def restrict_rows(values, weights, agg_table):
    return jnp.dot(values * weights, agg_table, precision=lax.Precision.HIGHEST)


def prolong_rows(values, weights, agg_table):
    return weights * jnp.einsum("nc,rc->nr", values, agg_table, precision=lax.Precision.HIGHEST)


def fine_extend(values, send_lists):
    halo_rows = send_lists.shape[1]
    outgoing = jnp.concatenate([values[:, send_lists[0]], values[:, send_lists[1]]], axis=1)
    widened = padded(outgoing, ((GRP_MEM, 1),), halo_rows)
    return jnp.concatenate([values, widened[:, :halo_rows], widened[:, 3 * halo_rows :]], axis=1)


def group_extend(values, send_lists):
    halo_rows = send_lists.shape[1]
    outgoing = jnp.concatenate([values[:, send_lists[0]], values[:, send_lists[1]]], axis=1)
    widened = with_halo(outgoing, ((GRP, 1),), halo_rows)
    return jnp.concatenate([values, widened[:, :halo_rows], widened[:, 3 * halo_rows :]], axis=1)


def inner_sum(first_vec, second_vec):
    return jnp.sum(first_vec * second_vec, axis=1)


def joined_products(residual, precond, images, direction, along):
    return (
        over_axes(inner_sum(residual, precond), GRP_MEM),
        over_axes(inner_sum(precond, images), GRP_MEM),
        over_axes(inner_sum(precond, along), GRP_MEM),
        over_axes(inner_sum(direction, images), GRP_MEM),
    )


def shards(
    right_side,
    fine_tiles,
    fine_columns,
    fine_sends,
    fine_weights,
    fine_groups,
    group_tiles,
    group_columns,
    group_sends,
    group_weights,
    group_groups,
    coarse_tiles,
    coarse_columns,
):
    fine_count = fine_weights.shape[0] // AGG1
    group_length = group_weights.shape[0]
    coarse_share = group_length // AGG2
    fine_table = aggregate_table(fine_groups, fine_count)
    group_table = aggregate_table(group_groups, coarse_share)
    fine_scale = scaled_inverse(fine_tiles, fine_columns)
    group_scale = scaled_inverse(group_tiles, group_columns)
    coarse_scale = scaled_inverse(coarse_tiles, coarse_columns)

    def fine_apply(values):
        return tile_apply(fine_tiles, fine_columns, fine_extend(values, fine_sends))

    def group_apply(values):
        return tile_apply(group_tiles, group_columns, group_extend(values, group_sends))

    residual = right_side
    solution = jnp.zeros_like(right_side)
    direction = jnp.zeros_like(right_side)
    along = jnp.zeros_like(right_side)
    curv_sum = jnp.zeros((right_side.shape[0],), jnp.float32)
    energy = jnp.ones((right_side.shape[0],), jnp.float32)
    for iteration in range(ITERS):
        fine_iter = fine_scale * residual
        fine_left = residual - fine_apply(fine_iter)
        lowered = restrict_rows(fine_left, fine_weights, fine_table)
        group_rhs = gathered_copies(lowered, MEM, 1)
        group_iter = group_scale * group_rhs
        group_left = group_rhs - group_apply(group_iter)
        coarse_part = restrict_rows(group_left, group_weights, group_table)
        coarse_rhs = gathered_copies(coarse_part, GRP, 1)
        coarse_iter = coarse_scale * coarse_rhs
        coarse_iter = coarse_iter + coarse_scale * (
            coarse_rhs - tile_apply(coarse_tiles, coarse_columns, coarse_iter)
        )
        raised = lax.dynamic_slice_in_dim(
            coarse_iter, lax.axis_index(GRP) * coarse_share, coarse_share, 1
        )
        group_iter = group_iter + prolong_rows(raised, group_weights, group_table)
        group_iter = group_iter + group_scale * (group_rhs - group_apply(group_iter))
        spread = lax.dynamic_slice_in_dim(
            group_iter, lax.axis_index(MEM) * fine_count, fine_count, 1
        )
        fine_iter = fine_iter + prolong_rows(spread, fine_weights, fine_table)
        precond = fine_iter + fine_scale * (residual - fine_apply(fine_iter))
        images = fine_apply(precond)
        fresh, own_curv, cross_first, cross_second = joined_products(
            residual, precond, images, direction, along
        )
        if iteration == 0:
            beta_ratio = jnp.zeros_like(fresh)
        else:
            beta_ratio = fresh / energy
        direction = precond + beta_ratio[:, None] * direction
        along = images + beta_ratio[:, None] * along
        curv_sum = (
            own_curv
            + beta_ratio * (cross_first + cross_second)
            + beta_ratio * beta_ratio * curv_sum
        )
        step_size = (fresh / curv_sum)[:, None]
        solution = solution + step_size * direction
        residual = residual - step_size * along
        energy = fresh
    return (solution, residual)


def solution(mesh):
    finer = Mesh(mesh.devices.reshape(8, 4, 4, 2), ("grp_0", "grp_1", "mem_0", "mem_1"))
    return jax.shard_map(
        shards,
        mesh=finer,
        in_specs=(
            P(None, GRP_MEM),
            P(GRP_MEM, None, None, None),
            P(GRP_MEM, None),
            P(GRP_MEM, None),
            P(GRP_MEM),
            P(GRP_MEM),
            P(GRP, None, None, None),
            P(GRP, None),
            P(GRP, None),
            P(GRP),
            P(GRP),
            P(),
            P(),
        ),
        out_specs=(P(None, GRP_MEM), P(None, GRP_MEM)),
        check_vma=False,
    )
```

profile of v0, /device:TPU:1, one launch (start us, length us, event | category | flops | bytes accessed | tf_op | source)
XLA Modules:
  0.0 538.3 jit_solution(96542499755285463)
XLA Ops:
  3.4 18.4 %copy.219 = f32[16,3,128,128]{0,1,3,2:T(4,128)} copy(f32[16,3,128,128]{3,2,1,0:T(8,128)} %param.14) | data formatting | bytes 6291456 | tf_op args[1]
  40.9 16.7 %copy.221 = f32[16,3,128,128]{0,1,3,2:T(4,128)} copy(f32[16,3,128,128]{3,2,1,0:T(8,128)S(1)} %copy-done.1) | data formatting | bytes 6291456 | tf_op args[6]
  70.1 5.0 all-to-all-start
  99.4 5.6 %convolution_bitcast_fusion.9 = f32[16,4,8,128]{3,2,1,0:T(8,128)S(1)} fusion(f32[32,16,3,128]{3,0,2,1:T(8,128)} %bitcast.320, f32[16,3,128,128]{3,2,1,0:T(8,128)} %param.19), kind=kOutput, calls=%fused_computation.55 | convolution fusion | flops 301989888 | bytes 4194304 | tf_op jit(solution)/shard_map/bkij,nbkj->nbi/dot_general | solution.py:76
  108.5 16.4 %all-to-all-start.1 = ((f32[32,1,2048]{2,1,0:T(1,128)}), f32[32,1,2048]{2,1,0:T(1,128)S(1)}, u32[]{:S(2)}, u32[]{:S(2)}) async-start(f32[32,1,2048]{2,1,0:T(1,128)} %reshape.581), calls=%async_computation.1 | async-start | bytes 524288 | tf_op jit(solution)/shard_map/all_to_all | solution.py:65
  125.2 18.4 %copy.239 = f32[16,3,128,128]{0,1,3,2:T(4,128)} copy(f32[16,3,128,128]{3,2,1,0:T(8,128)} %param.24) | data formatting | bytes 6291456 | tf_op args[11]
  160.3 5.6 %convolution_bitcast_fusion.8 = f32[16,4,8,128]{3,2,1,0:T(8,128)S(1)} fusion(f32[32,16,3,128]{3,0,2,1:T(8,128)} %bitcast.321, f32[16,3,128,128]{3,2,1,0:T(8,128)} %param.24), kind=kOutput, calls=%fused_computation.54 | convolution fusion | flops 301989888 | bytes 4194304 | tf_op jit(solution)/shard_map/bkij,nbkj->nbi/dot_general | solution.py:76
  184.6 5.6 %convolution_bitcast_fusion.7 = f32[16,4,8,128]{3,2,1,0:T(8,128)S(1)} fusion(f32[32,16,3,128]{3,0,2,1:T(8,128)} %bitcast.322, f32[16,3,128,128]{3,2,1,0:T(8,128)} %param.19), kind=kOutput, calls=%fused_computation.53 | convolution fusion | flops 301989888 | bytes 4194304 | tf_op jit(solution)/shard_map/bkij,nbkj->nbi/dot_general | solution.py:76
  200.6 6.5 %collective-permute-start.6 = (f32[32,256]{1,0:T(8,128)S(1)}, f32[32,256]{1,0:T(8,128)S(1)}, u32[]{:S(2)}, u32[]{:S(2)}) collective-permute-start(f32[32,256]{1,0:T(8,128)S(1)} %bitcast.355), channel_id=1, source_target_pairs={{0,1},{1,2},{2,3},{3,4},{4,5},{5,6},{6,7},{7,8},{8,9},{9,10},{10,1... | collective-permute-start | bytes 98312 | tf_op jit(solution)/shard_map/ppermute | solution.py:26
  214.9 4.6 convolution_bitcast_fusion.6
  238.3 4.7 fusion.39
  243.9 15.7 %all-reduce.1 = (f32[32]{0:T(128)S(1)}, f32[32]{0:T(128)S(1)}, f32[32]{0:T(128)S(1)}) all-reduce(f32[32]{0:T(128)S(1)} %get-tuple-element.8, f32[32]{0:T(128)S(1)} %get-tuple-element.7, f32[32]{0:T(128)S(1)} %add.232), channel_id=1, replica_groups=mesh['grp_0'=8,'grp_1'=4,'mem_0'=4,'mem_1'=2] {'grp_0'}, use_global_device_ids=true, to_apply=%region_4.5 | all-reduce | flops 96 | bytes 768 | tf_op jit(solution)/shard_map/psum | solution.py:53
  259.6 9.3 %all-reduce.5 = (f32[32]{0:T(128)S(1)}, f32[32]{0:T(128)S(1)}, f32[32]{0:T(128)S(1)}) all-reduce(f32[32]{0:T(128)S(1)} %get-tuple-element.12, f32[32]{0:T(128)S(1)} %get-tuple-element.13, f32[32]{0:T(128)S(1)} %get-tuple-element.14), channel_id=1, replica_groups=mesh['grp_0'=8,'grp_1'=4,'mem_0'=4,'mem_1'=2] {'grp_1'}, use_global_device_ids=true, to_apply=%region_5.6 | all-reduce | flops 96 | bytes 768 | tf_op jit(solution)/shard_map/psum | solution.py:53
  268.9 18.0 %all-reduce.3 = (f32[32]{0:T(128)S(1)}, f32[32]{0:T(128)S(1)}, f32[32]{0:T(128)S(1)}) all-reduce(f32[32]{0:T(128)S(1)} %get-tuple-element.24, f32[32]{0:T(128)S(1)} %get-tuple-element.25, f32[32]{0:T(128)S(1)} %get-tuple-element.26), channel_id=1, replica_groups=mesh['grp_0'=8,'grp_1'=4,'mem_0'=4,'mem_1'=2] {'mem_0'}, use_global_device_ids=true, to_apply=%region_6.7 | all-reduce | flops 96 | bytes 768 | tf_op jit(solution)/shard_map/psum | solution.py:53
  318.9 12.4 %all_to_all.20 = f32[8,32,256]{2,1,0:T(8,128)S(1)} all-to-all(f32[8,32,256]{2,1,0:T(8,128)S(1)} %broadcast_in_dim.30), channel_id=1, replica_groups=mesh['grp_0'=8,'grp_1'=4,'mem_0'=4,'mem_1'=2] {'mem_0','mem_1'}, dimensions={0} | all-to-all | bytes 524288 | tf_op jit(solution)/shard_map/all_to_all | solution.py:65
  351.2 5.6 %convolution_bitcast_fusion.4 = f32[16,4,8,128]{3,2,1,0:T(8,128)S(1)} fusion(f32[32,16,3,128]{3,0,2,1:T(8,128)} %bitcast.325, f32[16,3,128,128]{3,2,1,0:T(8,128)} %param.19), kind=kOutput, calls=%fused_computation.50 | convolution fusion | flops 301989888 | bytes 4194304 | tf_op jit(solution)/shard_map/bkij,nbkj->nbi/dot_general | solution.py:76
  360.4 25.7 %all_to_all.21 = f32[32,1,2048]{2,1,0:T(1,128)} all-to-all(f32[32,1,2048]{2,1,0:T(1,128)} %reshape.583), channel_id=1, replica_groups=mesh['grp_0'=8,'grp_1'=4,'mem_0'=4,'mem_1'=2] {'grp_0','grp_1'}, dimensions={0} | all-to-all | bytes 524288 | tf_op jit(solution)/shard_map/all_to_all | solution.py:65
  401.1 5.6 %convolution_bitcast_fusion.3 = f32[16,4,8,128]{3,2,1,0:T(8,128)S(1)} fusion(f32[32,16,3,128]{3,0,2,1:T(8,128)} %bitcast.316, f32[16,3,128,128]{3,2,1,0:T(8,128)} %param.24), kind=kOutput, calls=%fused_computation.49 | convolution fusion | flops 301989888 | bytes 4194304 | tf_op jit(solution)/shard_map/bkij,nbkj->nbi/dot_general | solution.py:76
  426.6 5.6 %convolution_bitcast_fusion.2 = f32[16,4,8,128]{3,2,1,0:T(8,128)S(1)} fusion(f32[32,16,3,128]{3,0,2,1:T(8,128)} %bitcast.317, f32[16,3,128,128]{3,2,1,0:T(8,128)} %param.19), kind=kOutput, calls=%fused_computation.48 | convolution fusion | flops 301989888 | bytes 4194304 | tf_op jit(solution)/shard_map/bkij,nbkj->nbi/dot_general | solution.py:76
  444.4 6.8 %collective-permute-start.16 = (f32[32,256]{1,0:T(8,128)S(1)}, f32[32,256]{1,0:T(8,128)S(1)}, u32[]{:S(2)}, u32[]{:S(2)}) collective-permute-start(f32[32,256]{1,0:T(8,128)S(1)} %bitcast.358), channel_id=1, source_target_pairs={{0,1},{1,2},{2,3},{3,4},{4,5},{5,6},{6,7},{7,8},{8,9},{9,10},{10,1... | collective-permute-start | bytes 98312 | tf_op jit(solution)/shard_map/ppermute | solution.py:26
  486.9 4.6 convolution_bitcast_fusion
  492.3 14.7 %all-reduce = (f32[32]{0:T(128)S(1)}, f32[32]{0:T(128)S(1)}, f32[32]{0:T(128)S(1)}) all-reduce(f32[32]{0:T(128)S(1)} %get-tuple-element.5, f32[32]{0:T(128)S(1)} %get-tuple-element.3, f32[32]{0:T(128)S(1)} %add.239), channel_id=1, replica_groups=mesh['grp_0'=8,'grp_1'=4,'mem_0'=4,'mem_1'=2] {'grp_0'}, use_global_device_ids=true, to_apply=%region_24.25 | all-reduce | flops 96 | bytes 768 | tf_op jit(solution)/shard_map/psum | solution.py:53
  507.0 8.1 %all-reduce.4 = (f32[32]{0:T(128)S(1)}, f32[32]{0:T(128)S(1)}, f32[32]{0:T(128)S(1)}) all-reduce(f32[32]{0:T(128)S(1)} %get-tuple-element.9, f32[32]{0:T(128)S(1)} %get-tuple-element.10, f32[32]{0:T(128)S(1)} %get-tuple-element.11), channel_id=1, replica_groups=mesh['grp_0'=8,'grp_1'=4,'mem_0'=4,'mem_1'=2] {'grp_1'}, use_global_device_ids=true, to_apply=%region_25.26 | all-reduce | flops 96 | bytes 768 | tf_op jit(solution)/shard_map/psum | solution.py:53
  515.1 17.4 %all-reduce.2 = (f32[32]{0:T(128)S(1)}, f32[32]{0:T(128)S(1)}, f32[32]{0:T(128)S(1)}) all-reduce(f32[32]{0:T(128)S(1)} %get-tuple-element.21, f32[32]{0:T(128)S(1)} %get-tuple-element.22, f32[32]{0:T(128)S(1)} %get-tuple-element.23), channel_id=1, replica_groups=mesh['grp_0'=8,'grp_1'=4,'mem_0'=4,'mem_1'=2] {'mem_0'}, use_global_device_ids=true, to_apply=%region_26.27 | all-reduce | flops 96 | bytes 768 | tf_op jit(solution)/shard_map/psum | solution.py:53
  (333 shorter events, 279.3 us)
Async XLA Ops:
  30.9 29.7 %collective-permute-start = (f32[32,256]{1,0:T(8,128)S(1)}, f32[32,256]{1,0:T(8,128)S(1)}, u32[]{:S(2)}, u32[]{:S(2)}) collective-permute-start(f32[32,256]{1,0:T(8,128)S(1)} %bitcast.349), channel_id=1, source_target_pairs={{0,1},{1,2},{2,3},{3,4},{4,5},{5,6},{6,7},{7,8},{8,9},{9,10},{10,1... | collective-permute-start | bytes 98312 | tf_op jit(solution)/shard_map/ppermute | solution.py:26
  38.2 23.1 %collective-permute-start.1 = (f32[32,256]{1,0:T(8,128)}, f32[32,256]{1,0:T(8,128)}, u32[]{:S(2)}, u32[]{:S(2)}) collective-permute-start(f32[32,256]{1,0:T(8,128)} %bitcast.10), channel_id=1, source_target_pairs={{1,0},{2,1},{3,2},{4,3},{5,4},{6,5},{7,6},{8,7},{9,8},{10,9},{11,1... | collective-permute-start | bytes 98312 | tf_op jit(solution)/shard_map/ppermute | solution.py:27
  70.1 11.5 %all-to-all-start = ((f32[8,32,256]{2,1,0:T(8,128)}), f32[8,32,256]{2,1,0:T(8,128)S(1)}, u32[]{:S(2)}, u32[]{:S(2)}) async-start(f32[8,32,256]{2,1,0:T(8,128)} %broadcast_in_dim.25), calls=%async_computation | async-start | bytes 524288 | tf_op jit(solution)/shard_map/all_to_all | solution.py:65
  88.3 6.3 %collective-permute-start.2 = (f32[32,128]{1,0:T(8,128)}, f32[32,128]{1,0:T(8,128)S(1)}, u32[]{:S(2)}, u32[]{:S(2)}) collective-permute-start(f32[32,128]{1,0:T(8,128)} %bitcast.363), channel_id=1, source_target_pairs={{0,8},{8,16},{16,24},{24,32},{32,40},{40,48},{48,56},{56,64},{64,7... | collective-permute-start | bytes 49160 | tf_op jit(solution)/shard_map/ppermute | solution.py:45
  92.4 4.5 collective-permute-start.3
  108.5 38.9 %all-to-all-start.1 = ((f32[32,1,2048]{2,1,0:T(1,128)}), f32[32,1,2048]{2,1,0:T(1,128)S(1)}, u32[]{:S(2)}, u32[]{:S(2)}) async-start(f32[32,1,2048]{2,1,0:T(1,128)} %reshape.581), calls=%async_computation.1 | async-start | bytes 524288 | tf_op jit(solution)/shard_map/all_to_all | solution.py:65
  174.4 5.0 collective-permute-start.4
  177.6 4.5 collective-permute-start.5
  200.6 8.5 %collective-permute-start.6 = (f32[32,256]{1,0:T(8,128)S(1)}, f32[32,256]{1,0:T(8,128)S(1)}, u32[]{:S(2)}, u32[]{:S(2)}) collective-permute-start(f32[32,256]{1,0:T(8,128)S(1)} %bitcast.355), channel_id=1, source_target_pairs={{0,1},{1,2},{2,3},{3,4},{4,5},{5,6},{6,7},{7,8},{8,9},{9,10},{10,1... | collective-permute-start | bytes 98312 | tf_op jit(solution)/shard_map/ppermute | solution.py:26
  207.1 5.2 collective-permute-start.7
  228.0 4.3 collective-permute-start.8
  229.9 5.2 collective-permute-start.9
  301.6 4.3 collective-permute-start.10
  303.9 5.2 collective-permute-start.11
  340.6 3.3 collective-permute-start.12
  342.6 4.5 collective-permute-start.13
  416.0 3.3 collective-permute-start.14
  417.9 4.5 collective-permute-start.15
  444.4 9.0 %collective-permute-start.16 = (f32[32,256]{1,0:T(8,128)S(1)}, f32[32,256]{1,0:T(8,128)S(1)}, u32[]{:S(2)}, u32[]{:S(2)}) collective-permute-start(f32[32,256]{1,0:T(8,128)S(1)} %bitcast.358), channel_id=1, source_target_pairs={{0,1},{1,2},{2,3},{3,4},{4,5},{5,6},{6,7},{7,8},{8,9},{9,10},{10,1... | collective-permute-start | bytes 98312 | tf_op jit(solution)/shard_map/ppermute | solution.py:26
  451.3 5.2 collective-permute-start.17
  475.6 4.3 collective-permute-start.18
  477.5 5.2 collective-permute-start.19
  486.9 48.8 %copy-start.53 = (f32[32]{0:T(128)S(1)}, f32[32]{0:T(128)}, u32[]{:S(2)}) copy-start(f32[32]{0:T(128)} %copy-done.52) | copy-start | bytes 388
  486.9 48.8 %copy-start.49 = (f32[32]{0:T(128)S(1)}, f32[32]{0:T(128)}, u32[]{:S(2)}) copy-start(f32[32]{0:T(128)} %copy-done.48) | copy-start | bytes 388
  (66 other events, 733.6 us)
where the time goes:
time: 549 us; the launch traced here: 538 us
  local copies, waits for them, and re-layouts  194 us (35%)
  blocking collectives  128 us (23%)
  starting transfers between devices  75.3 us (14%)
  matrix products  72.3 us (13%)
  other arithmetic  35.6 us (6%)
  waiting for transfers between devices  30.9 us (6%)
    psum x8, blocking collectives, over_axes(): shard = lax.psum(shard, axis)  89.7 us
    unnamed x143, local copies, waits for them, and re-layouts  64.8 us
    dot_general x12, matrix products, tile_apply(): jnp.einsum('bkij,nbkj->nbi', tile_set, picked, precision=lax.Precision.HI...  61 us
    all_to_all x2, blocking collectives, copy_for_each(): return lax.all_to_all(copies, axis, split_axis=0, concat_axis=0, tiled=True)  38.1 us
    gather x12, local copies, waits for them, and re-layouts, tile_apply(): picked = blocks[:, tile_cols, :]  24.8 us
    ppermute x6, starting transfers between devices, padded(): lax.ppermute(last, axis, up)  24.2 us
    all_to_all x2, starting transfers between devices, copy_for_each(): return lax.all_to_all(copies, axis, split_axis=0, concat_axis=0, tiled=True)  21.4 us
    gather x12, local copies, waits for them, and re-layouts, fine_extend(): values[:, send_lists[0]]  20.7 us
  transfers between devices with their start and end apart: 22, of which 10 were waited for; matrix products, arithmetic and copies ran while one was open for 9% of the time, Pallas kernels for 0%

commit v1 on v0

v1 whole, which is shorter than its diff:
```python
import functools

import jax
import jax.numpy as jnp
from jax import lax
from jax.experimental import pallas as pl
from jax.experimental.pallas import tpu as pltpu
from jax.sharding import Mesh
from jax.sharding import PartitionSpec as P

TILE = 128
AGG1 = 8
AGG2 = 32
ALL = ("grp_0", "grp_1", "mem_0", "mem_1")
GRP = ("grp_0", "grp_1")
MEM = ("mem_0", "mem_1")
RELAXATION = 0.7
F32 = jnp.float32
BF16 = jnp.bfloat16
VMEM_SPEC = pl.BlockSpec(memory_space=pltpu.VMEM)
SMEM_SPEC = pl.BlockSpec(memory_space=pltpu.SMEM)
LIMIT = 24 * 1024 * 1024


def shape(dims, dtype=F32):
    return jax.ShapeDtypeStruct(tuple(dims), dtype)


def run(kernel, name, outs, args, smem=(), scratch=(), flops=4_000_000_000):
    specs = [SMEM_SPEC if i in smem else VMEM_SPEC for i in range(len(args))]
    return pl.pallas_call(
        kernel,
        name=name,
        out_shape=tuple(outs),
        in_specs=specs,
        out_specs=tuple(VMEM_SPEC for _ in outs),
        scratch_shapes=list(scratch),
        compiler_params=pltpu.CompilerParams(vmem_limit_bytes=LIMIT),
        cost_estimate=pl.CostEstimate(flops=flops, transcendentals=0, bytes_accessed=4_000_000),
    )(*args)


def halves(value):
    high = value.astype(BF16)
    low = (value - high.astype(F32)).astype(BF16)
    return high, low


def stacked(value):
    high, low = halves(value)
    return jnp.concatenate([high, low], axis=0)


def doubled(value):
    both = stacked(value)
    return jnp.concatenate([both, both], axis=1)


def joined(both):
    rows = both.shape[0] // 2
    return both[:rows] + both[rows:]


def dot_nt(left, right):
    return lax.dot_general(left, right, (((1,), (1,)), ((), ())), preferred_element_type=F32)


def dot_nn(left, right):
    return lax.dot_general(left, right, (((1,), (0,)), ((), ())), preferred_element_type=F32)


def select_nn(value, onehot):
    return joined(dot_nn(stacked(value), onehot))


def select_nt(value, onehot):
    return joined(dot_nt(stacked(value), onehot))


def fill_blocks(blocks, value, first=0):
    for i in range(value.shape[1] // TILE):
        blocks[first + i] = doubled(value[:, i * TILE : (i + 1) * TILE])


def tile_rows(columns, weights, blocks, store, count, unroll=4):
    def step(i, carry):
        for j in range(unroll):
            b = i * unroll + j
            acc = dot_nt(blocks[columns[b, 0]], weights[b * 3])
            acc += dot_nt(blocks[columns[b, 1]], weights[b * 3 + 1])
            acc += dot_nt(blocks[columns[b, 2]], weights[b * 3 + 2])
            store(b, joined(acc))
        return carry

    lax.fori_loop(0, count // unroll, step, 0)


def lane_block(b):
    return pl.ds(pl.multiple_of(b * TILE, TILE), TILE)


def halo_rows(columns, weights, halo_blocks, image, own_blocks):
    def step(b, carry):
        for k in (1, 2):
            col = columns[b, k]

            @pl.when(col >= own_blocks)
            def _():
                acc = dot_nt(halo_blocks[col - own_blocks], weights[b * 3 + k])
                image[:, lane_block(b)] += joined(acc)

        return carry

    lax.fori_loop(0, own_blocks, step, 0)


def diagonal_scale(columns, tiles, scale):
    count = tiles.shape[0]
    rows = lax.broadcasted_iota(jnp.int32, (TILE, TILE), 0)
    lanes = lax.broadcasted_iota(jnp.int32, (TILE, TILE), 1)
    eye = rows == lanes

    def diagonal(b, k):
        return jnp.sum(jnp.where(eye, tiles[b, k], 0.0), axis=0, keepdims=True)

    for b in range(count):
        here = slice(b * TILE, (b + 1) * TILE)
        scale[:, here] = diagonal(b, 0)
        for k in (1, 2):

            @pl.when(columns[b, k] == b)
            def _():
                scale[:, here] += diagonal(b, k)

    scale[...] = RELAXATION / scale[...]


def pack_tile(tile):
    high, low = halves(tile)
    return jnp.concatenate([high, low], axis=1)


def onehot_by_lane(index_row, rows):
    place = lax.broadcasted_iota(jnp.int32, (rows, index_row.shape[1]), 0)
    return jnp.where(place == index_row, 1.0, 0.0).astype(BF16)


def first_kernel(columns, tiles, sends, source, scale, start, low_out, high_out, picks):
    diagonal_scale(columns, tiles, scale)
    rows = picks.shape[0]
    chunk = 256
    for i in range(rows // chunk):
        place = lax.broadcasted_iota(jnp.int32, (chunk, sends.shape[1]), 0) + i * chunk
        picks[i * chunk : (i + 1) * chunk, :] = jnp.where(place == sends[...], 1.0, 0.0).astype(BF16)
    begin = scale[...] * source[...]
    start[...] = begin
    out = select_nn(begin, picks[...])
    width = low_out.shape[1]
    low_out[...] = out[:, :width]
    high_out[...] = out[:, width:]


def pack_fine_kernel(tiles, groups, weights, table):
    for b in range(tiles.shape[0]):
        for k in range(3):
            weights[b * 3 + k] = pack_tile(tiles[b, k])
    table[...] = onehot_by_lane(groups[...], table.shape[0])


def inner_kernel(columns, weights, value, image, blocks):
    own = value.shape[1] // TILE
    fill_blocks(blocks, value[...])
    zero = jnp.zeros(blocks.shape[1:], BF16)
    for i in range(own, blocks.shape[0]):
        blocks[i] = zero

    def store(b, row):
        image[:, lane_block(b)] = row

    tile_rows(columns, weights, blocks, store, own)


def group_setup_kernel(
    place, columns, tiles, sends, weights, groups, ccolumns, ctiles,
    scale, packed, picks, table, cscale, cpacked, edge_low, edge_high,
):
    diagonal_scale(columns, tiles, scale)
    for b in range(tiles.shape[0]):
        for k in range(3):
            packed[b * 3 + k] = pack_tile(tiles[b, k])
    picks[...] = onehot_by_lane(sends[...], picks.shape[0])
    table[...] = onehot_by_lane(groups[...], table.shape[0])
    diagonal_scale(ccolumns, ctiles, cscale)
    for t in range(2):
        row = place[2 + t]
        for k in range(3):
            cpacked[t * 3 + k] = pack_tile(ctiles[row, k])
    length = weights.shape[1]
    numbers = groups[...].astype(F32)
    lines = lax.broadcasted_iota(jnp.int32, (8, length), 0)
    facts = jnp.where(lines == 0, weights[...], jnp.where(lines == 1, numbers, 0.0))
    picked = select_nn(facts, picks[...])
    half = edge_low.shape[1]
    edge_low[...] = picked[:, :half]
    edge_high[...] = picked[:, half:]


def group_edges_kernel(place, weights, groups, from_low, from_high, wide_weights, raise_table):
    length = weights.shape[1]
    half = from_low.shape[1]
    wide_weights[:, :length] = weights[...]
    wide_weights[:, length : length + half] = from_low[0:1, :]
    wide_weights[:, length + half :] = from_high[0:1, :]
    base = place[4]
    rows = raise_table.shape[0]
    raise_table[:, :length] = onehot_by_lane(groups[...] + base, rows)
    low = from_low[1:2, :].astype(jnp.int32) + (base - 64)
    high = from_high[1:2, :].astype(jnp.int32) + (base + 64)
    raise_table[:, length : length + half] = onehot_by_lane(low, rows)
    raise_table[:, length + half :] = onehot_by_lane(high, rows)


def restrict_kernel(
    columns, weights, image, from_low, from_high, source, agg_weights, table, extra, lowered,
    blocks, total,
):
    own = source.shape[1] // TILE
    fill_blocks(blocks, from_low[...])
    fill_blocks(blocks, from_high[...], from_low.shape[1] // TILE)
    total[...] = image[...]
    halo_rows(columns, weights, blocks, total, own)
    left = (source[...] - total[...]) * agg_weights[...]
    coarse = select_nt(left, table[...])
    width = table.shape[0]
    for i in range(lowered.shape[0]):
        lowered[i, :, :width] = coarse
        lowered[i, :, width:] = extra[...]


def group_start_kernel(gathered, scale, picks, group_rhs, start, low_out, high_out, extra):
    members = gathered.shape[0]
    width = group_rhs.shape[1] // members
    total = gathered[0, :, width:]
    for i in range(members):
        group_rhs[:, i * width : (i + 1) * width] = gathered[i, :, :width]
        if i:
            total += gathered[i, :, width:]
    extra[...] = total
    begin = scale[...] * group_rhs[...]
    start[...] = begin
    out = select_nn(begin, picks[...])
    half = low_out.shape[1]
    low_out[...] = out[:, :half]
    high_out[...] = out[:, half:]


def group_restrict_kernel(
    columns, weights, image, from_low, from_high, source, agg_weights, table, extra, payload,
    blocks, total,
):
    own = source.shape[1] // TILE
    fill_blocks(blocks, from_low[...])
    fill_blocks(blocks, from_high[...], from_low.shape[1] // TILE)
    total[...] = image[...]
    halo_rows(columns, weights, blocks, total, own)
    left = (source[...] - total[...]) * agg_weights[...]
    coarse = select_nt(left, table[...])
    half = coarse.shape[0] // 2
    packed = jnp.concatenate([coarse[:half, :64], coarse[half:, :64]], axis=1)
    lanes = lax.broadcasted_iota(jnp.int32, (8, TILE), 1)
    sums = jnp.zeros((8, TILE), F32)
    for j in range(4):
        part = jnp.where(lanes < 2, extra[8 * j : 8 * j + 8, :], 0.0)
        sums += pltpu.roll(part, 2 * j, 1) if j else part
    message = jnp.concatenate([packed, sums], axis=0)
    for i in range(payload.shape[0]):
        payload[i] = message


def coarse_kernel(
    place, ccolumns, columns, gathered, cscale, cpacked, own_start, from_low, from_high,
    group_rhs, scale, packed, wide_weights, raise_table, fine_start, fine_weights, fine_table,
    picks, fine_next, low_out, high_out, totals, blocks,
):
    lanes = lax.broadcasted_iota(jnp.int32, (16, TILE), 1)

    def block(t):
        first = gathered[2 * t, :16, :]
        second = gathered[2 * t + 1, :16, :]
        top = jnp.where(lanes < 64, first, pltpu.roll(second, 64, 1))
        bottom = jnp.where(lanes < 64, pltpu.roll(first, 64, 1), second)
        return jnp.concatenate([top, bottom], axis=0)

    sums = gathered[0, 16:24, :]
    for i in range(1, gathered.shape[0]):
        sums += gathered[i, 16:24, :]
    totals[...] = jnp.concatenate(
        [sums] + [pltpu.roll(sums, TILE - 2 * j, 1) for j in range(1, 4)], axis=0
    )
    solved = []
    for t in range(2):
        row = place[2 + t]
        acc = jnp.zeros((64, TILE), F32)
        for k in range(3):
            col = ccolumns[row, k]
            acc += dot_nt(doubled(cscale[col] * block(col)), cpacked[t * 3 + k])
        mine = block(row)
        iterate = cscale[row] * mine
        solved.append(iterate + cscale[row] * (mine - joined(acc)))
    pair = jnp.concatenate(solved, axis=1)
    raised = select_nn(pair, raise_table[...]) * wide_weights[...]
    length = own_start.shape[1]
    half = from_low.shape[1]
    now = own_start[...] + raised[:, :length]
    fill_blocks(blocks, now)
    fill_blocks(blocks, from_low[...] + raised[:, length : length + half], length // TILE)
    fill_blocks(
        blocks, from_high[...] + raised[:, length + half :], (length + half) // TILE
    )
    member = place[1]
    iterate_rows = []
    for j in range(2):
        b = member * 2 + j
        acc = dot_nt(blocks[columns[b, 0]], packed[b * 3])
        acc += dot_nt(blocks[columns[b, 1]], packed[b * 3 + 1])
        acc += dot_nt(blocks[columns[b, 2]], packed[b * 3 + 2])
        at = lane_block(b)
        mine = own_start[:, at]
        twice = blocks[b]
        current = twice[:32, :TILE].astype(F32) + twice[32:, :TILE].astype(F32)
        iterate_rows.append(current + scale[:, at] * (group_rhs[:, at] - joined(acc)))
    spread = jnp.concatenate(iterate_rows, axis=1)
    following = fine_start[...] + fine_weights[...] * select_nn(spread, fine_table[...])
    fine_next[...] = following
    out = select_nn(following, picks[...])
    width = low_out.shape[1]
    low_out[...] = out[:, :width]
    high_out[...] = out[:, width:]


def smooth_kernel(
    columns, weights, image, from_low, from_high, iterate, scale, source, picks,
    smoothed, low_out, high_out, blocks, total,
):
    own = source.shape[1] // TILE
    fill_blocks(blocks, from_low[...])
    fill_blocks(blocks, from_high[...], from_low.shape[1] // TILE)
    total[...] = image[...]
    halo_rows(columns, weights, blocks, total, own)
    value = iterate[...] + scale[...] * (source[...] - total[...])
    smoothed[...] = value
    out = select_nn(value, picks[...])
    width = low_out.shape[1]
    low_out[...] = out[:, :width]
    high_out[...] = out[:, width:]


def image_kernel(
    columns, weights, image, from_low, from_high, scale, residual, value, picks,
    product, start, low_out, high_out, extra, blocks,
):
    own = value.shape[1] // TILE
    fill_blocks(blocks, from_low[...])
    fill_blocks(blocks, from_high[...], from_low.shape[1] // TILE)
    product[...] = image[...]
    halo_rows(columns, weights, blocks, product, own)
    total = product[...]
    begin = scale[...] * total
    start[...] = begin
    out = select_nn(begin, picks[...])
    width = low_out.shape[1]
    low_out[...] = out[:, :width]
    high_out[...] = out[:, width:]
    energy = jnp.sum(residual[...] * value[...], axis=1, keepdims=True)
    curve = jnp.sum(value[...] * total, axis=1, keepdims=True)
    lanes = lax.broadcasted_iota(jnp.int32, (32, TILE), 1)
    extra[...] = jnp.where(lanes == 0, energy, jnp.where(lanes == 1, curve, 0.0))


def last_image_kernel(
    columns, weights, image, from_low, from_high, totals, residual, value, product, second,
    next_residual, next_value, next_product, partial, blocks, total,
):
    own = value.shape[1] // TILE
    fill_blocks(blocks, from_low[...])
    fill_blocks(blocks, from_high[...], from_low.shape[1] // TILE)
    total[...] = image[...]
    halo_rows(columns, weights, blocks, total, own)
    step = totals[:, 0:1] / totals[:, 1:2]
    left = residual[...] - step * product[...]
    fresh = value[...] - step * second[...]
    reach = product[...] - step * total[...]
    next_residual[...] = left
    next_value[...] = fresh
    next_product[...] = reach
    new = jnp.sum(left * fresh, axis=1, keepdims=True)
    own_curve = jnp.sum(fresh * reach, axis=1, keepdims=True)
    cross = jnp.sum(fresh * product[...] + value[...] * reach, axis=1, keepdims=True)
    lanes = lax.broadcasted_iota(jnp.int32, (32, TILE), 1)
    partial[...] = jnp.where(
        lanes == 0, new, jnp.where(lanes == 1, own_curve, jnp.where(lanes == 2, cross, 0.0))
    )


def sum_copies_kernel(parts, copies):
    total = parts[0]
    for i in range(1, parts.shape[0]):
        total += parts[i]
    for i in range(copies.shape[0]):
        copies[i] = total


def final_kernel(
    parts, totals, value, product, left, fresh, reach, solution, residual,
):
    sums = parts[0]
    for i in range(1, parts.shape[0]):
        sums += parts[i]
    energy = totals[:, 0:1]
    curve = totals[:, 1:2]
    step = energy / curve
    new = sums[:, 0:1]
    ratio = new / energy
    second_curve = sums[:, 1:2] + ratio * sums[:, 2:3] + ratio * ratio * curve
    second_step = new / second_curve
    solution[...] = step * value[...] + second_step * (fresh[...] + ratio * value[...])
    residual[...] = left[...] - second_step * (reach[...] + ratio * product[...])


def neighbours(low_out, high_out, axes):
    count = lax.axis_size(axes)
    up = [(i, i + 1) for i in range(count - 1)]
    down = [(b, a) for a, b in up]
    return lax.ppermute(high_out, axes, up), lax.ppermute(low_out, axes, down)


def exchanged(copies, axes):
    return lax.all_to_all(copies, axes, split_axis=0, concat_axis=0, tiled=True)


def shards(
    right_side,
    fine_tiles,
    fine_columns,
    fine_sends,
    fine_weights,
    fine_groups,
    group_tiles,
    group_columns,
    group_sends,
    group_weights,
    group_groups,
    coarse_tiles,
    coarse_columns,
):
    rhs, length = right_side.shape
    fine_count = length // AGG1
    group_length = group_weights.shape[0]
    share = group_length // AGG2
    members = lax.axis_size(MEM)
    group_total = lax.axis_size(GRP)
    fine_half = fine_sends.shape[1]
    group_half = group_sends.shape[1]
    fine_halo = 2 * fine_half // TILE
    group_halo = 2 * group_half // TILE
    fine_blocks = length // TILE
    group_blocks = group_length // TILE
    coarse_blocks = coarse_tiles.shape[0]

    fine_sends = fine_sends.reshape(1, -1)
    group_sends = group_sends.reshape(1, -1)
    fine_weights = fine_weights.reshape(1, -1)
    fine_groups = fine_groups.reshape(1, -1)
    group_weights = group_weights.reshape(1, -1)
    group_groups = group_groups.reshape(1, -1)

    grp = lax.axis_index(GRP)
    mem = lax.axis_index(MEM)
    row_a = jnp.maximum((grp - 1) // 2, 0)
    row_b = jnp.minimum(row_a + 1, coarse_blocks - 1)
    place = jnp.stack([grp, mem, row_a, row_b, grp * share - row_a * TILE]).astype(jnp.int32)

    block_scratch = pltpu.VMEM((fine_halo, 2 * rhs, 2 * TILE), BF16)
    group_block_scratch = pltpu.VMEM((group_halo, 2 * rhs, 2 * TILE), BF16)
    total_scratch = pltpu.VMEM((rhs, length), F32)
    edge = shape((rhs, fine_half))
    group_edge = shape((rhs, group_half))
    field = shape((rhs, length))

    fine_scale, fine_start, low_out, high_out, fine_picks = run(
        first_kernel, "first",
        [shape((1, length)), field, edge, edge, shape((length, 2 * fine_half), BF16)],
        (fine_columns, fine_tiles, fine_sends, right_side), smem=(0,),
    )
    before, after = neighbours(low_out, high_out, ALL)
    fine_packed, fine_table = run(
        pack_fine_kernel, "pack_fine",
        [shape((3 * fine_blocks, TILE, 2 * TILE), BF16), shape((fine_count, length), BF16)],
        (fine_tiles, fine_groups),
    )

    (group_scale, group_packed, group_picks, group_table, coarse_scale, coarse_packed,
     edge_low, edge_high) = run(
        group_setup_kernel, "group_setup",
        [
            shape((1, group_length)),
            shape((3 * group_blocks, TILE, 2 * TILE), BF16),
            shape((group_length, 2 * group_half), BF16),
            shape((TILE, group_length), BF16),
            shape((1, coarse_blocks * TILE)),
            shape((6, TILE, 2 * TILE), BF16),
            shape((8, group_half)),
            shape((8, group_half)),
        ],
        (place, group_columns, group_tiles, group_sends, group_weights, group_groups,
         coarse_columns, coarse_tiles),
        smem=(0, 1, 6),
    )
    coarse_scale = coarse_scale.reshape(coarse_blocks, 1, TILE)
    edge_before, edge_after = neighbours(edge_low, edge_high, GRP)
    wide_weights, raise_table = run(
        group_edges_kernel, "group_edges",
        [shape((1, group_length + 2 * group_half)),
         shape((2 * TILE, group_length + 2 * group_half), BF16)],
        (place, group_weights, group_groups, edge_before, edge_after), smem=(0,),
    )

    def inner(value):
        return run(
            inner_kernel, "inner", [field], (fine_columns, fine_packed, value), smem=(0,),
            scratch=[pltpu.VMEM((fine_blocks + fine_halo, 2 * rhs, 2 * TILE), BF16)],
        )[0]

    def group_inner(value):
        return run(
            inner_kernel, "group_inner", [field], (group_columns, group_packed, value), smem=(0,),
            scratch=[pltpu.VMEM((group_blocks + group_halo, 2 * rhs, 2 * TILE), BF16)],
        )[0]

    def vcycle(source, fine_start, before, after, extra):
        image = inner(fine_start)
        lowered = run(
            restrict_kernel, "restrict", [shape((members, rhs, fine_count + TILE))],
            (fine_columns, fine_packed, image, before, after, source, fine_weights, fine_table,
             extra),
            smem=(0,), scratch=[block_scratch, total_scratch],
        )[0]
        gathered = exchanged(lowered, MEM)
        group_rhs, group_start, low_out, high_out, extra = run(
            group_start_kernel, "group_start",
            [field, field, group_edge, group_edge, shape((rhs, TILE))],
            (gathered, group_scale, group_picks),
        )
        g_before, g_after = neighbours(low_out, high_out, GRP)
        image = group_inner(group_start)
        payload = run(
            group_restrict_kernel, "group_restrict", [shape((group_total, 24, TILE))],
            (group_columns, group_packed, image, g_before, g_after, group_rhs, group_weights,
             group_table, extra),
            smem=(0,), scratch=[group_block_scratch, total_scratch],
        )[0]
        gathered = exchanged(payload, GRP)
        fine_next, low_out, high_out, totals = run(
            coarse_kernel, "coarse", [field, edge, edge, shape((rhs, TILE))],
            (place, coarse_columns, group_columns, gathered, coarse_scale, coarse_packed,
             group_start, g_before, g_after, group_rhs, group_scale, group_packed, wide_weights,
             raise_table, fine_start, fine_weights, fine_table, fine_picks),
            smem=(0, 1, 2),
            scratch=[pltpu.VMEM((group_blocks + group_halo, 2 * rhs, 2 * TILE), BF16)],
        )
        before, after = neighbours(low_out, high_out, ALL)
        image = inner(fine_next)
        smoothed, low_out, high_out = run(
            smooth_kernel, "smooth", [field, edge, edge],
            (fine_columns, fine_packed, image, before, after, fine_next, fine_scale, source,
             fine_picks),
            smem=(0,), scratch=[block_scratch, total_scratch],
        )
        before, after = neighbours(low_out, high_out, ALL)
        image = inner(smoothed)
        return smoothed, image, before, after, totals

    nothing = jnp.zeros((rhs, TILE), F32)
    value, image, before, after, _ = vcycle(right_side, fine_start, before, after, nothing)
    product, start, low_out, high_out, extra = run(
        image_kernel, "image", [field, field, edge, edge, shape((rhs, TILE))],
        (fine_columns, fine_packed, image, before, after, fine_scale, right_side, value,
         fine_picks),
        smem=(0,), scratch=[block_scratch],
    )
    before, after = neighbours(low_out, high_out, ALL)
    second, image, before, after, totals = vcycle(product, start, before, after, extra)
    left, fresh, reach, partial = run(
        last_image_kernel, "last_image", [field, field, field, shape((rhs, TILE))],
        (fine_columns, fine_packed, image, before, after, totals, right_side, value, product,
         second),
        smem=(0,), scratch=[block_scratch, total_scratch],
    )
    copies = jnp.broadcast_to(partial, (members, rhs, TILE))
    copies = run(
        sum_copies_kernel, "sum_copies", [shape((group_total, rhs, TILE))],
        (exchanged(copies, MEM),),
    )[0]
    parts = exchanged(copies, GRP)
    solution, residual = run(
        final_kernel, "final", [field, field],
        (parts, totals, value, product, left, fresh, reach),
    )
    return solution, residual


def solution(mesh):
    finer = Mesh(mesh.devices.reshape(8, 4, 4, 2), ALL)
    return jax.shard_map(
        shards,
        mesh=finer,
        in_specs=(
            P(None, ALL),
            P(ALL, None, None, None),
            P(ALL, None),
            P(ALL, None),
            P(ALL),
            P(ALL),
            P(GRP, None, None, None),
            P(GRP, None),
            P(GRP, None),
            P(GRP),
            P(GRP),
            P(),
            P(),
        ),
        out_specs=(P(None, ALL), P(None, ALL)),
        check_vma=False,
    )
```

time: 549 us -> 253 us (0.46); the launches traced: 538 us -> 251 us
  local copies, waits for them, and re-layouts: 194 us -> 24.6 us
  matrix products: 72.3 us -> 0 us
  Pallas kernels: 0 us -> 48.6 us
  blocking collectives: 128 us -> 89 us
  other arithmetic: 35.6 us -> 0 us
  waiting for transfers between devices: 30.9 us -> 13.5 us
    gather x55 -> x0, local copies, waits for them, and re-layouts: 93.1 us -> none  [the longest x12 24.8 us: tile_apply(): picked = blocks[:, tile_cols, :]]
    psum x8 -> x0, blocking collectives: 89.7 us -> none  [over_axes(): shard = lax.psum(shard, axis)]
    dot_general x20 -> x0, matrix products: 72.3 us -> none  [the longest x12 61 us: tile_apply(): jnp.einsum('bkij,nbkj->nbi', tile_set, picked, precision=lax.Precision.HI...]
    all_to_all x2 -> x4, blocking collectives: 38.1 us -> 89 us  [exchanged(): return lax.all_to_all(copies, axes, split_axis=0, concat_axis=0, tiled=True)]
    pallas_call x0 -> x26, Pallas kernels: none -> 48.6 us  [run(): pl.pallas_call(kernel, name=name, out_shape=tuple(outs), in_specs=specs,...]
    unnamed x143 -> x76, local copies, waits for them, and re-layouts: 64.8 us -> 24.5 us
    ppermute x20 -> x18, waiting for transfers between devices: 26.5 us -> 10.3 us  [neighbours(): return (lax.ppermute(high_out, axes, up), lax.ppermute(low_out, axes, down))]
    reshape x10 -> x0, other arithmetic: 13.2 us -> none  [tile_apply(): blocks = extended.reshape(extended.shape[0], -1, tile_width)]
  transfers between devices with their start and end apart: 22 -> 20, of which waited for: 10 -> 9; matrix products, arithmetic and copies ran while one was open for 9% -> 0% of each run, Pallas kernels for 0% -> 9%
where the time goes in v1:
time: 253 us; the launch traced here: 251 us
  blocking collectives  89 us (35%)
  starting transfers between devices  74.2 us (29%)
  Pallas kernels  48.6 us (19%)
  local copies, waits for them, and re-layouts  24.6 us (10%)
  waiting for transfers between devices  13.5 us (5%)
    all_to_all x4, blocking collectives, exchanged(): return lax.all_to_all(copies, axes, split_axis=0, concat_axis=0, tiled=True)  89 us
    ppermute x18, starting transfers between devices, neighbours(): return (lax.ppermute(high_out, axes, up), lax.ppermute(low_out, axes, down))  52.6 us
    pallas_call x26, Pallas kernels, run(): pl.pallas_call(kernel, name=name, out_shape=tuple(outs), in_specs=specs,...  48.6 us
    unnamed x76, local copies, waits for them, and re-layouts  24.5 us
    all_to_all x2, starting transfers between devices, exchanged(): return lax.all_to_all(copies, axes, split_axis=0, concat_axis=0, tiled=True)  21.7 us
    ppermute x18, waiting for transfers between devices, neighbours(): return (lax.ppermute(high_out, axes, up), lax.ppermute(low_out, axes, down))  10.3 us
  transfers between devices with their start and end apart: 20, of which 9 were waited for; matrix products, arithmetic and copies ran while one was open for 0% of the time, Pallas kernels for 9%

profile of v1, /device:TPU:1, one launch (start us, length us, event | category | flops | bytes accessed | tf_op | source)
XLA Modules:
  0.0 251.1 jit_solution(17014257374513210998)
XLA Ops:
  6.6 4.6 %collective-permute-start = (f32[32,256]{1,0:T(8,128)S(1)}, f32[32,256]{1,0:T(8,128)S(1)}, u32[]{:S(2)}, u32[]{:S(2)}) collective-permute-start(f32[32,256]{1,0:T(8,128)S(1)} %get-tuple-element.54), channel_id=1, source_target_pairs={{0,1},{1,2},{2,3},{3,4},{4,5},{5,6},{6,7},{7,8},{8,9},{9,10},{10,1... | collective-permute-start | bytes 98312 | tf_op jit(solution)/shard_map/ppermute | solution.py:434
  14.8 2.3 inner.6.image
  20.5 2.9 %restrict.2 = f32[8,32,384]{2,1,0:T(8,128)} custom-call(s32[16,3]{1,0:T(8,128)S(1)} %copy.37.columns, bf16[48,128,256]{2,1,0:T(8,128)(2,1)S(1)} %copy-done.15, f32[32,2048]{1,0:T(8,128)S(1)} %inner.6.image, f32[32,256]{1,0:T(8,128)S(1)} %collective-permute-done.from_low, f32[32,256]{1,0:T(8,128)S(1)} %collective-permute-done.1.from_high, ...), custom_call_target="tpu_custom_call" | custom-call | flops 4000000000 | bytes 4000000 | tf_op jit(solution)/shard_map/restrict/pallas_call | solution.py:31
  23.4 5.3 %all-to-all-start = ((f32[8,32,384]{2,1,0:T(8,128)}), f32[8,32,384]{2,1,0:T(8,128)S(1)}, u32[]{:S(2)}, u32[]{:S(2)}) async-start(f32[8,32,384]{2,1,0:T(8,128)} %restrict.2), calls=%async_computation | async-start | bytes 786432 | tf_op jit(solution)/shard_map/all_to_all | solution.py:438
  32.5 2.7 %group_setup.1 = (f32[1,2048]{1,0:T(1,128)S(1)}, bf16[48,128,256]{2,1,0:T(8,128)(2,1)S(1)}, bf16[2048,256]{1,0:T(8,128)(2,1)S(1)}, bf16[128,2048]{1,0:T(8,128)(2...) custom-call(s32[5]{0:T(128)S(1)} %stack.23.place, ...), custom_call_target="tpu_custom_call" | custom-call | flops 4000000000 | bytes 4000000 | tf_op jit(solution)/shard_map/group_setup/pallas_call | solution.py:31
  40.2 4.4 %collective-permute-start.2 = (f32[32,128]{1,0:T(8,128)S(1)}, f32[32,128]{1,0:T(8,128)S(1)}, u32[]{:S(2)}, u32[]{:S(2)}) collective-permute-start(f32[32,128]{1,0:T(8,128)S(1)} %get-tuple-element.60), channel_id=1, source_target_pairs={{0,8},{8,16},{16,24},{24,32},{32,40},{40,48},{48,56},{56,64},{64,7... | collective-permute-start | bytes 49160 | tf_op jit(solution)/shard_map/ppermute | solution.py:434
  49.1 2.6 %group_restrict.2 = f32[32,24,128]{2,1,0:T(8,128)} custom-call(s32[16,3]{1,0:T(8,128)S(1)} %copy.33.columns, bf16[48,128,256]{2,1,0:T(8,128)(2,1)S(1)} %copy-done.11, f32[32,2048]{1,0:T(8,128)S(1)} %group_inner.2.image, f32[32,128]{1,0:T(8,128)S(1)} %collective-permute-done.2.from_low, f32[32,128]{1,0:T(8,128)S(1)} %collective-permute-done.3.from_high, ...), custom_call_target="tpu_custom_call" | custom-call | flops 4000000000 | bytes 4000000 | tf_op jit(solution)/shard_map/group_restrict/pallas_call | solution.py:31
  51.7 16.3 %all-to-all-start.1 = ((f32[32,24,128]{2,1,0:T(8,128)}), f32[32,24,128]{2,1,0:T(8,128)S(1)}, u32[]{:S(2)}, u32[]{:S(2)}) async-start(f32[32,24,128]{2,1,0:T(8,128)} %group_restrict.2), calls=%async_computation.1 | async-start | bytes 786432 | tf_op jit(solution)/shard_map/all_to_all | solution.py:438
  68.0 3.1 %collective-permute-start.4 = (f32[8,128]{1,0:T(8,128)S(1)}, f32[8,128]{1,0:T(8,128)S(1)}, u32[]{:S(2)}, u32[]{:S(2)}) collective-permute-start(f32[8,128]{1,0:T(8,128)S(1)} %get-tuple-element.67), channel_id=1, source_target_pairs={{0,8},{8,16},{16,24},{24,32},{32,40},{40,48},{48,56},{56,64},{64,7... | collective-permute-start | bytes 12296 | tf_op jit(solution)/shard_map/ppermute | solution.py:434
  72.5 3.4 %collective-permute-done.5.from_high = f32[8,128]{1,0:T(8,128)S(1)} collective-permute-done((f32[8,128]{1,0:T(8,128)S(1)}, f32[8,128]{1,0:T(8,128)S(1)}, u32[]{:S(2)}, u32[]{:S(2)}) %collective-permute-start.5) | collective-permute-done | bytes 4128 | tf_op jit(solution)/shard_map/ppermute | solution.py:434
  77.7 3.2 %all-to-all-done.1.gathered = f32[32,24,128]{2,1,0:T(8,128)S(1)} async-done(((f32[32,24,128]{2,1,0:T(8,128)}), f32[32,24,128]{2,1,0:T(8,128)S(1)}, u32[]{:S(2)}, u32[]{:S(2)}) %all-to-all-start.1) | async-done | bytes 393248 | tf_op jit(solution)/shard_map/all_to_all | solution.py:438
  87.2 2.9 %coarse.2 = (f32[32,2048]{1,0:T(8,128)S(1)}, f32[32,256]{1,0:T(8,128)S(1)}, f32[32,256]{1,0:T(8,128)S(1)}, f32[32,128]{1,0:T(8,128)}) custom-call(s32[5]{0:T(128)S(1)} %stack.23.place, s32[16,3]{1,0:T(8,128)S(1)} %copy.32.ccolumns, s32[16,3]{1,0:T(8,128)S(1)} %copy.33.columns, f32[32,24,128]{2,1,0:T(8,128)S(1)} %all-to-all-done.1.gathered, ...), custom_call_target="tpu_custom_call" | custom-call | flops 4000000000 | bytes 4000000 | tf_op jit(solution)/shard_map/coarse/pallas_call | solution.py:31
  90.0 6.6 %collective-permute-start.6 = (f32[32,256]{1,0:T(8,128)S(1)}, f32[32,256]{1,0:T(8,128)S(1)}, u32[]{:S(2)}, u32[]{:S(2)}) collective-permute-start(f32[32,256]{1,0:T(8,128)S(1)} %get-tuple-element.73), channel_id=1, source_target_pairs={{0,1},{1,2},{2,3},{3,4},{4,5},{5,6},{6,7},{7,8},{8,9},{9,10},{10,1... | collective-permute-start | bytes 98312 | tf_op jit(solution)/shard_map/ppermute | solution.py:434
  104.0 3.0 %collective-permute-start.8 = (f32[32,256]{1,0:T(8,128)S(1)}, f32[32,256]{1,0:T(8,128)S(1)}, u32[]{:S(2)}, u32[]{:S(2)}) collective-permute-start(f32[32,256]{1,0:T(8,128)S(1)} %get-tuple-element.77), channel_id=1, source_target_pairs={{0,1},{1,2},{2,3},{3,4},{4,5},{5,6},{6,7},{7,8},{8,9},{9,10},{10,1... | collective-permute-start | bytes 98312 | tf_op jit(solution)/shard_map/ppermute | solution.py:434
  114.4 3.0 %collective-permute-start.10 = (f32[32,256]{1,0:T(8,128)S(1)}, f32[32,256]{1,0:T(8,128)S(1)}, u32[]{:S(2)}, u32[]{:S(2)}) collective-permute-start(f32[32,256]{1,0:T(8,128)S(1)} %get-tuple-element.80), channel_id=1, source_target_pairs={{0,1},{1,2},{2,3},{3,4},{4,5},{5,6},{6,7},{7,8},{8,9},{9,10},{10,1... | collective-permute-start | bytes 98312 | tf_op jit(solution)/shard_map/ppermute | solution.py:434
  124.7 17.4 %all_to_all.30.gathered = f32[8,32,384]{2,1,0:T(8,128)S(1)} all-to-all(f32[8,32,384]{2,1,0:T(8,128)S(1)} %restrict.3), channel_id=1, replica_groups=mesh['grp_0'=8,'grp_1'=4,'mem_0'=4,'mem_1'=2] {'mem_0','mem_1'}, dimensions={0} | all-to-all | bytes 786432 | tf_op jit(solution)/shard_map/all_to_all | solution.py:438
  142.4 3.1 %collective-permute-start.12 = (f32[32,128]{1,0:T(8,128)S(1)}, f32[32,128]{1,0:T(8,128)S(1)}, u32[]{:S(2)}, u32[]{:S(2)}) collective-permute-start(f32[32,128]{1,0:T(8,128)S(1)} %get-tuple-element.85), channel_id=1, source_target_pairs={{0,8},{8,16},{16,24},{24,32},{32,40},{40,48},{48,56},{56,64},{64,7... | collective-permute-start | bytes 49160 | tf_op jit(solution)/shard_map/ppermute | solution.py:434
  151.8 31.0 %all_to_all.31.gathered = f32[32,24,128]{2,1,0:T(8,128)S(1)} all-to-all(f32[32,24,128]{2,1,0:T(8,128)S(1)} %group_restrict.3), channel_id=1, replica_groups=mesh['grp_0'=8,'grp_1'=4,'mem_0'=4,'mem_1'=2] {'grp_0','grp_1'}, dimensions={0} | all-to-all | bytes 786432 | tf_op jit(solution)/shard_map/all_to_all | solution.py:438
  182.8 2.3 coarse.3
  185.2 6.4 %collective-permute-start.14 = (f32[32,256]{1,0:T(8,128)S(1)}, f32[32,256]{1,0:T(8,128)S(1)}, u32[]{:S(2)}, u32[]{:S(2)}) collective-permute-start(f32[32,256]{1,0:T(8,128)S(1)} %get-tuple-element.90), channel_id=1, source_target_pairs={{0,1},{1,2},{2,3},{3,4},{4,5},{5,6},{6,7},{7,8},{8,9},{9,10},{10,1... | collective-permute-start | bytes 98312 | tf_op jit(solution)/shard_map/ppermute | solution.py:434
  193.5 2.3 inner.10.image
  199.0 3.0 %collective-permute-start.16 = (f32[32,256]{1,0:T(8,128)S(1)}, f32[32,256]{1,0:T(8,128)S(1)}, u32[]{:S(2)}, u32[]{:S(2)}) collective-permute-start(f32[32,256]{1,0:T(8,128)S(1)} %get-tuple-element.93), channel_id=1, source_target_pairs={{0,1},{1,2},{2,3},{3,4},{4,5},{5,6},{6,7},{7,8},{8,9},{9,10},{10,1... | collective-permute-start | bytes 98312 | tf_op jit(solution)/shard_map/ppermute | solution.py:434
  209.3 13.6 %all_to_all.32.parts = f32[8,32,128]{2,1,0:T(8,128)S(1)} all-to-all(f32[8,32,128]{2,1,0:T(8,128)S(1)} %broadcast_in_dim.7), channel_id=1, replica_groups=mesh['grp_0'=8,'grp_1'=4,'mem_0'=4,'mem_1'=2] {'mem_0','mem_1'}, dimensions={0} | all-to-all | bytes 262144 | tf_op jit(solution)/shard_map/all_to_all | solution.py:438
  222.9 27.1 %all_to_all.33.parts = f32[32,32,128]{2,1,0:T(8,128)S(1)} all-to-all(f32[32,32,128]{2,1,0:T(8,128)S(1)} %sum_copies.1), channel_id=1, replica_groups=mesh['grp_0'=8,'grp_1'=4,'mem_0'=4,'mem_1'=2] {'grp_0','grp_1'}, dimensions={0} | all-to-all | bytes 1048576 | tf_op jit(solution)/shard_map/all_to_all | solution.py:438
  (125 shorter events, 77.7 us)
Async XLA Ops:
  6.6 10.8 %collective-permute-start = (f32[32,256]{1,0:T(8,128)S(1)}, f32[32,256]{1,0:T(8,128)S(1)}, u32[]{:S(2)}, u32[]{:S(2)}) collective-permute-start(f32[32,256]{1,0:T(8,128)S(1)} %get-tuple-element.54), channel_id=1, source_target_pairs={{0,1},{1,2},{2,3},{3,4},{4,5},{5,6},{6,7},{7,8},{8,9},{9,10},{10,1... | collective-permute-start | bytes 98312 | tf_op jit(solution)/shard_map/ppermute | solution.py:434
  11.2 6.2 %collective-permute-start.1 = (f32[32,256]{1,0:T(8,128)S(1)}, f32[32,256]{1,0:T(8,128)S(1)}, u32[]{:S(2)}, u32[]{:S(2)}) collective-permute-start(f32[32,256]{1,0:T(8,128)S(1)} %get-tuple-element.55), channel_id=1, source_target_pairs={{1,0},{2,1},{3,2},{4,3},{5,4},{6,5},{7,6},{8,7},{9,8},{10,9},{11,1... | collective-permute-start | bytes 98312 | tf_op jit(solution)/shard_map/ppermute | solution.py:434
  23.4 15.2 %all-to-all-start = ((f32[8,32,384]{2,1,0:T(8,128)}), f32[8,32,384]{2,1,0:T(8,128)S(1)}, u32[]{:S(2)}, u32[]{:S(2)}) async-start(f32[8,32,384]{2,1,0:T(8,128)} %restrict.2), calls=%async_computation | async-start | bytes 786432 | tf_op jit(solution)/shard_map/all_to_all | solution.py:438
  40.2 8.0 %collective-permute-start.2 = (f32[32,128]{1,0:T(8,128)S(1)}, f32[32,128]{1,0:T(8,128)S(1)}, u32[]{:S(2)}, u32[]{:S(2)}) collective-permute-start(f32[32,128]{1,0:T(8,128)S(1)} %get-tuple-element.60), channel_id=1, source_target_pairs={{0,8},{8,16},{16,24},{24,32},{32,40},{40,48},{48,56},{56,64},{64,7... | collective-permute-start | bytes 49160 | tf_op jit(solution)/shard_map/ppermute | solution.py:434
  44.6 4.5 %collective-permute-start.3 = (f32[32,128]{1,0:T(8,128)S(1)}, f32[32,128]{1,0:T(8,128)S(1)}, u32[]{:S(2)}, u32[]{:S(2)}) collective-permute-start(f32[32,128]{1,0:T(8,128)S(1)} %get-tuple-element.61), channel_id=1, source_target_pairs={{8,0},{16,8},{24,16},{32,24},{40,32},{48,40},{56,48},{64,56},{72,6... | collective-permute-start | bytes 49160 | tf_op jit(solution)/shard_map/ppermute | solution.py:434
  51.7 29.2 %all-to-all-start.1 = ((f32[32,24,128]{2,1,0:T(8,128)}), f32[32,24,128]{2,1,0:T(8,128)S(1)}, u32[]{:S(2)}, u32[]{:S(2)}) async-start(f32[32,24,128]{2,1,0:T(8,128)} %group_restrict.2), calls=%async_computation.1 | async-start | bytes 786432 | tf_op jit(solution)/shard_map/all_to_all | solution.py:438
  68.0 4.4 %collective-permute-start.4 = (f32[8,128]{1,0:T(8,128)S(1)}, f32[8,128]{1,0:T(8,128)S(1)}, u32[]{:S(2)}, u32[]{:S(2)}) collective-permute-start(f32[8,128]{1,0:T(8,128)S(1)} %get-tuple-element.67), channel_id=1, source_target_pairs={{0,8},{8,16},{16,24},{24,32},{32,40},{40,48},{48,56},{56,64},{64,7... | collective-permute-start | bytes 12296 | tf_op jit(solution)/shard_map/ppermute | solution.py:434
  71.2 4.7 %collective-permute-start.5 = (f32[8,128]{1,0:T(8,128)S(1)}, f32[8,128]{1,0:T(8,128)S(1)}, u32[]{:S(2)}, u32[]{:S(2)}) collective-permute-start(f32[8,128]{1,0:T(8,128)S(1)} %get-tuple-element.68), channel_id=1, source_target_pairs={{8,0},{16,8},{24,16},{32,24},{40,32},{48,40},{56,48},{64,56},{72,6... | collective-permute-start | bytes 12296 | tf_op jit(solution)/shard_map/ppermute | solution.py:434
  87.2 11.3 %copy-start.16 = (bf16[48,128,256]{2,1,0:T(8,128)(2,1)S(1)}, bf16[48,128,256]{2,1,0:T(8,128)(2,1)}, u32[]{:S(2)}) copy-start(bf16[48,128,256]{2,1,0:T(8,128)(2,1)} %copy-done.14) | copy-start | bytes 9437188
  90.0 10.8 %collective-permute-start.6 = (f32[32,256]{1,0:T(8,128)S(1)}, f32[32,256]{1,0:T(8,128)S(1)}, u32[]{:S(2)}, u32[]{:S(2)}) collective-permute-start(f32[32,256]{1,0:T(8,128)S(1)} %get-tuple-element.73), channel_id=1, source_target_pairs={{0,1},{1,2},{2,3},{3,4},{4,5},{5,6},{6,7},{7,8},{8,9},{9,10},{10,1... | collective-permute-start | bytes 98312 | tf_op jit(solution)/shard_map/ppermute | solution.py:434
  96.6 5.2 %collective-permute-start.7 = (f32[32,256]{1,0:T(8,128)S(1)}, f32[32,256]{1,0:T(8,128)S(1)}, u32[]{:S(2)}, u32[]{:S(2)}) collective-permute-start(f32[32,256]{1,0:T(8,128)S(1)} %get-tuple-element.74), channel_id=1, source_target_pairs={{1,0},{2,1},{3,2},{4,3},{5,4},{6,5},{7,6},{8,7},{9,8},{10,9},{11,1... | collective-permute-start | bytes 98312 | tf_op jit(solution)/shard_map/ppermute | solution.py:434
  104.0 7.2 %collective-permute-start.8 = (f32[32,256]{1,0:T(8,128)S(1)}, f32[32,256]{1,0:T(8,128)S(1)}, u32[]{:S(2)}, u32[]{:S(2)}) collective-permute-start(f32[32,256]{1,0:T(8,128)S(1)} %get-tuple-element.77), channel_id=1, source_target_pairs={{0,1},{1,2},{2,3},{3,4},{4,5},{5,6},{6,7},{7,8},{8,9},{9,10},{10,1... | collective-permute-start | bytes 98312 | tf_op jit(solution)/shard_map/ppermute | solution.py:434
  107.0 5.2 %collective-permute-start.9 = (f32[32,256]{1,0:T(8,128)S(1)}, f32[32,256]{1,0:T(8,128)S(1)}, u32[]{:S(2)}, u32[]{:S(2)}) collective-permute-start(f32[32,256]{1,0:T(8,128)S(1)} %get-tuple-element.78), channel_id=1, source_target_pairs={{1,0},{2,1},{3,2},{4,3},{5,4},{6,5},{7,6},{8,7},{9,8},{10,9},{11,1... | collective-permute-start | bytes 98312 | tf_op jit(solution)/shard_map/ppermute | solution.py:434
  114.4 7.2 %collective-permute-start.10 = (f32[32,256]{1,0:T(8,128)S(1)}, f32[32,256]{1,0:T(8,128)S(1)}, u32[]{:S(2)}, u32[]{:S(2)}) collective-permute-start(f32[32,256]{1,0:T(8,128)S(1)} %get-tuple-element.80), channel_id=1, source_target_pairs={{0,1},{1,2},{2,3},{3,4},{4,5},{5,6},{6,7},{7,8},{8,9},{9,10},{10,1... | collective-permute-start | bytes 98312 | tf_op jit(solution)/shard_map/ppermute | solution.py:434
  117.3 5.2 %collective-permute-start.11 = (f32[32,256]{1,0:T(8,128)S(1)}, f32[32,256]{1,0:T(8,128)S(1)}, u32[]{:S(2)}, u32[]{:S(2)}) collective-permute-start(f32[32,256]{1,0:T(8,128)S(1)} %get-tuple-element.81), channel_id=1, source_target_pairs={{1,0},{2,1},{3,2},{4,3},{5,4},{6,5},{7,6},{8,7},{9,8},{10,9},{11,1... | collective-permute-start | bytes 98312 | tf_op jit(solution)/shard_map/ppermute | solution.py:434
  122.6 19.5 %copy-start.26 = (bf16[2048,256]{1,0:T(8,128)(2,1)S(1)}, bf16[2048,256]{1,0:T(8,128)(2,1)}, u32[]{:S(2)}) copy-start(bf16[2048,256]{1,0:T(8,128)(2,1)} %copy-done.24) | copy-start | bytes 3145732
  142.4 6.7 %collective-permute-start.12 = (f32[32,128]{1,0:T(8,128)S(1)}, f32[32,128]{1,0:T(8,128)S(1)}, u32[]{:S(2)}, u32[]{:S(2)}) collective-permute-start(f32[32,128]{1,0:T(8,128)S(1)} %get-tuple-element.85), channel_id=1, source_target_pairs={{0,8},{8,16},{16,24},{24,32},{32,40},{40,48},{48,56},{56,64},{64,7... | collective-permute-start | bytes 49160 | tf_op jit(solution)/shard_map/ppermute | solution.py:434
  145.5 4.5 %collective-permute-start.13 = (f32[32,128]{1,0:T(8,128)S(1)}, f32[32,128]{1,0:T(8,128)S(1)}, u32[]{:S(2)}, u32[]{:S(2)}) collective-permute-start(f32[32,128]{1,0:T(8,128)S(1)} %get-tuple-element.86), channel_id=1, source_target_pairs={{8,0},{16,8},{24,16},{32,24},{40,32},{48,40},{56,48},{64,56},{72,6... | collective-permute-start | bytes 49160 | tf_op jit(solution)/shard_map/ppermute | solution.py:434
  150.0 32.9 %copy-start.19 = (bf16[256,2304]{1,0:T(8,128)(2,1)S(1)}, bf16[256,2304]{1,0:T(8,128)(2,1)}, u32[]{:S(2)}) copy-start(bf16[256,2304]{1,0:T(8,128)(2,1)} %copy-done.17) | copy-start | bytes 3538948
  150.0 32.9 %copy-start.23 = (bf16[256,2048]{1,0:T(8,128)(2,1)S(1)}, bf16[256,2048]{1,0:T(8,128)(2,1)}, u32[]{:S(2)}) copy-start(bf16[256,2048]{1,0:T(8,128)(2,1)} %copy-done.20) | copy-start | bytes 3145732
  185.2 10.6 %collective-permute-start.14 = (f32[32,256]{1,0:T(8,128)S(1)}, f32[32,256]{1,0:T(8,128)S(1)}, u32[]{:S(2)}, u32[]{:S(2)}) collective-permute-start(f32[32,256]{1,0:T(8,128)S(1)} %get-tuple-element.90), channel_id=1, source_target_pairs={{0,1},{1,2},{2,3},{3,4},{4,5},{5,6},{6,7},{7,8},{8,9},{9,10},{10,1... | collective-permute-start | bytes 98312 | tf_op jit(solution)/shard_map/ppermute | solution.py:434
  191.6 5.2 %collective-permute-start.15 = (f32[32,256]{1,0:T(8,128)S(1)}, f32[32,256]{1,0:T(8,128)S(1)}, u32[]{:S(2)}, u32[]{:S(2)}) collective-permute-start(f32[32,256]{1,0:T(8,128)S(1)} %get-tuple-element.91), channel_id=1, source_target_pairs={{1,0},{2,1},{3,2},{4,3},{5,4},{6,5},{7,6},{8,7},{9,8},{10,9},{11,1... | collective-permute-start | bytes 98312 | tf_op jit(solution)/shard_map/ppermute | solution.py:434
  199.0 7.2 %collective-permute-start.16 = (f32[32,256]{1,0:T(8,128)S(1)}, f32[32,256]{1,0:T(8,128)S(1)}, u32[]{:S(2)}, u32[]{:S(2)}) collective-permute-start(f32[32,256]{1,0:T(8,128)S(1)} %get-tuple-element.93), channel_id=1, source_target_pairs={{0,1},{1,2},{2,3},{3,4},{4,5},{5,6},{6,7},{7,8},{8,9},{9,10},{10,1... | collective-permute-start | bytes 98312 | tf_op jit(solution)/shard_map/ppermute | solution.py:434
  202.0 5.2 %collective-permute-start.17 = (f32[32,256]{1,0:T(8,128)S(1)}, f32[32,256]{1,0:T(8,128)S(1)}, u32[]{:S(2)}, u32[]{:S(2)}) collective-permute-start(f32[32,256]{1,0:T(8,128)S(1)} %get-tuple-element.94), channel_id=1, source_target_pairs={{1,0},{2,1},{3,2},{4,3},{5,4},{6,5},{7,6},{8,7},{9,8},{10,9},{11,1... | collective-permute-start | bytes 98312 | tf_op jit(solution)/shard_map/ppermute | solution.py:434
  (32 other events, 101.8 us)

commit v2 on v1

v2 whole, which is shorter than its diff:
```python
import functools

import jax
import jax.numpy as jnp
from jax import lax
from jax.experimental import pallas as pl
from jax.experimental.pallas import tpu as pltpu
from jax.sharding import Mesh
from jax.sharding import PartitionSpec as P

TILE = 128
AGG1 = 8
AGG2 = 32
ALL = ("grp_0", "grp_1", "mem_0", "mem_1")
GRP = ("grp_0", "grp_1")
MEM = ("mem_0", "mem_1")
RELAXATION = 0.7
F32 = jnp.float32
BF16 = jnp.bfloat16
VMEM_SPEC = pl.BlockSpec(memory_space=pltpu.VMEM)
SMEM_SPEC = pl.BlockSpec(memory_space=pltpu.SMEM)
HBM_SPEC = pl.BlockSpec(memory_space=pltpu.HBM)
CHUNKS = 8
LIMIT = 24 * 1024 * 1024


def shape(dims, dtype=F32):
    return pltpu.VMEM(tuple(dims), dtype)


def hbm(dims, dtype=F32):
    return jax.ShapeDtypeStruct(tuple(dims), dtype)


def scalars(count):
    return pltpu.SMEM((count,), jnp.int32)


def run(
    kernel, name, outs, args, smem=(), hbm_args=(), scratch=(), smem_outs=(), flops=4_000_000_000
):
    specs = [
        SMEM_SPEC if i in smem else HBM_SPEC if i in hbm_args else VMEM_SPEC
        for i in range(len(args))
    ]
    return pl.pallas_call(
        kernel,
        name=name,
        out_shape=tuple(outs),
        in_specs=specs,
        out_specs=tuple(SMEM_SPEC if i in smem_outs else VMEM_SPEC for i in range(len(outs))),
        scratch_shapes=list(scratch),
        compiler_params=pltpu.CompilerParams(vmem_limit_bytes=LIMIT),
        cost_estimate=pl.CostEstimate(flops=flops, transcendentals=0, bytes_accessed=4_000_000),
    )(*args)


def halves(value):
    high = value.astype(BF16)
    low = (value - high.astype(F32)).astype(BF16)
    return high, low


def stacked(value):
    high, low = halves(value)
    return jnp.concatenate([high, low], axis=0)


def doubled(value):
    both = stacked(value)
    return jnp.concatenate([both, both], axis=1)


def joined(both):
    rows = both.shape[0] // 2
    return both[:rows] + both[rows:]


def dot_nt(left, right):
    return lax.dot_general(left, right, (((1,), (1,)), ((), ())), preferred_element_type=F32)


def dot_nn(left, right):
    return lax.dot_general(left, right, (((1,), (0,)), ((), ())), preferred_element_type=F32)


def select_nn(value, onehot):
    return joined(dot_nn(stacked(value), onehot))


def select_nt(value, onehot):
    return joined(dot_nt(stacked(value), onehot))


def fill_blocks(blocks, value, first=0):
    for i in range(value.shape[1] // TILE):
        blocks[first + i] = doubled(value[:, i * TILE : (i + 1) * TILE])


def lane_block(b):
    return pl.ds(pl.multiple_of(b * TILE, TILE), TILE)


def tile_rows(columns, weights, blocks, diagonal, value, store, count, unroll=4):
    def step(i, carry):
        for j in range(unroll):
            b = i * unroll + j
            acc = dot_nn(blocks[columns[0, b]], weights[b * 3])
            acc += dot_nn(blocks[columns[1, b]], weights[b * 3 + 1])
            acc += dot_nn(blocks[columns[2, b]], weights[b * 3 + 2])
            at = lane_block(b)
            store(at, joined(acc) + diagonal[:, at] * value[:, at])
        return carry

    lax.fori_loop(0, count // unroll, step, 0)


def own_blocks(blocks, value):
    own = value.shape[1] // TILE
    fill_blocks(blocks, value[...])
    zero = jnp.zeros(blocks.shape[1:], BF16)
    for i in range(own, blocks.shape[0]):
        blocks[i] = zero


def halo_products(place, spot, visits, weights, near, far, blocks):
    halos = blocks.shape[0]
    width = halos // 2
    fill_blocks(blocks.at[pl.ds(place[spot] * width, width)], near[...])
    fill_blocks(blocks.at[pl.ds((1 - place[spot]) * width, width)], far[...])
    found = []
    for i in range(2 * halos):
        acc = dot_nn(blocks[i % halos], weights[visits[2 * halos + i]])
        found.append((lane_block(visits[i]), joined(acc)))
    return found


def note_visits(columns, visits, own, halos):
    for i in range(2 * halos):
        visits[i] = 0
        visits[2 * halos + i] = 3 * own
    for b in range(own):
        for k in (1, 2):
            col = columns[k, b]

            @pl.when(col >= own)
            def _():
                at = (k - 1) * halos + col - own
                visits[at] = b
                visits[2 * halos + at] = 3 * b + k


def fetch(source, target, sems, chunks=CHUNKS):
    step = source.shape[0] // chunks
    copies = []
    for i in range(chunks):
        part = pl.ds(i * step, step)
        copies.append(pltpu.make_async_copy(source.at[part], target.at[part], sems.at[i]))
        copies[-1].start()
    return copies


def diagonal_scale(columns, tiles, scale, first, rows):
    lines = lax.broadcasted_iota(jnp.int32, (TILE, TILE), 0)
    lanes = lax.broadcasted_iota(jnp.int32, (TILE, TILE), 1)
    eye = lines == lanes

    def diagonal(b, k):
        return jnp.sum(jnp.where(eye, tiles[b, k], 0.0), axis=0, keepdims=True)

    for b in rows:
        here = slice(b * TILE, (b + 1) * TILE)
        mine = diagonal(b, 0)
        if first is not None:
            first[:, here] = mine
        scale[:, here] = mine
        for k in (1, 2):

            @pl.when(columns[k, b] == b)
            def _():
                scale[:, here] += diagonal(b, k)


def chunk_rows(i, count):
    step = count // CHUNKS
    return range(i * step, (i + 1) * step)


def pack_tile(tile):
    high, low = halves(tile.T)
    return jnp.concatenate([high, low], axis=0)


def pack_tiles(tiles, packed, which):
    rows = lax.broadcasted_iota(jnp.int32, (TILE, TILE), 0)
    lanes = lax.broadcasted_iota(jnp.int32, (TILE, TILE), 1)
    for b in which:
        packed[b * 3] = pack_tile(jnp.where(rows == lanes, 0.0, tiles[b, 0]))
        packed[b * 3 + 1] = pack_tile(tiles[b, 1])
        packed[b * 3 + 2] = pack_tile(tiles[b, 2])


def onehot_by_lane(index_row, rows):
    place = lax.broadcasted_iota(jnp.int32, (rows, index_row.shape[1]), 0)
    return jnp.where(place == index_row, 1.0, 0.0).astype(BF16)


def fill_picks(flag, sends, picks):
    up = flag == 1
    near = jnp.where(up, sends[1:2, :], sends[0:1, :])
    far = jnp.where(up, sends[0:1, :], sends[1:2, :])
    chosen = jnp.concatenate([near, far], axis=1)
    chunk = 256
    for i in range(picks.shape[0] // chunk):
        place = lax.broadcasted_iota(jnp.int32, (chunk, chosen.shape[1]), 0) + i * chunk
        picks[i * chunk : (i + 1) * chunk, :] = jnp.where(place == chosen, 1.0, 0.0).astype(BF16)


def put_pair(out, near, far):
    width = near.shape[1]
    near[...] = out[:, :width]
    far[...] = out[:, width:]


def pick_correction(out, part, picks, at):
    return out + joined(dot_nn(stacked(part), picks[at, :]))


def compact(wide, count):
    lanes = lax.broadcasted_iota(jnp.int32, (8, TILE), 1)
    sums = jnp.zeros((8, TILE), F32)
    for j in range(4):
        part = jnp.where(lanes < count, wide[8 * j : 8 * j + 8, :], 0.0)
        sums += pltpu.roll(part, count * j, 1) if j else part
    return sums


def spread_rows(sums, count):
    return jnp.concatenate(
        [sums] + [pltpu.roll(sums, TILE - count * j, 1) for j in range(1, 4)], axis=0
    )


def lane_columns(parts):
    lanes = lax.broadcasted_iota(jnp.int32, (32, TILE), 1)
    out = jnp.zeros((32, TILE), F32)
    for i, part in enumerate(parts):
        out = jnp.where(lanes == i, part, out)
    return out


def row_sum(value):
    return jnp.sum(value, axis=1, keepdims=True)


def copy_scalars(source, target):
    for k in range(source.shape[0]):
        for b in range(source.shape[1]):
            target[k, b] = source[k, b]


def first_kernel(
    place, columns, tiles_hbm, sends_hbm, source_hbm, *rest, lines,
):
    lines_hbm = rest[:lines]
    (scale, diagonal, start, near, far, picks, tiles, source, place_out, columns_out) = rest[
        lines : lines + 10
    ]
    kept = rest[lines + 10 : 2 * lines + 10]
    sends, sems = rest[2 * lines + 10 :]
    count = tiles.shape[0]
    early = pltpu.make_async_copy(sends_hbm, sends, sems.at[CHUNKS])
    early.start()
    copies = fetch(tiles_hbm, tiles, sems)
    others = [pltpu.make_async_copy(source_hbm, source, sems.at[CHUNKS + 1])]
    for i in range(lines):
        others.append(pltpu.make_async_copy(lines_hbm[i], kept[i], sems.at[CHUNKS + 2 + i]))
    for copy in others:
        copy.start()
    for i in range(place.shape[0]):
        place_out[i] = place[i]
    copy_scalars(columns, columns_out)
    early.wait()
    fill_picks(place[5], sends, picks)
    for i, copy in enumerate(copies):
        copy.wait()
        diagonal_scale(columns, tiles, scale, diagonal, chunk_rows(i, count))
    for copy in others:
        copy.wait()
    scale[...] = RELAXATION / scale[...]
    begin = scale[...] * source[...]
    start[...] = begin
    put_pair(select_nn(begin, picks[...]), near, far)


def pack_fine_kernel(columns, tiles, groups, packed, table, visits):
    own = tiles.shape[0]
    pack_tiles(tiles, packed, range(own))
    packed[3 * own] = jnp.zeros(packed.shape[1:], BF16)
    table[...] = onehot_by_lane(groups[...], table.shape[0])
    note_visits(columns, visits, own, 4)


def group_setup_kernel(
    place, columns, tiles_hbm, sends, weights, groups, ccolumns, ctiles_hbm,
    scale, diagonal, packed, picks, table, cscale, cpacked, edge_near, edge_far, visits,
    columns_out, ccolumns_out, tiles, ctiles, cline, sems, csems,
):
    count = tiles.shape[0]
    copy_scalars(columns, columns_out)
    copy_scalars(ccolumns, ccolumns_out)
    copies = fetch(tiles_hbm, tiles, sems)
    ccopies = fetch(ctiles_hbm, ctiles, csems)
    fill_picks(place[6], sends, picks)
    table[...] = onehot_by_lane(groups[...], table.shape[0])
    length = weights.shape[1]
    numbers = groups[...].astype(F32)
    lines = lax.broadcasted_iota(jnp.int32, (8, length), 0)
    facts = jnp.where(lines == 0, weights[...], jnp.where(lines == 1, numbers, 0.0))
    put_pair(select_nn(facts, picks[...]), edge_near, edge_far)
    note_visits(columns, visits, count, 2)
    for i, copy in enumerate(copies):
        copy.wait()
        diagonal_scale(columns, tiles, scale, diagonal, chunk_rows(i, count))
        pack_tiles(tiles, packed, chunk_rows(i, count))
    packed[3 * count] = jnp.zeros(packed.shape[1:], BF16)
    scale[...] = RELAXATION / scale[...]
    blocks = ctiles.shape[0]
    for i, copy in enumerate(ccopies):
        copy.wait()
        diagonal_scale(ccolumns, ctiles, cline, None, chunk_rows(i, blocks))
    for b in range(blocks):
        cscale[b] = RELAXATION / cline[:, b * TILE : (b + 1) * TILE]
    for t in range(2):
        row = place[2 + t]
        for k in range(3):
            cpacked[t * 3 + k] = pack_tile(ctiles[row, k])


def group_edges_kernel(place, weights, groups, near, far, wide_weights, raise_table):
    length = weights.shape[1]
    half = near.shape[1]
    base = place[4]
    up = place[6]
    rows = raise_table.shape[0]
    wide_weights[:, :length] = weights[...]
    raise_table[:, :length] = onehot_by_lane(groups[...] + base, rows)
    low = jnp.where(up == 1, far[...], near[...])
    high = jnp.where(up == 1, near[...], far[...])
    wide_weights[:, length : length + half] = low[0:1, :]
    wide_weights[:, length + half :] = high[0:1, :]
    low_at = low[1:2, :].astype(jnp.int32) + (base - 64)
    high_at = high[1:2, :].astype(jnp.int32) + (base + 64)
    raise_table[:, length : length + half] = onehot_by_lane(low_at, rows)
    raise_table[:, length + half :] = onehot_by_lane(high_at, rows)


def inner_restrict_kernel(
    columns, weights, diagonal, value, source, agg_weights, table, coarse, blocks, left
):
    own_blocks(blocks, value)

    def store(at, row):
        left[:, at] = (source[:, at] - row) * agg_weights[:, at]

    tile_rows(columns, weights, blocks, diagonal, value, store, value.shape[1] // TILE)
    coarse[...] = select_nt(left[...], table[...])


def restrict_kernel(
    place, visits, weights, coarse, near, far, agg_weights, table, *rest, spot, after
):
    rest = rest[after:]
    lowered, blocks = rest[-2:]
    out = coarse[...]
    for at, part in halo_products(place, spot, visits, weights, near, far, blocks):
        out -= joined(dot_nt(stacked(part * agg_weights[:, at]), table[:, at]))
    if len(rest) == 3:
        lines = compact(rest[0][...], 2)
        out = jnp.concatenate(
            [out, jnp.concatenate([lines, jnp.zeros_like(lines)], axis=1)], axis=0
        )
    for i in range(lowered.shape[0]):
        lowered[i] = out


def group_start_kernel(gathered, scale, picks, group_rhs, start, near, far, *extra):
    members = gathered.shape[0]
    width = group_rhs.shape[1] // members
    for i in range(members):
        group_rhs[:, i * width : (i + 1) * width] = gathered[i, :32, :]
    if extra:
        total = gathered[0, 32:40, :TILE]
        for i in range(1, members):
            total += gathered[i, 32:40, :TILE]
        extra[0][...] = total
    begin = scale[...] * group_rhs[...]
    start[...] = begin
    put_pair(select_nn(begin, picks[...]), near, far)


def group_restrict_kernel(
    place, visits, weights, coarse, near, far, agg_weights, table, *rest, spot, after
):
    rest = rest[after:]
    payload, blocks = rest[-2:]
    out = coarse[...]
    for at, part in halo_products(place, spot, visits, weights, near, far, blocks):
        out -= joined(dot_nt(stacked(part * agg_weights[:, at]), table[:, at]))
    half = out.shape[0] // 2
    message = jnp.concatenate([out[:half, :64], out[half:, :64]], axis=1)
    if len(rest) == 3:
        message = jnp.concatenate([message, rest[0][...]], axis=0)
    for i in range(payload.shape[0]):
        payload[i] = message


def coarse_kernel(
    place, ccolumns, columns, gathered, cscale, cpacked, own_start, near, far,
    group_rhs, scale, diagonal, packed, wide_weights, raise_table, fine_start, fine_weights,
    fine_table, picks, *rest,
):
    blocks, current = rest[-2:]
    fine_next, near_out, far_out = rest[:3]
    lanes = lax.broadcasted_iota(jnp.int32, (16, TILE), 1)

    def block(t):
        first = gathered[2 * t, :16, :]
        second = gathered[2 * t + 1, :16, :]
        top = jnp.where(lanes < 64, first, pltpu.roll(second, 64, 1))
        bottom = jnp.where(lanes < 64, pltpu.roll(first, 64, 1), second)
        return jnp.concatenate([top, bottom], axis=0)

    if len(rest) == 6:
        sums = gathered[0, 16:24, :]
        for i in range(1, gathered.shape[0]):
            sums += gathered[i, 16:24, :]
        rest[3][...] = spread_rows(sums, 2)
    solved = []
    for t in range(2):
        row = place[2 + t]
        acc = jnp.zeros((64, TILE), F32)
        for k in range(3):
            col = ccolumns[k, row]
            acc += dot_nn(doubled(cscale[col] * block(col)), cpacked[t * 3 + k])
        mine = block(row)
        iterate = cscale[row] * mine
        solved.append(iterate + cscale[row] * (mine - joined(acc)))
    pair = jnp.concatenate(solved, axis=1)
    raised = select_nn(pair, raise_table[...]) * wide_weights[...]
    length = own_start.shape[1]
    half = near.shape[1]
    now = own_start[...] + raised[:, :length]
    current[...] = now
    fill_blocks(blocks, now)
    up = place[6]
    low = jnp.where(up == 1, far[...], near[...])
    high = jnp.where(up == 1, near[...], far[...])
    fill_blocks(blocks, low + raised[:, length : length + half], length // TILE)
    fill_blocks(blocks, high + raised[:, length + half :], (length + half) // TILE)
    member = place[1]
    iterate_rows = []
    for j in range(2):
        b = member * 2 + j
        acc = dot_nn(blocks[columns[0, b]], packed[b * 3])
        acc += dot_nn(blocks[columns[1, b]], packed[b * 3 + 1])
        acc += dot_nn(blocks[columns[2, b]], packed[b * 3 + 2])
        at = lane_block(b)
        mine = current[:, at]
        image = joined(acc) + diagonal[:, at] * mine
        iterate_rows.append(mine + scale[:, at] * (group_rhs[:, at] - image))
    spread = jnp.concatenate(iterate_rows, axis=1)
    following = fine_start[...] + fine_weights[...] * select_nn(spread, fine_table[...])
    fine_next[...] = following
    put_pair(select_nn(following, picks[...]), near_out, far_out)


def inner_smooth_kernel(
    columns, weights, diagonal, value, source, scale, picks, smoothed, out, blocks
):
    own_blocks(blocks, value)

    def store(at, row):
        smoothed[:, at] = value[:, at] + scale[:, at] * (source[:, at] - row)

    tile_rows(columns, weights, blocks, diagonal, value, store, value.shape[1] // TILE)
    out[...] = select_nn(smoothed[...], picks[...])


def smooth_kernel(
    place, visits, weights, inner, inner_out, near, far, scale, picks,
    smoothed, near_out, far_out, blocks,
):
    smoothed[...] = inner[...]
    out = inner_out[...]
    for at, part in halo_products(place, 5, visits, weights, near, far, blocks):
        change = -scale[:, at] * part
        smoothed[:, at] += change
        out = pick_correction(out, change, picks, at)
    put_pair(out, near_out, far_out)


def inner_image_kernel(
    columns, weights, diagonal, value, scale, residual, picks, product, out, sums, blocks
):
    own_blocks(blocks, value)

    def store(at, row):
        product[:, at] = row

    tile_rows(columns, weights, blocks, diagonal, value, store, value.shape[1] // TILE)
    image = product[...]
    out[...] = select_nn(scale[...] * image, picks[...])
    field = value[...]
    sums[...] = lane_columns([row_sum(residual[...] * field), row_sum(field * image)])


def image_kernel(
    place, visits, weights, inner, inner_out, inner_sums, near, far, scale, value, picks,
    product, start, near_out, far_out, sums, blocks,
):
    product[...] = inner[...]
    out = inner_out[...]
    curve = jnp.zeros((32, TILE), F32)
    for at, part in halo_products(place, 5, visits, weights, near, far, blocks):
        product[:, at] += part
        curve += value[:, at] * part
        out = pick_correction(out, scale[:, at] * part, picks, at)
    put_pair(out, near_out, far_out)
    start[...] = scale[...] * product[...]
    sums[...] = inner_sums[...] + lane_columns([jnp.zeros((32, 1), F32), row_sum(curve)])


def inner_last_kernel(
    columns, weights, diagonal, second, residual, value, product, image, sums, blocks,
):
    own_blocks(blocks, second)

    def store(at, row):
        image[:, at] = row

    tile_rows(columns, weights, blocks, diagonal, second, store, second.shape[1] // TILE)
    follow = image[...]
    field = second[...]
    along = product[...]
    zero = jnp.zeros((32, 1), F32)
    sums[...] = lane_columns(
        [
            zero,
            zero,
            row_sum(residual[...] * field),
            row_sum(along * field),
            row_sum(value[...] * follow + field * along),
            row_sum(field * follow),
        ]
    )


def last_kernel(
    place, visits, weights, inner, inner_sums, first_sums, near, far, value, second,
    image, copies, blocks,
):
    image[...] = inner[...]
    cross = jnp.zeros((32, TILE), F32)
    curve = jnp.zeros((32, TILE), F32)
    for at, part in halo_products(place, 5, visits, weights, near, far, blocks):
        image[:, at] += part
        cross += value[:, at] * part
        curve += second[:, at] * part
    zero = jnp.zeros((32, 1), F32)
    sums = inner_sums[...] + first_sums[...]
    sums += lane_columns([zero, zero, zero, zero, row_sum(cross), row_sum(curve)])
    message = compact(sums, 6)
    for i in range(copies.shape[0]):
        copies[i] = message


def sum_copies_kernel(parts, copies):
    total = parts[0]
    for i in range(1, parts.shape[0]):
        total += parts[i]
    for i in range(copies.shape[0]):
        copies[i] = total


def final_kernel(parts, start, value, product, second, image, solution, residual):
    small = parts[0]
    for i in range(1, parts.shape[0]):
        small += parts[i]
    sums = spread_rows(small, 6)
    energy, curve, along, across, cross, last = (sums[:, i : i + 1] for i in range(6))
    step = energy / curve
    new = step * (step * across - along)
    ratio = new / energy
    grown = 1.0 + ratio
    second_curve = grown * (grown * curve - step * cross) + step * step * last
    second_step = new / second_curve
    field = value[...]
    product_now = product[...]
    solution[...] = step * field + second_step * (grown * field - step * second[...])
    residual[...] = (start[...] - step * product_now) - second_step * (
        grown * product_now - step * image[...]
    )


def neighbours(near_out, far_out, axes):
    count = lax.axis_size(axes)
    near = [(i, i ^ 1) for i in range(count)]
    far = [(i, i + 1) for i in range(1, count - 1, 2)]
    far = far + [(b, a) for a, b in far]
    far_in = lax.ppermute(far_out, axes, far)
    return lax.ppermute(near_out, axes, near), far_in


def exchanged(copies, axes):
    return lax.all_to_all(copies, axes, split_axis=0, concat_axis=0, tiled=True)


def shards(
    right_side,
    fine_tiles,
    fine_columns,
    fine_sends,
    fine_weights,
    fine_groups,
    group_tiles,
    group_columns,
    group_sends,
    group_weights,
    group_groups,
    coarse_tiles,
    coarse_columns,
):
    rhs, length = right_side.shape
    fine_count = length // AGG1
    group_length = group_weights.shape[0]
    share = group_length // AGG2
    members = lax.axis_size(MEM)
    group_total = lax.axis_size(GRP)
    fine_half = fine_sends.shape[1]
    group_half = group_sends.shape[1]
    fine_halo = 2 * fine_half // TILE
    group_halo = 2 * group_half // TILE
    fine_blocks = length // TILE
    group_blocks = group_length // TILE
    coarse_blocks = coarse_tiles.shape[0]

    fine_weights = fine_weights.reshape(1, -1)
    fine_groups = fine_groups.reshape(1, -1)
    group_weights = group_weights.reshape(1, -1)
    group_groups = group_groups.reshape(1, -1)
    fine_columns = fine_columns.T
    group_columns = group_columns.T
    coarse_columns = coarse_columns.T

    grp = lax.axis_index(GRP)
    mem = lax.axis_index(MEM)
    row_a = jnp.maximum((grp - 1) // 2, 0)
    row_b = jnp.minimum(row_a + 1, coarse_blocks - 1)
    place = jnp.stack(
        [grp, mem, row_a, row_b, grp * share - row_a * TILE, 1 - mem % 2, 1 - grp % 2]
    ).astype(jnp.int32)

    def block_scratch(count):
        return pltpu.VMEM((count, 2 * rhs, 2 * TILE), BF16)

    edge = shape((rhs, fine_half))
    group_edge = shape((rhs, group_half))
    field = shape((rhs, length))
    line = shape((1, length))
    small = shape((rhs, TILE))
    picked = shape((rhs, 2 * fine_half))

    pinned = [
        pltpu.with_memory_space_constraint(x, pltpu.HBM)
        for x in (fine_tiles, fine_sends, right_side, fine_weights, fine_groups, group_weights,
                  group_groups, group_sends)
    ]
    group_tiles = pltpu.with_memory_space_constraint(group_tiles, pltpu.HBM)
    coarse_tiles = pltpu.with_memory_space_constraint(coarse_tiles, pltpu.HBM)
    (fine_scale, fine_diagonal, fine_start, near, far, fine_picks, fine_tiles, right_side,
     place, fine_columns, fine_weights, fine_groups, group_weights, group_groups,
     group_sends) = run(
        functools.partial(first_kernel, lines=5), "first",
        [line, line, field, edge, edge, shape((length, 2 * fine_half), BF16),
         shape(fine_tiles.shape), field, scalars(7), pltpu.SMEM(fine_columns.shape, jnp.int32),
         line, shape((1, length), jnp.int32), line, shape((1, group_length), jnp.int32),
         shape(group_sends.shape, jnp.int32)],
        [place, fine_columns] + pinned, smem=(0, 1), hbm_args=range(2, 10), smem_outs=(8, 9),
        scratch=[pltpu.VMEM(fine_sends.shape, jnp.int32),
                 pltpu.SemaphoreType.DMA((CHUNKS + 7,))],
    )
    near, far = neighbours(near, far, ALL)
    fine_packed, fine_table, fine_visits = run(
        pack_fine_kernel, "pack_fine",
        [shape((3 * fine_blocks + 1, 2 * TILE, TILE), BF16), shape((fine_count, length), BF16),
         scalars(4 * fine_halo)],
        (fine_columns, fine_tiles, fine_groups), smem=(0,), smem_outs=(2,),
    )

    (group_scale, group_diagonal, group_packed, group_picks, group_table, coarse_scale,
     coarse_packed, edge_near, edge_far, group_visits, group_columns, coarse_columns) = run(
        group_setup_kernel, "group_setup",
        [
            line,
            line,
            shape((3 * group_blocks + 1, 2 * TILE, TILE), BF16),
            shape((group_length, 2 * group_half), BF16),
            shape((TILE, group_length), BF16),
            shape((coarse_blocks, 1, TILE)),
            shape((6, 2 * TILE, TILE), BF16),
            shape((8, group_half)),
            shape((8, group_half)),
            scalars(4 * group_halo),
            pltpu.SMEM(group_columns.shape, jnp.int32),
            pltpu.SMEM(coarse_columns.shape, jnp.int32),
        ],
        (place, group_columns, group_tiles, group_sends, group_weights, group_groups,
         coarse_columns, coarse_tiles),
        smem=(0, 1, 6), smem_outs=(9, 10, 11), hbm_args=(2, 7),
        scratch=[pltpu.VMEM(group_tiles.shape, F32), pltpu.VMEM(coarse_tiles.shape, F32),
                 pltpu.VMEM((1, coarse_blocks * TILE), F32),
                 pltpu.SemaphoreType.DMA((CHUNKS,)), pltpu.SemaphoreType.DMA((CHUNKS,))],
    )
    edge_near, edge_far = neighbours(edge_near, edge_far, GRP)
    wide_weights, raise_table = run(
        group_edges_kernel, "group_edges",
        [shape((1, group_length + 2 * group_half)),
         shape((2 * TILE, group_length + 2 * group_half), BF16)],
        (place, group_weights, group_groups, edge_near, edge_far), smem=(0,),
    )

    def vcycle(source, fine_start, near, far, extra, first_after=(), second_after=()):
        carried = () if extra is None else (extra,)
        coarse = run(
            inner_restrict_kernel, "inner_restrict", [shape((rhs, fine_count))],
            (fine_columns, fine_packed, fine_diagonal, fine_start, source, fine_weights,
             fine_table),
            smem=(0,), scratch=[block_scratch(fine_blocks + fine_halo), pltpu.VMEM((rhs, length), F32)],
        )[0]
        lowered = run(
            functools.partial(restrict_kernel, spot=5, after=len(first_after)), "restrict",
            [shape((members, rhs + 8 * len(carried), fine_count))],
            (place, fine_visits, fine_packed, coarse, near, far, fine_weights, fine_table)
            + first_after + carried,
            smem=(0, 1), scratch=[block_scratch(fine_halo)],
        )[0]
        gathered = exchanged(lowered, MEM)
        group_rhs, group_start, near, far, *carried = run(
            group_start_kernel, "group_start",
            [field, field, group_edge, group_edge] + [shape((8, TILE)) for _ in carried],
            (gathered, group_scale, group_picks),
        )
        g_near, g_far = neighbours(near, far, GRP)
        coarse = run(
            inner_restrict_kernel, "group_inner", [shape((rhs, TILE))],
            (group_columns, group_packed, group_diagonal, group_start, group_rhs,
             group_weights, group_table),
            smem=(0,), scratch=[block_scratch(group_blocks + group_halo), pltpu.VMEM((rhs, length), F32)],
        )[0]
        payload = run(
            functools.partial(group_restrict_kernel, spot=6, after=len(second_after)),
            "group_restrict",
            [shape((group_total, 16 + 8 * len(carried), TILE))],
            (place, group_visits, group_packed, coarse, g_near, g_far, group_weights,
             group_table) + second_after + tuple(carried),
            smem=(0, 1), scratch=[block_scratch(group_halo)],
        )[0]
        gathered = exchanged(payload, GRP)
        fine_next, near, far, *totals = run(
            coarse_kernel, "coarse", [field, edge, edge] + [small for _ in carried],
            (place, coarse_columns, group_columns, gathered, coarse_scale, coarse_packed,
             group_start, g_near, g_far, group_rhs, group_scale, group_diagonal, group_packed,
             wide_weights, raise_table, fine_start, fine_weights, fine_table, fine_picks),
            smem=(0, 1, 2),
            scratch=[block_scratch(group_blocks + group_halo), pltpu.VMEM((rhs, length), F32)],
        )
        near, far = neighbours(near, far, ALL)
        inside, out = run(
            inner_smooth_kernel, "inner_smooth", [field, picked],
            (fine_columns, fine_packed, fine_diagonal, fine_next, source, fine_scale,
             fine_picks),
            smem=(0,), scratch=[block_scratch(fine_blocks + fine_halo)],
        )
        smoothed, near, far = run(
            smooth_kernel, "smooth", [field, edge, edge],
            (place, fine_visits, fine_packed, inside, out, near, far, fine_scale, fine_picks),
            smem=(0, 1), scratch=[block_scratch(fine_halo)],
        )
        near, far = neighbours(near, far, ALL)
        return smoothed, near, far, totals

    value, near, far, _ = vcycle(
        right_side, fine_start, near, far, None, (wide_weights,)
    )
    inside, out, sums = run(
        inner_image_kernel, "inner_image", [field, picked, small],
        (fine_columns, fine_packed, fine_diagonal, value, fine_scale, right_side, fine_picks),
        smem=(0,), scratch=[block_scratch(fine_blocks + fine_halo)],
    )
    product, start, near, far, sums = run(
        image_kernel, "image", [field, field, edge, edge, small],
        (place, fine_visits, fine_packed, inside, out, sums, near, far, fine_scale, value,
         fine_picks),
        smem=(0, 1), scratch=[block_scratch(fine_halo)],
    )
    near, far = neighbours(near, far, ALL)
    second, near, far, _ = vcycle(product, start, near, far, None)
    inside, more = run(
        inner_last_kernel, "inner_last", [field, small],
        (fine_columns, fine_packed, fine_diagonal, second, right_side, value, product),
        smem=(0,), scratch=[block_scratch(fine_blocks + fine_halo)],
    )
    image, copies = run(
        last_kernel, "last", [field, shape((members, 8, TILE))],
        (place, fine_visits, fine_packed, inside, more, sums, near, far, value, second),
        smem=(0, 1), scratch=[block_scratch(fine_halo)],
    )
    copies = run(
        sum_copies_kernel, "sum_copies", [shape((group_total, 8, TILE))],
        (exchanged(copies, MEM),),
    )[0]
    parts = exchanged(copies, GRP)
    solution, residual = run(
        final_kernel, "final", [hbm((rhs, length)), hbm((rhs, length))],
        (parts, right_side, value, product, second, image),
    )
    return solution, residual


def solution(mesh):
    finer = Mesh(mesh.devices.reshape(8, 4, 4, 2), ALL)
    return jax.shard_map(
        shards,
        mesh=finer,
        in_specs=(
            P(None, ALL),
            P(ALL, None, None, None),
            P(ALL, None),
            P(ALL, None),
            P(ALL),
            P(ALL),
            P(GRP, None, None, None),
            P(GRP, None),
            P(GRP, None),
            P(GRP),
            P(GRP),
            P(),
            P(),
        ),
        out_specs=(P(None, ALL), P(None, ALL)),
        check_vma=False,
    )
```

time: 253 us -> 181 us (0.72)
  starting transfers between devices: 74.2 us -> 31.8 us
  local copies, waits for them, and re-layouts: 24.6 us -> 0.78 us
  blocking collectives: 89 us -> 111 us
  Pallas kernels: 48.6 us -> 29.7 us
  waiting for transfers between devices: 13.5 us -> 6.62 us
    unnamed x76 -> x6, local copies, waits for them, and re-layouts: 24.5 us -> 0.69 us
    all_to_all x4 -> x6, blocking collectives: 89 us -> 111 us  [exchanged(): return lax.all_to_all(copies, axes, split_axis=0, concat_axis=0, tiled=True)]
    all_to_all x2 -> x0, starting transfers between devices: 21.7 us -> none  [exchanged(): return lax.all_to_all(copies, axes, split_axis=0, concat_axis=0, tiled=True)]
    ppermute x18, starting transfers between devices: 52.6 us -> 31.8 us  [the longest x9 16 us: neighbours(): far_in = lax.ppermute(far_out, axes, far)]
    pallas_call x26, Pallas kernels: 48.6 us -> 29.7 us  [run(): pl.pallas_call(kernel, name=name, out_shape=tuple(outs), in_specs=specs,...]
    ppermute x18, waiting for transfers between devices: 10.3 us -> 6.62 us  [the longest x9 6.06 us: neighbours(): far_in = lax.ppermute(far_out, axes, far)]
    all_to_all x2 -> x0, waiting for transfers between devices: 3.24 us -> none  [exchanged(): return lax.all_to_all(copies, axes, split_axis=0, concat_axis=0, tiled=True)]
  transfers between devices with their start and end apart: 20 -> 18, of which waited for: 9 -> 6; matrix products, arithmetic and copies ran while one was open for 0% -> 0% of each run, Pallas kernels for 9% -> 10%
where the time goes in v2:
time: 181 us
  blocking collectives  111 us (61%)
  starting transfers between devices  31.8 us (18%)
  Pallas kernels  29.7 us (16%)
  waiting for transfers between devices  6.62 us (4%)
    all_to_all x6, blocking collectives, exchanged(): return lax.all_to_all(copies, axes, split_axis=0, concat_axis=0, tiled=True)  111 us
    pallas_call x26, Pallas kernels, run(): pl.pallas_call(kernel, name=name, out_shape=tuple(outs), in_specs=specs,...  29.7 us
    ppermute x9, starting transfers between devices, neighbours(): far_in = lax.ppermute(far_out, axes, far)  16 us
    ppermute x9, starting transfers between devices, neighbours(): return (lax.ppermute(near_out, axes, near), far_in)  15.8 us
    ppermute x9, waiting for transfers between devices, neighbours(): far_in = lax.ppermute(far_out, axes, far)  6.06 us
  transfers between devices with their start and end apart: 18, of which 6 were waited for; matrix products, arithmetic and copies ran while one was open for 0% of the time, Pallas kernels for 10%

profile of v2, /device:TPU:1, one launch (start us, length us, event | category | flops | bytes accessed | tf_op | source)
XLA Modules:
  0.0 180.7 jit_solution(2945343354012801581)
XLA Ops:
  1.5 3.1 %first.1 = (f32[1,2048]{1,0:T(1,128)S(1)}, f32[1,2048]{1,0:T(1,128)S(1)}, f32[32,2048]{1,0:T(8,128)S(1)}, f32[32,256]{1,0:T(8,128)S(1)}, f32[32,256]{1,0:T(8,128...) custom-call(s32[7]{0:T(128)S(1)} %stack.31.place, ...), custom_call_target="tpu_custom_call" | custom-call | flops 4000000000 | bytes 4000000 | tf_op jit(solution)/shard_map/first/pallas_call | solution.py:46
  4.6 3.3 %collective-permute-start = (f32[32,256]{1,0:T(8,128)S(1)}, f32[32,256]{1,0:T(8,128)S(1)}, u32[]{:S(2)}, u32[]{:S(2)}) collective-permute-start(f32[32,256]{1,0:T(8,128)S(1)} %get-tuple-element.89), channel_id=1, source_target_pairs={{0,1},{1,0},{2,3},{3,2},{4,5},{5,4},{6,7},{7,6},{8,9},{9,8},{10,11... | collective-permute-start | bytes 98312 | tf_op jit(solution)/shard_map/ppermute | solution.py:612
  7.9 1.9 %collective-permute-start.1 = (f32[32,256]{1,0:T(8,128)S(1)}, f32[32,256]{1,0:T(8,128)S(1)}, u32[]{:S(2)}, u32[]{:S(2)}) collective-permute-start(f32[32,256]{1,0:T(8,128)S(1)} %get-tuple-element.90), channel_id=1, source_target_pairs={{1,2},{3,4},{5,6},{7,8},{9,10},{11,12},{13,14},{15,16},{17,18},{19... | collective-permute-start | bytes 98312 | tf_op jit(solution)/shard_map/ppermute | solution.py:611
  9.8 4.9 %group_setup.1 = (f32[1,2048]{1,0:T(1,128)S(1)}, f32[1,2048]{1,0:T(1,128)S(1)}, bf16[49,256,128]{2,1,0:T(8,128)(2,1)S(1)}, bf16[2048,256]{1,0:T(8,128)(2,1)S(1)}...) custom-call(s32[7]{0:T(128)S(4)} %get-tuple-element.70.place, ...), custom_call_target="tpu_custom_call" | custom-call | flops 4000000000 | bytes 4000000 | tf_op jit(solution)/shard_map/group_setup/pallas_call | solution.py:46
  17.3 1.6 inner_restrict.2.coarse
  19.6 11.1 %all_to_all.30.gathered = f32[8,32,256]{2,1,0:T(8,128)S(1)} all-to-all(f32[8,32,256]{2,1,0:T(8,128)S(1)} %restrict.2), channel_id=1, replica_groups=mesh['grp_0'=8,'grp_1'=4,'mem_0'=4,'mem_1'=2] {'mem_0','mem_1'}, dimensions={0} | all-to-all | bytes 524288 | tf_op jit(solution)/shard_map/all_to_all | solution.py:616
  31.0 4.0 %collective-permute-start.4 = (f32[32,128]{1,0:T(8,128)S(1)}, f32[32,128]{1,0:T(8,128)S(1)}, u32[]{:S(2)}, u32[]{:S(2)}) collective-permute-start(f32[32,128]{1,0:T(8,128)S(1)} %get-tuple-element.99), channel_id=1, source_target_pairs={{0,8},{8,0},{16,24},{24,16},{32,40},{40,32},{48,56},{56,48},{64,72... | collective-permute-start | bytes 49160 | tf_op jit(solution)/shard_map/ppermute | solution.py:612
  37.5 26.2 %all_to_all.31.gathered = f32[32,16,128]{2,1,0:T(8,128)S(1)} all-to-all(f32[32,16,128]{2,1,0:T(8,128)S(1)} %group_restrict.2), channel_id=1, replica_groups=mesh['grp_0'=8,'grp_1'=4,'mem_0'=4,'mem_1'=2] {'grp_0','grp_1'}, dimensions={0} | all-to-all | bytes 524288 | tf_op jit(solution)/shard_map/all_to_all | solution.py:616
  65.1 3.8 %collective-permute-start.6 = (f32[32,256]{1,0:T(8,128)S(1)}, f32[32,256]{1,0:T(8,128)S(1)}, u32[]{:S(2)}, u32[]{:S(2)}) collective-permute-start(f32[32,256]{1,0:T(8,128)S(1)} %get-tuple-element.109), channel_id=1, source_target_pairs={{0,1},{1,0},{2,3},{3,2},{4,5},{5,4},{6,7},{7,6},{8,9},{9,8},{10,11... | collective-permute-start | bytes 98312 | tf_op jit(solution)/shard_map/ppermute | solution.py:612
  68.9 2.3 %collective-permute-start.7 = (f32[32,256]{1,0:T(8,128)S(1)}, f32[32,256]{1,0:T(8,128)S(1)}, u32[]{:S(2)}, u32[]{:S(2)}) collective-permute-start(f32[32,256]{1,0:T(8,128)S(1)} %get-tuple-element.110), channel_id=1, source_target_pairs={{1,2},{3,4},{5,6},{7,8},{9,10},{11,12},{13,14},{15,16},{17,18},{19... | collective-permute-start | bytes 98312 | tf_op jit(solution)/shard_map/ppermute | solution.py:611
  71.2 1.6 inner_smooth.2
  74.6 2.6 %collective-permute-start.9 = (f32[32,256]{1,0:T(8,128)S(1)}, f32[32,256]{1,0:T(8,128)S(1)}, u32[]{:S(2)}, u32[]{:S(2)}) collective-permute-start(f32[32,256]{1,0:T(8,128)S(1)} %get-tuple-element.116), channel_id=1, source_target_pairs={{1,2},{3,4},{5,6},{7,8},{9,10},{11,12},{13,14},{15,16},{17,18},{19... | collective-permute-start | bytes 98312 | tf_op jit(solution)/shard_map/ppermute | solution.py:611
  77.2 1.6 inner_image.1
  80.3 2.7 %collective-permute-start.11 = (f32[32,256]{1,0:T(8,128)S(1)}, f32[32,256]{1,0:T(8,128)S(1)}, u32[]{:S(2)}, u32[]{:S(2)}) collective-permute-start(f32[32,256]{1,0:T(8,128)S(1)} %get-tuple-element.120), channel_id=1, source_target_pairs={{1,2},{3,4},{5,6},{7,8},{9,10},{11,12},{13,14},{15,16},{17,18},{19... | collective-permute-start | bytes 98312 | tf_op jit(solution)/shard_map/ppermute | solution.py:611
  83.0 1.6 inner_restrict.3.coarse
  86.0 15.1 %all_to_all.32.gathered = f32[8,32,256]{2,1,0:T(8,128)S(1)} all-to-all(f32[8,32,256]{2,1,0:T(8,128)S(1)} %restrict.3), channel_id=1, replica_groups=mesh['grp_0'=8,'grp_1'=4,'mem_0'=4,'mem_1'=2] {'mem_0','mem_1'}, dimensions={0} | all-to-all | bytes 524288 | tf_op jit(solution)/shard_map/all_to_all | solution.py:616
  104.5 28.4 %all_to_all.33.gathered = f32[32,16,128]{2,1,0:T(8,128)S(1)} all-to-all(f32[32,16,128]{2,1,0:T(8,128)S(1)} %group_restrict.3), channel_id=1, replica_groups=mesh['grp_0'=8,'grp_1'=4,'mem_0'=4,'mem_1'=2] {'grp_0','grp_1'}, dimensions={0} | all-to-all | bytes 524288 | tf_op jit(solution)/shard_map/all_to_all | solution.py:616
  134.3 3.8 %collective-permute-start.14 = (f32[32,256]{1,0:T(8,128)S(1)}, f32[32,256]{1,0:T(8,128)S(1)}, u32[]{:S(2)}, u32[]{:S(2)}) collective-permute-start(f32[32,256]{1,0:T(8,128)S(1)} %get-tuple-element.128), channel_id=1, source_target_pairs={{0,1},{1,0},{2,3},{3,2},{4,5},{5,4},{6,7},{7,6},{8,9},{9,8},{10,11... | collective-permute-start | bytes 98312 | tf_op jit(solution)/shard_map/ppermute | solution.py:612
  138.1 2.1 %collective-permute-start.15 = (f32[32,256]{1,0:T(8,128)S(1)}, f32[32,256]{1,0:T(8,128)S(1)}, u32[]{:S(2)}, u32[]{:S(2)}) collective-permute-start(f32[32,256]{1,0:T(8,128)S(1)} %get-tuple-element.129), channel_id=1, source_target_pairs={{1,2},{3,4},{5,6},{7,8},{9,10},{11,12},{13,14},{15,16},{17,18},{19... | collective-permute-start | bytes 98312 | tf_op jit(solution)/shard_map/ppermute | solution.py:611
  140.2 1.6 inner_smooth.3
  141.8 1.5 collective-permute-done.15.far
  143.8 2.6 %collective-permute-start.17 = (f32[32,256]{1,0:T(8,128)S(1)}, f32[32,256]{1,0:T(8,128)S(1)}, u32[]{:S(2)}, u32[]{:S(2)}) collective-permute-start(f32[32,256]{1,0:T(8,128)S(1)} %get-tuple-element.135), channel_id=1, source_target_pairs={{1,2},{3,4},{5,6},{7,8},{9,10},{11,12},{13,14},{15,16},{17,18},{19... | collective-permute-start | bytes 98312 | tf_op jit(solution)/shard_map/ppermute | solution.py:611
  149.4 11.3 %all_to_all.34.parts = f32[8,8,128]{2,1,0:T(8,128)S(1)} all-to-all(f32[8,8,128]{2,1,0:T(8,128)S(1)} %get-tuple-element.136), channel_id=1, replica_groups=mesh['grp_0'=8,'grp_1'=4,'mem_0'=4,'mem_1'=2] {'mem_0','mem_1'}, dimensions={0} | all-to-all | bytes 65536 | tf_op jit(solution)/shard_map/all_to_all | solution.py:616
  160.7 18.8 %all_to_all.35.parts = f32[32,8,128]{2,1,0:T(8,128)S(1)} all-to-all(f32[32,8,128]{2,1,0:T(8,128)S(1)} %sum_copies.1), channel_id=1, replica_groups=mesh['grp_0'=8,'grp_1'=4,'mem_0'=4,'mem_1'=2] {'grp_0','grp_1'}, dimensions={0} | all-to-all | bytes 262144 | tf_op jit(solution)/shard_map/all_to_all | solution.py:616
  (51 shorter events, 22.4 us)
Async XLA Ops:
  0.8 0.7 copy-start
  1.4 8.3 %copy-start.1 = (s32[16,3]{0,1:T(4,128)S(1)}, s32[16,3]{0,1:T(4,128)}, u32[]{:S(2)}) copy-start(s32[16,3]{0,1:T(4,128)} %param.20) | copy-start | bytes 580
  1.4 8.3 %copy-start.2 = (s32[16,3]{0,1:T(4,128)S(1)}, s32[16,3]{0,1:T(4,128)}, u32[]{:S(2)}) copy-start(s32[16,3]{0,1:T(4,128)} %param.25) | copy-start | bytes 580
  4.6 14.6 %collective-permute-start = (f32[32,256]{1,0:T(8,128)S(1)}, f32[32,256]{1,0:T(8,128)S(1)}, u32[]{:S(2)}, u32[]{:S(2)}) collective-permute-start(f32[32,256]{1,0:T(8,128)S(1)} %get-tuple-element.89), channel_id=1, source_target_pairs={{0,1},{1,0},{2,3},{3,2},{4,5},{5,4},{6,7},{7,6},{8,9},{9,8},{10,11... | collective-permute-start | bytes 98312 | tf_op jit(solution)/shard_map/ppermute | solution.py:612
  7.9 11.3 %collective-permute-start.1 = (f32[32,256]{1,0:T(8,128)S(1)}, f32[32,256]{1,0:T(8,128)S(1)}, u32[]{:S(2)}, u32[]{:S(2)}) collective-permute-start(f32[32,256]{1,0:T(8,128)S(1)} %get-tuple-element.90), channel_id=1, source_target_pairs={{1,2},{3,4},{5,6},{7,8},{9,10},{11,12},{13,14},{15,16},{17,18},{19... | collective-permute-start | bytes 98312 | tf_op jit(solution)/shard_map/ppermute | solution.py:611
  14.7 4.2 %collective-permute-start.2 = (f32[8,128]{1,0:T(8,128)S(1)}, f32[8,128]{1,0:T(8,128)S(1)}, u32[]{:S(2)}, u32[]{:S(2)}) collective-permute-start(f32[8,128]{1,0:T(8,128)S(1)} %get-tuple-element.91), channel_id=1, source_target_pairs={{0,8},{8,0},{16,24},{24,16},{32,40},{40,32},{48,56},{56,48},{64,72... | collective-permute-start | bytes 12296 | tf_op jit(solution)/shard_map/ppermute | solution.py:612
  15.5 3.4 %collective-permute-start.3 = (f32[8,128]{1,0:T(8,128)S(1)}, f32[8,128]{1,0:T(8,128)S(1)}, u32[]{:S(2)}, u32[]{:S(2)}) collective-permute-start(f32[8,128]{1,0:T(8,128)S(1)} %get-tuple-element.92), channel_id=1, source_target_pairs={{8,16},{24,32},{40,48},{56,64},{72,80},{88,96},{104,112},{120,128}... | collective-permute-start | bytes 12296 | tf_op jit(solution)/shard_map/ppermute | solution.py:611
  31.0 6.1 %collective-permute-start.4 = (f32[32,128]{1,0:T(8,128)S(1)}, f32[32,128]{1,0:T(8,128)S(1)}, u32[]{:S(2)}, u32[]{:S(2)}) collective-permute-start(f32[32,128]{1,0:T(8,128)S(1)} %get-tuple-element.99), channel_id=1, source_target_pairs={{0,8},{8,0},{16,24},{24,16},{32,40},{40,32},{48,56},{56,48},{64,72... | collective-permute-start | bytes 49160 | tf_op jit(solution)/shard_map/ppermute | solution.py:612
  35.0 2.1 %collective-permute-start.5 = (f32[32,128]{1,0:T(8,128)S(1)}, f32[32,128]{1,0:T(8,128)S(1)}, u32[]{:S(2)}, u32[]{:S(2)}) collective-permute-start(f32[32,128]{1,0:T(8,128)S(1)} %get-tuple-element.100), channel_id=1, source_target_pairs={{8,16},{24,32},{40,48},{56,64},{72,80},{88,96},{104,112},{120,128}... | collective-permute-start | bytes 49160 | tf_op jit(solution)/shard_map/ppermute | solution.py:611
  65.1 7.7 %collective-permute-start.6 = (f32[32,256]{1,0:T(8,128)S(1)}, f32[32,256]{1,0:T(8,128)S(1)}, u32[]{:S(2)}, u32[]{:S(2)}) collective-permute-start(f32[32,256]{1,0:T(8,128)S(1)} %get-tuple-element.109), channel_id=1, source_target_pairs={{0,1},{1,0},{2,3},{3,2},{4,5},{5,4},{6,7},{7,6},{8,9},{9,8},{10,11... | collective-permute-start | bytes 98312 | tf_op jit(solution)/shard_map/ppermute | solution.py:612
  68.9 5.2 %collective-permute-start.7 = (f32[32,256]{1,0:T(8,128)S(1)}, f32[32,256]{1,0:T(8,128)S(1)}, u32[]{:S(2)}, u32[]{:S(2)}) collective-permute-start(f32[32,256]{1,0:T(8,128)S(1)} %get-tuple-element.110), channel_id=1, source_target_pairs={{1,2},{3,4},{5,6},{7,8},{9,10},{11,12},{13,14},{15,16},{17,18},{19... | collective-permute-start | bytes 98312 | tf_op jit(solution)/shard_map/ppermute | solution.py:611
  74.6 4.3 %collective-permute-start.8 = (f32[32,256]{1,0:T(8,128)S(1)}, f32[32,256]{1,0:T(8,128)S(1)}, u32[]{:S(2)}, u32[]{:S(2)}) collective-permute-start(f32[32,256]{1,0:T(8,128)S(1)} %get-tuple-element.115), channel_id=1, source_target_pairs={{0,1},{1,0},{2,3},{3,2},{4,5},{5,4},{6,7},{7,6},{8,9},{9,8},{10,11... | collective-permute-start | bytes 98312 | tf_op jit(solution)/shard_map/ppermute | solution.py:612
  74.6 5.2 %collective-permute-start.9 = (f32[32,256]{1,0:T(8,128)S(1)}, f32[32,256]{1,0:T(8,128)S(1)}, u32[]{:S(2)}, u32[]{:S(2)}) collective-permute-start(f32[32,256]{1,0:T(8,128)S(1)} %get-tuple-element.116), channel_id=1, source_target_pairs={{1,2},{3,4},{5,6},{7,8},{9,10},{11,12},{13,14},{15,16},{17,18},{19... | collective-permute-start | bytes 98312 | tf_op jit(solution)/shard_map/ppermute | solution.py:611
  80.3 4.3 %collective-permute-start.10 = (f32[32,256]{1,0:T(8,128)S(1)}, f32[32,256]{1,0:T(8,128)S(1)}, u32[]{:S(2)}, u32[]{:S(2)}) collective-permute-start(f32[32,256]{1,0:T(8,128)S(1)} %get-tuple-element.119), channel_id=1, source_target_pairs={{0,1},{1,0},{2,3},{3,2},{4,5},{5,4},{6,7},{7,6},{8,9},{9,8},{10,11... | collective-permute-start | bytes 98312 | tf_op jit(solution)/shard_map/ppermute | solution.py:612
  80.3 5.2 %collective-permute-start.11 = (f32[32,256]{1,0:T(8,128)S(1)}, f32[32,256]{1,0:T(8,128)S(1)}, u32[]{:S(2)}, u32[]{:S(2)}) collective-permute-start(f32[32,256]{1,0:T(8,128)S(1)} %get-tuple-element.120), channel_id=1, source_target_pairs={{1,2},{3,4},{5,6},{7,8},{9,10},{11,12},{13,14},{15,16},{17,18},{19... | collective-permute-start | bytes 98312 | tf_op jit(solution)/shard_map/ppermute | solution.py:611
  101.4 2.6 %collective-permute-start.12 = (f32[32,128]{1,0:T(8,128)S(1)}, f32[32,128]{1,0:T(8,128)S(1)}, u32[]{:S(2)}, u32[]{:S(2)}) collective-permute-start(f32[32,128]{1,0:T(8,128)S(1)} %get-tuple-element.123), channel_id=1, source_target_pairs={{0,8},{8,0},{16,24},{24,16},{32,40},{40,32},{48,56},{56,48},{64,72... | collective-permute-start | bytes 49160 | tf_op jit(solution)/shard_map/ppermute | solution.py:612
  101.5 2.6 %collective-permute-start.13 = (f32[32,128]{1,0:T(8,128)S(1)}, f32[32,128]{1,0:T(8,128)S(1)}, u32[]{:S(2)}, u32[]{:S(2)}) collective-permute-start(f32[32,128]{1,0:T(8,128)S(1)} %get-tuple-element.124), channel_id=1, source_target_pairs={{8,16},{24,32},{40,48},{56,64},{72,80},{88,96},{104,112},{120,128}... | collective-permute-start | bytes 49160 | tf_op jit(solution)/shard_map/ppermute | solution.py:611
  134.3 7.5 %collective-permute-start.14 = (f32[32,256]{1,0:T(8,128)S(1)}, f32[32,256]{1,0:T(8,128)S(1)}, u32[]{:S(2)}, u32[]{:S(2)}) collective-permute-start(f32[32,256]{1,0:T(8,128)S(1)} %get-tuple-element.128), channel_id=1, source_target_pairs={{0,1},{1,0},{2,3},{3,2},{4,5},{5,4},{6,7},{7,6},{8,9},{9,8},{10,11... | collective-permute-start | bytes 98312 | tf_op jit(solution)/shard_map/ppermute | solution.py:612
  138.1 5.2 %collective-permute-start.15 = (f32[32,256]{1,0:T(8,128)S(1)}, f32[32,256]{1,0:T(8,128)S(1)}, u32[]{:S(2)}, u32[]{:S(2)}) collective-permute-start(f32[32,256]{1,0:T(8,128)S(1)} %get-tuple-element.129), channel_id=1, source_target_pairs={{1,2},{3,4},{5,6},{7,8},{9,10},{11,12},{13,14},{15,16},{17,18},{19... | collective-permute-start | bytes 98312 | tf_op jit(solution)/shard_map/ppermute | solution.py:611
  143.8 4.0 %collective-permute-start.16 = (f32[32,256]{1,0:T(8,128)S(1)}, f32[32,256]{1,0:T(8,128)S(1)}, u32[]{:S(2)}, u32[]{:S(2)}) collective-permute-start(f32[32,256]{1,0:T(8,128)S(1)} %get-tuple-element.134), channel_id=1, source_target_pairs={{0,1},{1,0},{2,3},{3,2},{4,5},{5,4},{6,7},{7,6},{8,9},{9,8},{10,11... | collective-permute-start | bytes 98312 | tf_op jit(solution)/shard_map/ppermute | solution.py:612
  143.8 5.2 %collective-permute-start.17 = (f32[32,256]{1,0:T(8,128)S(1)}, f32[32,256]{1,0:T(8,128)S(1)}, u32[]{:S(2)}, u32[]{:S(2)}) collective-permute-start(f32[32,256]{1,0:T(8,128)S(1)} %get-tuple-element.135), channel_id=1, source_target_pairs={{1,2},{3,4},{5,6},{7,8},{9,10},{11,12},{13,14},{15,16},{17,18},{19... | collective-permute-start | bytes 98312 | tf_op jit(solution)/shard_map/ppermute | solution.py:611

commit v3 on v2

--- a/solution.py
+++ b/solution.py
@@ -302,31 +302,76 @@
 
 
 def group_setup_kernel(
-    place, columns, tiles_hbm, sends, weights, groups, ccolumns, ctiles_hbm,
-    scale, diagonal, packed, picks, table, cscale, cpacked, edge_near, edge_far, visits,
-    columns_out, ccolumns_out, tiles, ctiles, cline, sems, csems,
+    place, columns, tiles_hbm, sends, weights, groups,
+    scale, diagonal, packed, picks, table, raise_table, edge_near, edge_far, visits,
+    columns_out, tiles, sems,
 ):
     count = tiles.shape[0]
+    copies = fetch(tiles_hbm, tiles, sems)
     copy_scalars(columns, columns_out)
-    copy_scalars(ccolumns, ccolumns_out)
-    copies = fetch(tiles_hbm, tiles, sems)
-    ccopies = fetch(ctiles_hbm, ctiles, csems)
+    note_visits(columns, visits, count, 2)
     fill_picks(place[6], sends, picks)
     table[...] = onehot_by_lane(groups[...], table.shape[0])
+    raise_table[...] = onehot_by_lane(groups[...] + place[4], raise_table.shape[0])
     length = weights.shape[1]
     numbers = groups[...].astype(F32)
     lines = lax.broadcasted_iota(jnp.int32, (8, length), 0)
     facts = jnp.where(lines == 0, weights[...], jnp.where(lines == 1, numbers, 0.0))
     put_pair(select_nn(facts, picks[...]), edge_near, edge_far)
-    note_visits(columns, visits, count, 2)
     for i, copy in enumerate(copies):
         copy.wait()
         diagonal_scale(columns, tiles, scale, diagonal, chunk_rows(i, count))
         pack_tiles(tiles, packed, chunk_rows(i, count))
     packed[3 * count] = jnp.zeros(packed.shape[1:], BF16)
     scale[...] = RELAXATION / scale[...]
+
+
+def inner_restrict_kernel(
+    columns, weights, diagonal, value, source, agg_weights, table, coarse, blocks, left
+):
+    own_blocks(blocks, value)
+
+    def store(at, row):
+        left[:, at] = (source[:, at] - row) * agg_weights[:, at]
+
+    tile_rows(columns, weights, blocks, diagonal, value, store, value.shape[1] // TILE)
+    coarse[...] = select_nt(left[...], table[...])
+
+
+def restrict_kernel(
+    place, visits, weights, coarse, far, near, agg_weights, table, *rest, spot, after
+):
+    lowered, blocks = rest[after:]
+    out = coarse[...]
+    for at, part in halo_products(place, spot, visits, weights, near, far, blocks):
+        out -= joined(dot_nt(stacked(part * agg_weights[:, at]), table[:, at]))
+    for i in range(lowered.shape[0]):
+        lowered[i] = out
+
+
+def group_start_kernel(gathered, scale, picks, *rest):
+    facts = rest[:-4]
+    group_rhs, start, near, far = rest[-4:]
+    members = gathered.shape[0]
+    width = group_rhs.shape[1] // members
+    for i in range(members):
+        group_rhs[:, i * width : (i + 1) * width] = gathered[i]
+    begin = scale[...] * group_rhs[...]
+    start[...] = begin
+    rows = begin.shape[0]
+    put_pair(select_nn(begin, picks[...]), near.at[:rows], far.at[:rows])
+    if facts:
+        near[rows:, :] = facts[0][...]
+        far[rows:, :] = facts[1][...]
+
+
+def coarse_setup_kernel(
+    place, ccolumns, ctiles_hbm, after, cscale, cpacked, ccolumns_out, ctiles, cline, csems
+):
+    copies = fetch(ctiles_hbm, ctiles, csems)
+    copy_scalars(ccolumns, ccolumns_out)
     blocks = ctiles.shape[0]
-    for i, copy in enumerate(ccopies):
+    for i, copy in enumerate(copies):
         copy.wait()
         diagonal_scale(ccolumns, ctiles, cline, None, chunk_rows(i, blocks))
     for b in range(blocks):
@@ -337,91 +382,43 @@
             cpacked[t * 3 + k] = pack_tile(ctiles[row, k])
 
 
-def group_edges_kernel(place, weights, groups, near, far, wide_weights, raise_table):
-    length = weights.shape[1]
-    half = near.shape[1]
-    base = place[4]
-    up = place[6]
-    rows = raise_table.shape[0]
-    wide_weights[:, :length] = weights[...]
-    raise_table[:, :length] = onehot_by_lane(groups[...] + base, rows)
-    low = jnp.where(up == 1, far[...], near[...])
-    high = jnp.where(up == 1, near[...], far[...])
-    wide_weights[:, length : length + half] = low[0:1, :]
-    wide_weights[:, length + half :] = high[0:1, :]
-    low_at = low[1:2, :].astype(jnp.int32) + (base - 64)
-    high_at = high[1:2, :].astype(jnp.int32) + (base + 64)
-    raise_table[:, length : length + half] = onehot_by_lane(low_at, rows)
-    raise_table[:, length + half :] = onehot_by_lane(high_at, rows)
-
-
-def inner_restrict_kernel(
-    columns, weights, diagonal, value, source, agg_weights, table, coarse, blocks, left
-):
-    own_blocks(blocks, value)
-
-    def store(at, row):
-        left[:, at] = (source[:, at] - row) * agg_weights[:, at]
-
-    tile_rows(columns, weights, blocks, diagonal, value, store, value.shape[1] // TILE)
-    coarse[...] = select_nt(left[...], table[...])
-
-
-def restrict_kernel(
-    place, visits, weights, coarse, near, far, agg_weights, table, *rest, spot, after
-):
-    rest = rest[after:]
-    lowered, blocks = rest[-2:]
+def group_restrict_kernel(
+    place, visits, weights, coarse, far, near, agg_weights, table, *rest, edges
+):
+    rest = rest[1:] if edges else rest
+    payload, blocks = rest[0], rest[-1]
+    rows = coarse.shape[0]
     out = coarse[...]
-    for at, part in halo_products(place, spot, visits, weights, near, far, blocks):
+    for at, part in halo_products(
+        place, 6, visits, weights, near.at[:rows], far.at[:rows], blocks
+    ):
         out -= joined(dot_nt(stacked(part * agg_weights[:, at]), table[:, at]))
-    if len(rest) == 3:
-        lines = compact(rest[0][...], 2)
-        out = jnp.concatenate(
-            [out, jnp.concatenate([lines, jnp.zeros_like(lines)], axis=1)], axis=0
-        )
-    for i in range(lowered.shape[0]):
-        lowered[i] = out
-
-
-def group_start_kernel(gathered, scale, picks, group_rhs, start, near, far, *extra):
-    members = gathered.shape[0]
-    width = group_rhs.shape[1] // members
-    for i in range(members):
-        group_rhs[:, i * width : (i + 1) * width] = gathered[i, :32, :]
-    if extra:
-        total = gathered[0, 32:40, :TILE]
-        for i in range(1, members):
-            total += gathered[i, 32:40, :TILE]
-        extra[0][...] = total
-    begin = scale[...] * group_rhs[...]
-    start[...] = begin
-    put_pair(select_nn(begin, picks[...]), near, far)
-
-
-def group_restrict_kernel(
-    place, visits, weights, coarse, near, far, agg_weights, table, *rest, spot, after
-):
-    rest = rest[after:]
-    payload, blocks = rest[-2:]
-    out = coarse[...]
-    for at, part in halo_products(place, spot, visits, weights, near, far, blocks):
-        out -= joined(dot_nt(stacked(part * agg_weights[:, at]), table[:, at]))
-    half = out.shape[0] // 2
+    half = rows // 2
     message = jnp.concatenate([out[:half, :64], out[half:, :64]], axis=1)
-    if len(rest) == 3:
-        message = jnp.concatenate([message, rest[0][...]], axis=0)
     for i in range(payload.shape[0]):
         payload[i] = message
+    if edges:
+        edge_weights, edge_table = rest[1:3]
+        base = place[4]
+        up = place[6]
+        low = jnp.where(up == 1, far[rows:, :], near[rows:, :])
+        high = jnp.where(up == 1, near[rows:, :], far[rows:, :])
+        edge_weights[...] = jnp.concatenate([low[0:1, :], high[0:1, :]], axis=1)
+        numbers = jnp.concatenate(
+            [
+                low[1:2, :].astype(jnp.int32) + (base - 64),
+                high[1:2, :].astype(jnp.int32) + (base + 64),
+            ],
+            axis=1,
+        )
+        edge_table[...] = onehot_by_lane(numbers, edge_table.shape[0])
 
 
 def coarse_kernel(
-    place, ccolumns, columns, gathered, cscale, cpacked, own_start, near, far,
-    group_rhs, scale, diagonal, packed, wide_weights, raise_table, fine_start, fine_weights,
-    fine_table, picks, *rest,
-):
-    blocks, current = rest[-2:]
-    fine_next, near_out, far_out = rest[:3]
+    place, ccolumns, columns, gathered, cscale, cpacked, own_start, far, near,
+    group_rhs, scale, diagonal, packed, group_weights, raise_table, edge_weights, edge_table,
+    fine_start, fine_weights, fine_table, picks, fine_next, near_out, far_out, blocks, current,
+):
     lanes = lax.broadcasted_iota(jnp.int32, (16, TILE), 1)
 
     def block(t):
@@ -431,11 +428,6 @@
         bottom = jnp.where(lanes < 64, pltpu.roll(first, 64, 1), second)
         return jnp.concatenate([top, bottom], axis=0)
 
-    if len(rest) == 6:
-        sums = gathered[0, 16:24, :]
-        for i in range(1, gathered.shape[0]):
-            sums += gathered[i, 16:24, :]
-        rest[3][...] = spread_rows(sums, 2)
     solved = []
     for t in range(2):
         row = place[2 + t]
@@ -447,17 +439,17 @@
         iterate = cscale[row] * mine
         solved.append(iterate + cscale[row] * (mine - joined(acc)))
     pair = jnp.concatenate(solved, axis=1)
-    raised = select_nn(pair, raise_table[...]) * wide_weights[...]
-    length = own_start.shape[1]
+    rows, length = own_start.shape
     half = near.shape[1]
-    now = own_start[...] + raised[:, :length]
+    now = own_start[...] + select_nn(pair, raise_table[...]) * group_weights[...]
+    raised = select_nn(pair, edge_table[...]) * edge_weights[...]
     current[...] = now
     fill_blocks(blocks, now)
     up = place[6]
-    low = jnp.where(up == 1, far[...], near[...])
-    high = jnp.where(up == 1, near[...], far[...])
-    fill_blocks(blocks, low + raised[:, length : length + half], length // TILE)
-    fill_blocks(blocks, high + raised[:, length + half :], (length + half) // TILE)
+    low = jnp.where(up == 1, far[:rows], near[:rows])
+    high = jnp.where(up == 1, near[:rows], far[:rows])
+    fill_blocks(blocks, low + raised[:, :half], length // TILE)
+    fill_blocks(blocks, high + raised[:, half:], (length + half) // TILE)
     member = place[1]
     iterate_rows = []
     for j in range(2):
@@ -488,7 +480,7 @@
 
 
 def smooth_kernel(
-    place, visits, weights, inner, inner_out, near, far, scale, picks,
+    place, visits, weights, inner, inner_out, far, near, scale, picks,
     smoothed, near_out, far_out, blocks,
 ):
     smoothed[...] = inner[...]
@@ -516,7 +508,7 @@
 
 
 def image_kernel(
-    place, visits, weights, inner, inner_out, inner_sums, near, far, scale, value, picks,
+    place, visits, weights, inner, inner_out, inner_sums, far, near, scale, value, picks,
     product, start, near_out, far_out, sums, blocks,
 ):
     product[...] = inner[...]
@@ -557,7 +549,7 @@
 
 
 def last_kernel(
-    place, visits, weights, inner, inner_sums, first_sums, near, far, value, second,
+    place, visits, weights, inner, inner_sums, first_sums, far, near, value, second,
     image, copies, blocks,
 ):
     image[...] = inner[...]
@@ -698,8 +690,8 @@
         (fine_columns, fine_tiles, fine_groups), smem=(0,), smem_outs=(2,),
     )
 
-    (group_scale, group_diagonal, group_packed, group_picks, group_table, coarse_scale,
-     coarse_packed, edge_near, edge_far, group_visits, group_columns, coarse_columns) = run(
+    (group_scale, group_diagonal, group_packed, group_picks, group_table, raise_table,
+     edge_near, edge_far, group_visits, group_columns) = run(
         group_setup_kernel, "group_setup",
         [
             line,
@@ -707,31 +699,35 @@
             shape((3 * group_blocks + 1, 2 * TILE, TILE), BF16),
             shape((group_length, 2 * group_half), BF16),
             shape((TILE, group_length), BF16),
-            shape((coarse_blocks, 1, TILE)),
-            shape((6, 2 * TILE, TILE), BF16),
+            shape((2 * TILE, group_length), BF16),
             shape((8, group_half)),
             shape((8, group_half)),
             scalars(4 * group_halo),
             pltpu.SMEM(group_columns.shape, jnp.int32),
-            pltpu.SMEM(coarse_columns.shape, jnp.int32),
         ],
-        (place, group_columns, group_tiles, group_sends, group_weights, group_groups,
-         coarse_columns, coarse_tiles),
-        smem=(0, 1, 6), smem_outs=(9, 10, 11), hbm_args=(2, 7),
-        scratch=[pltpu.VMEM(group_tiles.shape, F32), pltpu.VMEM(coarse_tiles.shape, F32),
-                 pltpu.VMEM((1, coarse_blocks * TILE), F32),
-                 pltpu.SemaphoreType.DMA((CHUNKS,)), pltpu.SemaphoreType.DMA((CHUNKS,))],
-    )
-    edge_near, edge_far = neighbours(edge_near, edge_far, GRP)
-    wide_weights, raise_table = run(
-        group_edges_kernel, "group_edges",
-        [shape((1, group_length + 2 * group_half)),
-         shape((2 * TILE, group_length + 2 * group_half), BF16)],
-        (place, group_weights, group_groups, edge_near, edge_far), smem=(0,),
-    )
-
-    def vcycle(source, fine_start, near, far, extra, first_after=(), second_after=()):
-        carried = () if extra is None else (extra,)
+        (place, group_columns, group_tiles, group_sends, group_weights, group_groups),
+        smem=(0, 1), smem_outs=(8, 9), hbm_args=(2,),
+        scratch=[pltpu.VMEM(group_tiles.shape, F32), pltpu.SemaphoreType.DMA((CHUNKS,))],
+    )
+    facts = (edge_near, edge_far)
+    def coarse_parts(after):
+        return run(
+            coarse_setup_kernel, "coarse_setup",
+            [
+                shape((coarse_blocks, 1, TILE)),
+                shape((6, 2 * TILE, TILE), BF16),
+                pltpu.SMEM(coarse_columns.shape, jnp.int32),
+            ],
+            (place, coarse_columns, coarse_tiles, after), smem=(0, 1), smem_outs=(2,),
+            hbm_args=(2,),
+            scratch=[pltpu.VMEM(coarse_tiles.shape, F32),
+                     pltpu.VMEM((1, coarse_blocks * TILE), F32),
+                     pltpu.SemaphoreType.DMA((CHUNKS,))],
+        )
+
+    kept = {}
+
+    def vcycle(source, fine_start, near, far, edges, held):
         coarse = run(
             inner_restrict_kernel, "inner_restrict", [shape((rhs, fine_count))],
             (fine_columns, fine_packed, fine_diagonal, fine_start, source, fine_weights,
@@ -739,39 +735,46 @@
             smem=(0,), scratch=[block_scratch(fine_blocks + fine_halo), pltpu.VMEM((rhs, length), F32)],
         )[0]
         lowered = run(
-            functools.partial(restrict_kernel, spot=5, after=len(first_after)), "restrict",
-            [shape((members, rhs + 8 * len(carried), fine_count))],
-            (place, fine_visits, fine_packed, coarse, near, far, fine_weights, fine_table)
-            + first_after + carried,
+            functools.partial(restrict_kernel, spot=5, after=len(held)), "restrict",
+            [shape((members, rhs, fine_count))],
+            (place, fine_visits, fine_packed, coarse, far, near, fine_weights, fine_table)
+            + held,
             smem=(0, 1), scratch=[block_scratch(fine_halo)],
         )[0]
         gathered = exchanged(lowered, MEM)
-        group_rhs, group_start, near, far, *carried = run(
-            group_start_kernel, "group_start",
-            [field, field, group_edge, group_edge] + [shape((8, TILE)) for _ in carried],
-            (gathered, group_scale, group_picks),
+        extra = facts if edges is None else ()
+        message = shape((rhs + 8 * bool(extra), group_half))
+        group_rhs, group_start, near, far = run(
+            group_start_kernel, "group_start", [field, field, message, message],
+            (gathered, group_scale, group_picks) + extra,
         )
         g_near, g_far = neighbours(near, far, GRP)
+        if edges is None:
+            kept["coarse"] = coarse_parts(near)
+        coarse_scale, coarse_packed, coarse_cols = kept["coarse"]
         coarse = run(
             inner_restrict_kernel, "group_inner", [shape((rhs, TILE))],
             (group_columns, group_packed, group_diagonal, group_start, group_rhs,
              group_weights, group_table),
             smem=(0,), scratch=[block_scratch(group_blocks + group_halo), pltpu.VMEM((rhs, length), F32)],
         )[0]
-        payload = run(
-            functools.partial(group_restrict_kernel, spot=6, after=len(second_after)),
-            "group_restrict",
-            [shape((group_total, 16 + 8 * len(carried), TILE))],
-            (place, group_visits, group_packed, coarse, g_near, g_far, group_weights,
-             group_table) + second_after + tuple(carried),
+        payload, *made = run(
+            functools.partial(group_restrict_kernel, edges=edges is None), "group_restrict",
+            [shape((group_total, 16, TILE))]
+            + ([shape((1, 2 * group_half)), shape((2 * TILE, 2 * group_half), BF16)]
+               if edges is None else []),
+            (place, group_visits, group_packed, coarse, g_far, g_near, group_weights,
+             group_table) + ((coarse_scale,) if edges is None else ()),
             smem=(0, 1), scratch=[block_scratch(group_halo)],
-        )[0]
+        )
+        edges = tuple(made) if edges is None else edges
         gathered = exchanged(payload, GRP)
-        fine_next, near, far, *totals = run(
-            coarse_kernel, "coarse", [field, edge, edge] + [small for _ in carried],
-            (place, coarse_columns, group_columns, gathered, coarse_scale, coarse_packed,
-             group_start, g_near, g_far, group_rhs, group_scale, group_diagonal, group_packed,
-             wide_weights, raise_table, fine_start, fine_weights, fine_table, fine_picks),
+        fine_next, near, far = run(
+            coarse_kernel, "coarse", [field, edge, edge],
+            (place, coarse_cols, group_columns, gathered, coarse_scale, coarse_packed,
+             group_start, g_far, g_near, group_rhs, group_scale, group_diagonal, group_packed,
+             group_weights, raise_table, *edges, fine_start, fine_weights, fine_table,
+             fine_picks),
             smem=(0, 1, 2),
             scratch=[block_scratch(group_blocks + group_halo), pltpu.VMEM((rhs, length), F32)],
         )
@@ -784,15 +787,13 @@
         )
         smoothed, near, far = run(
             smooth_kernel, "smooth", [field, edge, edge],
-            (place, fine_visits, fine_packed, inside, out, near, far, fine_scale, fine_picks),
+            (place, fine_visits, fine_packed, inside, out, far, near, fine_scale, fine_picks),
             smem=(0, 1), scratch=[block_scratch(fine_halo)],
         )
         near, far = neighbours(near, far, ALL)
-        return smoothed, near, far, totals
-
-    value, near, far, _ = vcycle(
-        right_side, fine_start, near, far, None, (wide_weights,)
-    )
+        return smoothed, near, far, edges
+
+    value, near, far, edges = vcycle(right_side, fine_start, near, far, None, (edge_near,))
     inside, out, sums = run(
         inner_image_kernel, "inner_image", [field, picked, small],
         (fine_columns, fine_packed, fine_diagonal, value, fine_scale, right_side, fine_picks),
@@ -800,12 +801,12 @@
     )
     product, start, near, far, sums = run(
         image_kernel, "image", [field, field, edge, edge, small],
-        (place, fine_visits, fine_packed, inside, out, sums, near, far, fine_scale, value,
+        (place, fine_visits, fine_packed, inside, out, sums, far, near, fine_scale, value,
          fine_picks),
         smem=(0, 1), scratch=[block_scratch(fine_halo)],
     )
     near, far = neighbours(near, far, ALL)
-    second, near, far, _ = vcycle(product, start, near, far, None)
+    second, near, far, _ = vcycle(product, start, near, far, edges, ())
     inside, more = run(
         inner_last_kernel, "inner_last", [field, small],
         (fine_columns, fine_packed, fine_diagonal, second, right_side, value, product),
@@ -813,7 +814,7 @@
     )
     image, copies = run(
         last_kernel, "last", [field, shape((members, 8, TILE))],
-        (place, fine_visits, fine_packed, inside, more, sums, near, far, value, second),
+        (place, fine_visits, fine_packed, inside, more, sums, far, near, value, second),
         smem=(0, 1), scratch=[block_scratch(fine_halo)],
     )
     copies = run(

time: 181 us -> 176 us (0.972)
  blocking collectives: 111 us -> 104 us
  waiting for transfers between devices: 6.62 us -> 0.83 us
  starting transfers between devices: 31.8 us -> 36.7 us
  Pallas kernels: 29.7 us -> 31.7 us
    ppermute x9 -> x8, starting transfers between devices: 16 us -> 27.7 us  [neighbours(): far_in = lax.ppermute(far_out, axes, far)]
    ppermute x9 -> x8, starting transfers between devices: 15.8 us -> 8.97 us  [neighbours(): return (lax.ppermute(near_out, axes, near), far_in)]
    all_to_all x6, blocking collectives: 111 us -> 104 us  [exchanged(): return lax.all_to_all(copies, axes, split_axis=0, concat_axis=0, tiled=True)]
    ppermute x9 -> x8, waiting for transfers between devices: 6.06 us -> 0.81 us  [neighbours(): far_in = lax.ppermute(far_out, axes, far)]
    pallas_call x26, Pallas kernels: 29.7 us -> 31.7 us  [run(): pl.pallas_call(kernel, name=name, out_shape=tuple(outs), in_specs=specs,...]
  transfers between devices with their start and end apart: 18 -> 16, of which waited for: 6 -> 3; matrix products, arithmetic and copies ran while one was open for 0% -> 0% of each run, Pallas kernels for 10% -> 12%
where the time goes in v3:
time: 176 us; the launch traced here: 175 us
  blocking collectives  104 us (59%)
  starting transfers between devices  36.7 us (21%)
  Pallas kernels  31.7 us (18%)
    all_to_all x6, blocking collectives, exchanged(): return lax.all_to_all(copies, axes, split_axis=0, concat_axis=0, tiled=True)  104 us
    pallas_call x26, Pallas kernels, run(): pl.pallas_call(kernel, name=name, out_shape=tuple(outs), in_specs=specs,...  31.7 us
    ppermute x8, starting transfers between devices, neighbours(): far_in = lax.ppermute(far_out, axes, far)  27.7 us
    ppermute x8, starting transfers between devices, neighbours(): return (lax.ppermute(near_out, axes, near), far_in)  8.97 us
  transfers between devices with their start and end apart: 16, of which 3 were waited for; matrix products, arithmetic and copies ran while one was open for 0% of the time, Pallas kernels for 12%

profile of v3, /device:TPU:1, one launch (start us, length us, event | category | flops | bytes accessed | tf_op | source)
XLA Modules:
  0.0 175.1 jit_solution(15208986683961661717)
XLA Ops:
  1.4 3.1 %first.1 = (f32[1,2048]{1,0:T(1,128)S(1)}, f32[1,2048]{1,0:T(1,128)S(1)}, f32[32,2048]{1,0:T(8,128)S(1)}, f32[32,256]{1,0:T(8,128)S(1)}, f32[32,256]{1,0:T(8,128...) custom-call(s32[7]{0:T(128)S(1)} %stack.31.place, ...), custom_call_target="tpu_custom_call" | custom-call | flops 4000000000 | bytes 4000000 | tf_op jit(solution)/shard_map/first/pallas_call | solution.py:46
  4.6 4.6 %collective-permute-start = (f32[32,256]{1,0:T(8,128)S(1)}, f32[32,256]{1,0:T(8,128)S(1)}, u32[]{:S(2)}, u32[]{:S(2)}) collective-permute-start(f32[32,256]{1,0:T(8,128)S(1)} %get-tuple-element.83), channel_id=1, source_target_pairs={{1,2},{3,4},{5,6},{7,8},{9,10},{11,12},{13,14},{15,16},{17,18},{19... | collective-permute-start | bytes 98312 | tf_op jit(solution)/shard_map/ppermute | solution.py:603
  10.4 1.6 inner_restrict.2.coarse
  12.1 4.3 %group_setup.1 = (f32[1,2048]{1,0:T(1,128)S(1)}, f32[1,2048]{1,0:T(1,128)S(1)}, bf16[49,256,128]{2,1,0:T(8,128)(2,1)S(1)}, bf16[2048,256]{1,0:T(8,128)(2,1)S(1)}...) custom-call(s32[7]{0:T(128)S(4)} %get-tuple-element.72.place, ...), custom_call_target="tpu_custom_call" | custom-call | flops 4000000000 | bytes 4000000 | tf_op jit(solution)/shard_map/group_setup/pallas_call | solution.py:46
  16.9 10.9 %all_to_all.30.gathered = f32[8,32,256]{2,1,0:T(8,128)S(1)} all-to-all(f32[8,32,256]{2,1,0:T(8,128)S(1)} %restrict.2), channel_id=1, replica_groups=mesh['grp_0'=8,'grp_1'=4,'mem_0'=4,'mem_1'=2] {'mem_0','mem_1'}, dimensions={0} | all-to-all | bytes 524288 | tf_op jit(solution)/shard_map/all_to_all | solution.py:608
  28.8 3.7 %collective-permute-start.3 = (f32[40,128]{1,0:T(8,128)S(1)}, f32[40,128]{1,0:T(8,128)S(1)}, u32[]{:S(2)}, u32[]{:S(2)}) collective-permute-start(f32[40,128]{1,0:T(8,128)S(1)} %get-tuple-element.92.after), channel_id=1, source_target_pairs={{0,8},{8,0},{16,24},{24,16},{32,40},{40,32},{48,56},{56,48},{64,72... | collective-permute-start | bytes 61448 | tf_op jit(solution)/shard_map/ppermute | solution.py:604
  32.5 2.7 %coarse_setup.1 = (f32[16,1,128]{2,1,0:T(1,128)S(1)}, bf16[6,256,128]{2,1,0:T(8,128)(2,1)S(1)}, s32[3,16]{1,0:T(4,128)S(4)}) custom-call(s32[7]{0:T(128)S(4)} %get-tuple-element.72.place, s32[3,16]{1,0:T(4,128)S(1)} %bitcast.16, f32[16,3,128,128]{3,2,1,0:T(8,128)} %ctiles_hbm.1, f32[40,128]{1,0:T(8,128)S(1)} %get-tuple-element.92.after), custom_call_target="tpu_custom_call" | custom-call | flops 4000000000 | bytes 4000000 | tf_op jit(solution)/shard_map/coarse_setup/pallas_call | solution.py:46
  35.2 1.5 group_inner.2.coarse
  37.1 22.2 %all_to_all.31.gathered = f32[32,16,128]{2,1,0:T(8,128)S(1)} all-to-all(f32[32,16,128]{2,1,0:T(8,128)S(1)} %get-tuple-element.103), channel_id=1, replica_groups=mesh['grp_0'=8,'grp_1'=4,'mem_0'=4,'mem_1'=2] {'grp_0','grp_1'}, dimensions={0} | all-to-all | bytes 524288 | tf_op jit(solution)/shard_map/all_to_all | solution.py:608
  60.8 5.9 %collective-permute-start.4 = (f32[32,256]{1,0:T(8,128)S(1)}, f32[32,256]{1,0:T(8,128)S(1)}, u32[]{:S(2)}, u32[]{:S(2)}) collective-permute-start(f32[32,256]{1,0:T(8,128)S(1)} %get-tuple-element.113), channel_id=1, source_target_pairs={{1,2},{3,4},{5,6},{7,8},{9,10},{11,12},{13,14},{15,16},{17,18},{19... | collective-permute-start | bytes 98312 | tf_op jit(solution)/shard_map/ppermute | solution.py:603
  66.9 1.6 inner_smooth.2
  69.0 3.3 %collective-permute-start.6 = (f32[32,256]{1,0:T(8,128)S(1)}, f32[32,256]{1,0:T(8,128)S(1)}, u32[]{:S(2)}, u32[]{:S(2)}) collective-permute-start(f32[32,256]{1,0:T(8,128)S(1)} %get-tuple-element.119), channel_id=1, source_target_pairs={{1,2},{3,4},{5,6},{7,8},{9,10},{11,12},{13,14},{15,16},{17,18},{19... | collective-permute-start | bytes 98312 | tf_op jit(solution)/shard_map/ppermute | solution.py:603
  72.4 1.7 inner_image.1
  74.7 3.3 %collective-permute-start.8 = (f32[32,256]{1,0:T(8,128)S(1)}, f32[32,256]{1,0:T(8,128)S(1)}, u32[]{:S(2)}, u32[]{:S(2)}) collective-permute-start(f32[32,256]{1,0:T(8,128)S(1)} %get-tuple-element.123), channel_id=1, source_target_pairs={{1,2},{3,4},{5,6},{7,8},{9,10},{11,12},{13,14},{15,16},{17,18},{19... | collective-permute-start | bytes 98312 | tf_op jit(solution)/shard_map/ppermute | solution.py:603
  78.1 1.6 inner_restrict.3.coarse
  80.4 13.9 %all_to_all.32.gathered = f32[8,32,256]{2,1,0:T(8,128)S(1)} all-to-all(f32[8,32,256]{2,1,0:T(8,128)S(1)} %restrict.3), channel_id=1, replica_groups=mesh['grp_0'=8,'grp_1'=4,'mem_0'=4,'mem_1'=2] {'mem_0','mem_1'}, dimensions={0} | all-to-all | bytes 524288 | tf_op jit(solution)/shard_map/all_to_all | solution.py:608
  95.3 4.5 %collective-permute-start.11 = (f32[32,128]{1,0:T(8,128)S(1)}, f32[32,128]{1,0:T(8,128)S(1)}, u32[]{:S(2)}, u32[]{:S(2)}) collective-permute-start(f32[32,128]{1,0:T(8,128)S(1)} %get-tuple-element.128), channel_id=1, source_target_pairs={{0,8},{8,0},{16,24},{24,16},{32,40},{40,32},{48,56},{56,48},{64,72... | collective-permute-start | bytes 49160 | tf_op jit(solution)/shard_map/ppermute | solution.py:604
  99.8 1.4 group_inner.3.coarse
  101.7 26.1 %all_to_all.33.gathered = f32[32,16,128]{2,1,0:T(8,128)S(1)} all-to-all(f32[32,16,128]{2,1,0:T(8,128)S(1)} %group_restrict.3), channel_id=1, replica_groups=mesh['grp_0'=8,'grp_1'=4,'mem_0'=4,'mem_1'=2] {'grp_0','grp_1'}, dimensions={0} | all-to-all | bytes 524288 | tf_op jit(solution)/shard_map/all_to_all | solution.py:608
  129.2 5.9 %collective-permute-start.12 = (f32[32,256]{1,0:T(8,128)S(1)}, f32[32,256]{1,0:T(8,128)S(1)}, u32[]{:S(2)}, u32[]{:S(2)}) collective-permute-start(f32[32,256]{1,0:T(8,128)S(1)} %get-tuple-element.132), channel_id=1, source_target_pairs={{1,2},{3,4},{5,6},{7,8},{9,10},{11,12},{13,14},{15,16},{17,18},{19... | collective-permute-start | bytes 98312 | tf_op jit(solution)/shard_map/ppermute | solution.py:603
  135.2 1.6 inner_smooth.3
  137.3 3.5 %collective-permute-start.14 = (f32[32,256]{1,0:T(8,128)S(1)}, f32[32,256]{1,0:T(8,128)S(1)}, u32[]{:S(2)}, u32[]{:S(2)}) collective-permute-start(f32[32,256]{1,0:T(8,128)S(1)} %get-tuple-element.138), channel_id=1, source_target_pairs={{1,2},{3,4},{5,6},{7,8},{9,10},{11,12},{13,14},{15,16},{17,18},{19... | collective-permute-start | bytes 98312 | tf_op jit(solution)/shard_map/ppermute | solution.py:603
  143.0 10.1 %all_to_all.34.parts = f32[8,8,128]{2,1,0:T(8,128)S(1)} all-to-all(f32[8,8,128]{2,1,0:T(8,128)S(1)} %get-tuple-element.140), channel_id=1, replica_groups=mesh['grp_0'=8,'grp_1'=4,'mem_0'=4,'mem_1'=2] {'mem_0','mem_1'}, dimensions={0} | all-to-all | bytes 65536 | tf_op jit(solution)/shard_map/all_to_all | solution.py:608
  153.0 20.9 %all_to_all.35.parts = f32[32,8,128]{2,1,0:T(8,128)S(1)} all-to-all(f32[32,8,128]{2,1,0:T(8,128)S(1)} %sum_copies.1), channel_id=1, replica_groups=mesh['grp_0'=8,'grp_1'=4,'mem_0'=4,'mem_1'=2] {'grp_0','grp_1'}, dimensions={0} | all-to-all | bytes 262144 | tf_op jit(solution)/shard_map/all_to_all | solution.py:608
  (47 shorter events, 14.3 us)
Async XLA Ops:
  0.8 0.7 copy-start
  4.6 11.8 %collective-permute-start = (f32[32,256]{1,0:T(8,128)S(1)}, f32[32,256]{1,0:T(8,128)S(1)}, u32[]{:S(2)}, u32[]{:S(2)}) collective-permute-start(f32[32,256]{1,0:T(8,128)S(1)} %get-tuple-element.83), channel_id=1, source_target_pairs={{1,2},{3,4},{5,6},{7,8},{9,10},{11,12},{13,14},{15,16},{17,18},{19... | collective-permute-start | bytes 98312 | tf_op jit(solution)/shard_map/ppermute | solution.py:603
  9.1 7.2 %collective-permute-start.1 = (f32[32,256]{1,0:T(8,128)S(1)}, f32[32,256]{1,0:T(8,128)S(1)}, u32[]{:S(2)}, u32[]{:S(2)}) collective-permute-start(f32[32,256]{1,0:T(8,128)S(1)} %get-tuple-element.84), channel_id=1, source_target_pairs={{0,1},{1,0},{2,3},{3,2},{4,5},{5,4},{6,7},{7,6},{8,9},{9,8},{10,11... | collective-permute-start | bytes 98312 | tf_op jit(solution)/shard_map/ppermute | solution.py:604
  10.4 1.6 copy-start.1
  27.8 4.7 %copy-start.2 = (s32[16,3]{0,1:T(4,128)S(1)}, s32[16,3]{0,1:T(4,128)}, u32[]{:S(2)}) copy-start(s32[16,3]{0,1:T(4,128)} %param.25) | copy-start | bytes 580
  28.1 8.6 %collective-permute-start.2 = (f32[40,128]{1,0:T(8,128)S(1)}, f32[40,128]{1,0:T(8,128)S(1)}, u32[]{:S(2)}, u32[]{:S(2)}) collective-permute-start(f32[40,128]{1,0:T(8,128)S(1)} %get-tuple-element.101), channel_id=1, source_target_pairs={{8,16},{24,32},{40,48},{56,64},{72,80},{88,96},{104,112},{120,128}... | collective-permute-start | bytes 61448 | tf_op jit(solution)/shard_map/ppermute | solution.py:603
  28.8 7.9 %collective-permute-start.3 = (f32[40,128]{1,0:T(8,128)S(1)}, f32[40,128]{1,0:T(8,128)S(1)}, u32[]{:S(2)}, u32[]{:S(2)}) collective-permute-start(f32[40,128]{1,0:T(8,128)S(1)} %get-tuple-element.92.after), channel_id=1, source_target_pairs={{0,8},{8,0},{16,24},{24,16},{32,40},{40,32},{48,56},{56,48},{64,72... | collective-permute-start | bytes 61448 | tf_op jit(solution)/shard_map/ppermute | solution.py:604
  60.8 7.8 %collective-permute-start.4 = (f32[32,256]{1,0:T(8,128)S(1)}, f32[32,256]{1,0:T(8,128)S(1)}, u32[]{:S(2)}, u32[]{:S(2)}) collective-permute-start(f32[32,256]{1,0:T(8,128)S(1)} %get-tuple-element.113), channel_id=1, source_target_pairs={{1,2},{3,4},{5,6},{7,8},{9,10},{11,12},{13,14},{15,16},{17,18},{19... | collective-permute-start | bytes 98312 | tf_op jit(solution)/shard_map/ppermute | solution.py:603
  66.6 1.9 %collective-permute-start.5 = (f32[32,256]{1,0:T(8,128)S(1)}, f32[32,256]{1,0:T(8,128)S(1)}, u32[]{:S(2)}, u32[]{:S(2)}) collective-permute-start(f32[32,256]{1,0:T(8,128)S(1)} %get-tuple-element.114), channel_id=1, source_target_pairs={{0,1},{1,0},{2,3},{3,2},{4,5},{5,4},{6,7},{7,6},{8,9},{9,8},{10,11... | collective-permute-start | bytes 98312 | tf_op jit(solution)/shard_map/ppermute | solution.py:604
  69.0 5.2 %collective-permute-start.6 = (f32[32,256]{1,0:T(8,128)S(1)}, f32[32,256]{1,0:T(8,128)S(1)}, u32[]{:S(2)}, u32[]{:S(2)}) collective-permute-start(f32[32,256]{1,0:T(8,128)S(1)} %get-tuple-element.119), channel_id=1, source_target_pairs={{1,2},{3,4},{5,6},{7,8},{9,10},{11,12},{13,14},{15,16},{17,18},{19... | collective-permute-start | bytes 98312 | tf_op jit(solution)/shard_map/ppermute | solution.py:603
  72.3 1.9 %collective-permute-start.7 = (f32[32,256]{1,0:T(8,128)S(1)}, f32[32,256]{1,0:T(8,128)S(1)}, u32[]{:S(2)}, u32[]{:S(2)}) collective-permute-start(f32[32,256]{1,0:T(8,128)S(1)} %get-tuple-element.120), channel_id=1, source_target_pairs={{0,1},{1,0},{2,3},{3,2},{4,5},{5,4},{6,7},{7,6},{8,9},{9,8},{10,11... | collective-permute-start | bytes 98312 | tf_op jit(solution)/shard_map/ppermute | solution.py:604
  74.7 5.2 %collective-permute-start.8 = (f32[32,256]{1,0:T(8,128)S(1)}, f32[32,256]{1,0:T(8,128)S(1)}, u32[]{:S(2)}, u32[]{:S(2)}) collective-permute-start(f32[32,256]{1,0:T(8,128)S(1)} %get-tuple-element.123), channel_id=1, source_target_pairs={{1,2},{3,4},{5,6},{7,8},{9,10},{11,12},{13,14},{15,16},{17,18},{19... | collective-permute-start | bytes 98312 | tf_op jit(solution)/shard_map/ppermute | solution.py:603
  78.0 1.9 %collective-permute-start.9 = (f32[32,256]{1,0:T(8,128)S(1)}, f32[32,256]{1,0:T(8,128)S(1)}, u32[]{:S(2)}, u32[]{:S(2)}) collective-permute-start(f32[32,256]{1,0:T(8,128)S(1)} %get-tuple-element.124), channel_id=1, source_target_pairs={{0,1},{1,0},{2,3},{3,2},{4,5},{5,4},{6,7},{7,6},{8,9},{9,8},{10,11... | collective-permute-start | bytes 98312 | tf_op jit(solution)/shard_map/ppermute | solution.py:604
  94.6 6.7 %collective-permute-start.10 = (f32[32,128]{1,0:T(8,128)S(1)}, f32[32,128]{1,0:T(8,128)S(1)}, u32[]{:S(2)}, u32[]{:S(2)}) collective-permute-start(f32[32,128]{1,0:T(8,128)S(1)} %get-tuple-element.127), channel_id=1, source_target_pairs={{8,16},{24,32},{40,48},{56,64},{72,80},{88,96},{104,112},{120,128}... | collective-permute-start | bytes 49160 | tf_op jit(solution)/shard_map/ppermute | solution.py:603
  95.3 6.0 %collective-permute-start.11 = (f32[32,128]{1,0:T(8,128)S(1)}, f32[32,128]{1,0:T(8,128)S(1)}, u32[]{:S(2)}, u32[]{:S(2)}) collective-permute-start(f32[32,128]{1,0:T(8,128)S(1)} %get-tuple-element.128), channel_id=1, source_target_pairs={{0,8},{8,0},{16,24},{24,16},{32,40},{40,32},{48,56},{56,48},{64,72... | collective-permute-start | bytes 49160 | tf_op jit(solution)/shard_map/ppermute | solution.py:604
  129.2 7.7 %collective-permute-start.12 = (f32[32,256]{1,0:T(8,128)S(1)}, f32[32,256]{1,0:T(8,128)S(1)}, u32[]{:S(2)}, u32[]{:S(2)}) collective-permute-start(f32[32,256]{1,0:T(8,128)S(1)} %get-tuple-element.132), channel_id=1, source_target_pairs={{1,2},{3,4},{5,6},{7,8},{9,10},{11,12},{13,14},{15,16},{17,18},{19... | collective-permute-start | bytes 98312 | tf_op jit(solution)/shard_map/ppermute | solution.py:603
  135.1 1.8 %collective-permute-start.13 = (f32[32,256]{1,0:T(8,128)S(1)}, f32[32,256]{1,0:T(8,128)S(1)}, u32[]{:S(2)}, u32[]{:S(2)}) collective-permute-start(f32[32,256]{1,0:T(8,128)S(1)} %get-tuple-element.133), channel_id=1, source_target_pairs={{0,1},{1,0},{2,3},{3,2},{4,5},{5,4},{6,7},{7,6},{8,9},{9,8},{10,11... | collective-permute-start | bytes 98312 | tf_op jit(solution)/shard_map/ppermute | solution.py:604
  137.3 5.2 %collective-permute-start.14 = (f32[32,256]{1,0:T(8,128)S(1)}, f32[32,256]{1,0:T(8,128)S(1)}, u32[]{:S(2)}, u32[]{:S(2)}) collective-permute-start(f32[32,256]{1,0:T(8,128)S(1)} %get-tuple-element.138), channel_id=1, source_target_pairs={{1,2},{3,4},{5,6},{7,8},{9,10},{11,12},{13,14},{15,16},{17,18},{19... | collective-permute-start | bytes 98312 | tf_op jit(solution)/shard_map/ppermute | solution.py:603
  140.8 1.8 %collective-permute-start.15 = (f32[32,256]{1,0:T(8,128)S(1)}, f32[32,256]{1,0:T(8,128)S(1)}, u32[]{:S(2)}, u32[]{:S(2)}) collective-permute-start(f32[32,256]{1,0:T(8,128)S(1)} %get-tuple-element.139), channel_id=1, source_target_pairs={{0,1},{1,0},{2,3},{3,2},{4,5},{5,4},{6,7},{7,6},{8,9},{9,8},{10,11... | collective-permute-start | bytes 98312 | tf_op jit(solution)/shard_map/ppermute | solution.py:604

commit v4 on v3

--- a/solution.py
+++ b/solution.py
@@ -303,16 +303,13 @@
 
 def group_setup_kernel(
     place, columns, tiles_hbm, sends, weights, groups,
-    scale, diagonal, packed, picks, table, raise_table, edge_near, edge_far, visits,
-    columns_out, tiles, sems,
+    scale, diagonal, tiles, picks, edge_near, edge_far, visits, columns_out, sems,
 ):
     count = tiles.shape[0]
     copies = fetch(tiles_hbm, tiles, sems)
     copy_scalars(columns, columns_out)
     note_visits(columns, visits, count, 2)
     fill_picks(place[6], sends, picks)
-    table[...] = onehot_by_lane(groups[...], table.shape[0])
-    raise_table[...] = onehot_by_lane(groups[...] + place[4], raise_table.shape[0])
     length = weights.shape[1]
     numbers = groups[...].astype(F32)
     lines = lax.broadcasted_iota(jnp.int32, (8, length), 0)
@@ -321,9 +318,13 @@
     for i, copy in enumerate(copies):
         copy.wait()
         diagonal_scale(columns, tiles, scale, diagonal, chunk_rows(i, count))
-        pack_tiles(tiles, packed, chunk_rows(i, count))
+    scale[...] = RELAXATION / scale[...]
+
+
+def group_pack_kernel(tiles, after, packed):
+    count = tiles.shape[0]
+    pack_tiles(tiles, packed, range(count))
     packed[3 * count] = jnp.zeros(packed.shape[1:], BF16)
-    scale[...] = RELAXATION / scale[...]
 
 
 def inner_restrict_kernel(
@@ -366,10 +367,13 @@
 
 
 def coarse_setup_kernel(
-    place, ccolumns, ctiles_hbm, after, cscale, cpacked, ccolumns_out, ctiles, cline, csems
+    place, ccolumns, ctiles_hbm, groups, after, cscale, cpacked, ccolumns_out, table, raise_table,
+    ctiles, cline, csems,
 ):
     copies = fetch(ctiles_hbm, ctiles, csems)
     copy_scalars(ccolumns, ccolumns_out)
+    table[...] = onehot_by_lane(groups[...], table.shape[0])
+    raise_table[...] = onehot_by_lane(groups[...] + place[4], raise_table.shape[0])
     blocks = ctiles.shape[0]
     for i, copy in enumerate(copies):
         copy.wait()
@@ -690,24 +694,22 @@
         (fine_columns, fine_tiles, fine_groups), smem=(0,), smem_outs=(2,),
     )
 
-    (group_scale, group_diagonal, group_packed, group_picks, group_table, raise_table,
-     edge_near, edge_far, group_visits, group_columns) = run(
+    (group_scale, group_diagonal, group_tiles, group_picks, edge_near, edge_far,
+     group_visits, group_columns) = run(
         group_setup_kernel, "group_setup",
         [
             line,
             line,
-            shape((3 * group_blocks + 1, 2 * TILE, TILE), BF16),
+            shape(group_tiles.shape),
             shape((group_length, 2 * group_half), BF16),
-            shape((TILE, group_length), BF16),
-            shape((2 * TILE, group_length), BF16),
             shape((8, group_half)),
             shape((8, group_half)),
             scalars(4 * group_halo),
             pltpu.SMEM(group_columns.shape, jnp.int32),
         ],
         (place, group_columns, group_tiles, group_sends, group_weights, group_groups),
-        smem=(0, 1), smem_outs=(8, 9), hbm_args=(2,),
-        scratch=[pltpu.VMEM(group_tiles.shape, F32), pltpu.SemaphoreType.DMA((CHUNKS,))],
+        smem=(0, 1), smem_outs=(6, 7), hbm_args=(2,),
+        scratch=[pltpu.SemaphoreType.DMA((CHUNKS,))],
     )
     facts = (edge_near, edge_far)
     def coarse_parts(after):
@@ -717,9 +719,11 @@
                 shape((coarse_blocks, 1, TILE)),
                 shape((6, 2 * TILE, TILE), BF16),
                 pltpu.SMEM(coarse_columns.shape, jnp.int32),
+                shape((TILE, group_length), BF16),
+                shape((2 * TILE, group_length), BF16),
             ],
-            (place, coarse_columns, coarse_tiles, after), smem=(0, 1), smem_outs=(2,),
-            hbm_args=(2,),
+            (place, coarse_columns, coarse_tiles, group_groups, after), smem=(0, 1),
+            smem_outs=(2,), hbm_args=(2,),
             scratch=[pltpu.VMEM(coarse_tiles.shape, F32),
                      pltpu.VMEM((1, coarse_blocks * TILE), F32),
                      pltpu.SemaphoreType.DMA((CHUNKS,))],
@@ -751,7 +755,12 @@
         g_near, g_far = neighbours(near, far, GRP)
         if edges is None:
             kept["coarse"] = coarse_parts(near)
-        coarse_scale, coarse_packed, coarse_cols = kept["coarse"]
+            kept["packed"] = run(
+                group_pack_kernel, "group_pack",
+                [shape((3 * group_blocks + 1, 2 * TILE, TILE), BF16)], (group_tiles, near),
+            )[0]
+        group_packed = kept["packed"]
+        coarse_scale, coarse_packed, coarse_cols, group_table, raise_table = kept["coarse"]
         coarse = run(
             inner_restrict_kernel, "group_inner", [shape((rhs, TILE))],
             (group_columns, group_packed, group_diagonal, group_start, group_rhs,

time: 176 us -> 174 us (0.989)
  starting transfers between devices: 36.7 us -> 34 us
  blocking collectives: 104 us -> 106 us
    ppermute x8, starting transfers between devices: 8.97 us -> 6.5 us  [neighbours(): return (lax.ppermute(near_out, axes, near), far_in)]
    pallas_call x26 -> x27, Pallas kernels: 31.7 us -> 31 us  [run(): pl.pallas_call(kernel, name=name, out_shape=tuple(outs), in_specs=specs,...]
  transfers between devices with their start and end apart: 16 -> 16, of which waited for: 3 -> 2; matrix products, arithmetic and copies ran while one was open for 0% -> 0% of each run, Pallas kernels for 12% -> 11%
where the time goes in v4:
time: 174 us; the launch traced here: 173 us
  blocking collectives  106 us (61%)
  starting transfers between devices  34 us (20%)
  Pallas kernels  31 us (18%)
    all_to_all x6, blocking collectives, exchanged(): return lax.all_to_all(copies, axes, split_axis=0, concat_axis=0, tiled=True)  106 us
    pallas_call x27, Pallas kernels, run(): pl.pallas_call(kernel, name=name, out_shape=tuple(outs), in_specs=specs,...  31 us
    ppermute x8, starting transfers between devices, neighbours(): far_in = lax.ppermute(far_out, axes, far)  27.5 us
    ppermute x8, starting transfers between devices, neighbours(): return (lax.ppermute(near_out, axes, near), far_in)  6.5 us
  transfers between devices with their start and end apart: 16, of which 2 were waited for; matrix products, arithmetic and copies ran while one was open for 0% of the time, Pallas kernels for 11%

profile of v4, /device:TPU:1, one launch (start us, length us, event | category | flops | bytes accessed | tf_op | source)
XLA Modules:
  0.0 173.3 jit_solution(6021092969359865365)
XLA Ops:
  1.4 3.1 %first.1 = (f32[1,2048]{1,0:T(1,128)S(1)}, f32[1,2048]{1,0:T(1,128)S(1)}, f32[32,2048]{1,0:T(8,128)S(1)}, f32[32,256]{1,0:T(8,128)S(1)}, f32[32,256]{1,0:T(8,128...) custom-call(s32[7]{0:T(128)S(1)} %stack.31.place, ...), custom_call_target="tpu_custom_call" | custom-call | flops 4000000000 | bytes 4000000 | tf_op jit(solution)/shard_map/first/pallas_call | solution.py:46
  4.6 4.6 %collective-permute-start = (f32[32,256]{1,0:T(8,128)S(1)}, f32[32,256]{1,0:T(8,128)S(1)}, u32[]{:S(2)}, u32[]{:S(2)}) collective-permute-start(f32[32,256]{1,0:T(8,128)S(1)} %get-tuple-element.84), channel_id=1, source_target_pairs={{1,2},{3,4},{5,6},{7,8},{9,10},{11,12},{13,14},{15,16},{17,18},{19... | collective-permute-start | bytes 98312 | tf_op jit(solution)/shard_map/ppermute | solution.py:607
  10.4 2.7 %group_setup.1 = (f32[1,2048]{1,0:T(1,128)S(1)}, f32[1,2048]{1,0:T(1,128)S(1)}, f32[16,3,128,128]{3,2,1,0:T(8,128)S(1)}, bf16[2048,256]{1,0:T(8,128)(2,1)S(1)}, ...) custom-call(s32[7]{0:T(128)S(4)} %get-tuple-element.72.place, ...), custom_call_target="tpu_custom_call" | custom-call | flops 4000000000 | bytes 4000000 | tf_op jit(solution)/shard_map/group_setup/pallas_call | solution.py:46
  13.2 1.6 inner_restrict.2.coarse
  15.3 10.9 %all_to_all.30.gathered = f32[8,32,256]{2,1,0:T(8,128)S(1)} all-to-all(f32[8,32,256]{2,1,0:T(8,128)S(1)} %restrict.2), channel_id=1, replica_groups=mesh['grp_0'=8,'grp_1'=4,'mem_0'=4,'mem_1'=2] {'mem_0','mem_1'}, dimensions={0} | all-to-all | bytes 524288 | tf_op jit(solution)/shard_map/all_to_all | solution.py:612
  29.3 2.7 %coarse_setup.1 = (f32[16,1,128]{2,1,0:T(1,128)S(1)}, bf16[6,256,128]{2,1,0:T(8,128)(2,1)S(1)}, s32[3,16]{1,0:T(4,128)S(4)}, bf16[128,2048]{1,0:T(8,128)(2,1)S(1)}, bf16[256,2048]{1,0:T(8,128)(2,1)S(1)}) custom-call(s32[7]{0:T(128)S(4)} %get-tuple-element.72.place, s32[3,16]{1,0:T(4,128)S(1)} %bitcast.16, f32[16,3,128,128]{3,2,1,0:T(8,128)} %ctiles_hbm.1, ...), custom_call_target="tpu_custom_call" | custom-call | flops 4000000000 | bytes 4000000 | tf_op jit(solution)/shard_map/coarse_setup/pallas_call | solution.py:46
  32.0 1.5 group_inner.2.coarse
  33.9 23.6 %all_to_all.31.gathered = f32[32,16,128]{2,1,0:T(8,128)S(1)} all-to-all(f32[32,16,128]{2,1,0:T(8,128)S(1)} %get-tuple-element.103), channel_id=1, replica_groups=mesh['grp_0'=8,'grp_1'=4,'mem_0'=4,'mem_1'=2] {'grp_0','grp_1'}, dimensions={0} | all-to-all | bytes 524288 | tf_op jit(solution)/shard_map/all_to_all | solution.py:612
  59.0 5.6 %collective-permute-start.4 = (f32[32,256]{1,0:T(8,128)S(1)}, f32[32,256]{1,0:T(8,128)S(1)}, u32[]{:S(2)}, u32[]{:S(2)}) collective-permute-start(f32[32,256]{1,0:T(8,128)S(1)} %get-tuple-element.113), channel_id=1, source_target_pairs={{1,2},{3,4},{5,6},{7,8},{9,10},{11,12},{13,14},{15,16},{17,18},{19... | collective-permute-start | bytes 98312 | tf_op jit(solution)/shard_map/ppermute | solution.py:607
  64.6 1.6 inner_smooth.2
  66.7 3.5 %collective-permute-start.6 = (f32[32,256]{1,0:T(8,128)S(1)}, f32[32,256]{1,0:T(8,128)S(1)}, u32[]{:S(2)}, u32[]{:S(2)}) collective-permute-start(f32[32,256]{1,0:T(8,128)S(1)} %get-tuple-element.119), channel_id=1, source_target_pairs={{1,2},{3,4},{5,6},{7,8},{9,10},{11,12},{13,14},{15,16},{17,18},{19... | collective-permute-start | bytes 98312 | tf_op jit(solution)/shard_map/ppermute | solution.py:607
  70.5 1.6 inner_image.1
  72.6 3.3 %collective-permute-start.8 = (f32[32,256]{1,0:T(8,128)S(1)}, f32[32,256]{1,0:T(8,128)S(1)}, u32[]{:S(2)}, u32[]{:S(2)}) collective-permute-start(f32[32,256]{1,0:T(8,128)S(1)} %get-tuple-element.123), channel_id=1, source_target_pairs={{1,2},{3,4},{5,6},{7,8},{9,10},{11,12},{13,14},{15,16},{17,18},{19... | collective-permute-start | bytes 98312 | tf_op jit(solution)/shard_map/ppermute | solution.py:607
  76.0 1.6 inner_restrict.3.coarse
  78.3 14.1 %all_to_all.32.gathered = f32[8,32,256]{2,1,0:T(8,128)S(1)} all-to-all(f32[8,32,256]{2,1,0:T(8,128)S(1)} %restrict.3), channel_id=1, replica_groups=mesh['grp_0'=8,'grp_1'=4,'mem_0'=4,'mem_1'=2] {'mem_0','mem_1'}, dimensions={0} | all-to-all | bytes 524288 | tf_op jit(solution)/shard_map/all_to_all | solution.py:612
  93.4 4.5 %collective-permute-start.11 = (f32[32,128]{1,0:T(8,128)S(1)}, f32[32,128]{1,0:T(8,128)S(1)}, u32[]{:S(2)}, u32[]{:S(2)}) collective-permute-start(f32[32,128]{1,0:T(8,128)S(1)} %get-tuple-element.128), channel_id=1, source_target_pairs={{0,8},{8,0},{16,24},{24,16},{32,40},{40,32},{48,56},{56,48},{64,72... | collective-permute-start | bytes 49160 | tf_op jit(solution)/shard_map/ppermute | solution.py:608
  97.9 1.5 group_inner.3.coarse
  99.8 26.1 %all_to_all.33.gathered = f32[32,16,128]{2,1,0:T(8,128)S(1)} all-to-all(f32[32,16,128]{2,1,0:T(8,128)S(1)} %group_restrict.3), channel_id=1, replica_groups=mesh['grp_0'=8,'grp_1'=4,'mem_0'=4,'mem_1'=2] {'grp_0','grp_1'}, dimensions={0} | all-to-all | bytes 524288 | tf_op jit(solution)/shard_map/all_to_all | solution.py:612
  126.0 1.4 coarse.3
  127.4 5.9 %collective-permute-start.12 = (f32[32,256]{1,0:T(8,128)S(1)}, f32[32,256]{1,0:T(8,128)S(1)}, u32[]{:S(2)}, u32[]{:S(2)}) collective-permute-start(f32[32,256]{1,0:T(8,128)S(1)} %get-tuple-element.132), channel_id=1, source_target_pairs={{1,2},{3,4},{5,6},{7,8},{9,10},{11,12},{13,14},{15,16},{17,18},{19... | collective-permute-start | bytes 98312 | tf_op jit(solution)/shard_map/ppermute | solution.py:607
  133.4 1.6 inner_smooth.3
  135.5 3.5 %collective-permute-start.14 = (f32[32,256]{1,0:T(8,128)S(1)}, f32[32,256]{1,0:T(8,128)S(1)}, u32[]{:S(2)}, u32[]{:S(2)}) collective-permute-start(f32[32,256]{1,0:T(8,128)S(1)} %get-tuple-element.138), channel_id=1, source_target_pairs={{1,2},{3,4},{5,6},{7,8},{9,10},{11,12},{13,14},{15,16},{17,18},{19... | collective-permute-start | bytes 98312 | tf_op jit(solution)/shard_map/ppermute | solution.py:607
  141.1 10.0 %all_to_all.34.parts = f32[8,8,128]{2,1,0:T(8,128)S(1)} all-to-all(f32[8,8,128]{2,1,0:T(8,128)S(1)} %get-tuple-element.140), channel_id=1, replica_groups=mesh['grp_0'=8,'grp_1'=4,'mem_0'=4,'mem_1'=2] {'mem_0','mem_1'}, dimensions={0} | all-to-all | bytes 65536 | tf_op jit(solution)/shard_map/all_to_all | solution.py:612
  151.2 20.9 %all_to_all.35.parts = f32[32,8,128]{2,1,0:T(8,128)S(1)} all-to-all(f32[32,8,128]{2,1,0:T(8,128)S(1)} %sum_copies.1), channel_id=1, replica_groups=mesh['grp_0'=8,'grp_1'=4,'mem_0'=4,'mem_1'=2] {'grp_0','grp_1'}, dimensions={0} | all-to-all | bytes 262144 | tf_op jit(solution)/shard_map/all_to_all | solution.py:612
  (48 shorter events, 14.9 us)
Async XLA Ops:
  0.8 0.7 copy-start
  4.6 10.2 %collective-permute-start = (f32[32,256]{1,0:T(8,128)S(1)}, f32[32,256]{1,0:T(8,128)S(1)}, u32[]{:S(2)}, u32[]{:S(2)}) collective-permute-start(f32[32,256]{1,0:T(8,128)S(1)} %get-tuple-element.84), channel_id=1, source_target_pairs={{1,2},{3,4},{5,6},{7,8},{9,10},{11,12},{13,14},{15,16},{17,18},{19... | collective-permute-start | bytes 98312 | tf_op jit(solution)/shard_map/ppermute | solution.py:607
  9.1 5.6 %collective-permute-start.1 = (f32[32,256]{1,0:T(8,128)S(1)}, f32[32,256]{1,0:T(8,128)S(1)}, u32[]{:S(2)}, u32[]{:S(2)}) collective-permute-start(f32[32,256]{1,0:T(8,128)S(1)} %get-tuple-element.85), channel_id=1, source_target_pairs={{0,1},{1,0},{2,3},{3,2},{4,5},{5,4},{6,7},{7,6},{8,9},{9,8},{10,11... | collective-permute-start | bytes 98312 | tf_op jit(solution)/shard_map/ppermute | solution.py:608
  9.2 1.2 copy-start.1
  26.5 7.0 %collective-permute-start.3 = (f32[40,128]{1,0:T(8,128)S(1)}, f32[40,128]{1,0:T(8,128)S(1)}, u32[]{:S(2)}, u32[]{:S(2)}) collective-permute-start(f32[40,128]{1,0:T(8,128)S(1)} %get-tuple-element.92.after), channel_id=1, source_target_pairs={{0,8},{8,0},{16,24},{24,16},{32,40},{40,32},{48,56},{56,48},{64,72... | collective-permute-start | bytes 61448 | tf_op jit(solution)/shard_map/ppermute | solution.py:608
  27.7 1.6 copy-start.2
  28.6 4.8 %collective-permute-start.2 = (f32[40,128]{1,0:T(8,128)S(1)}, f32[40,128]{1,0:T(8,128)S(1)}, u32[]{:S(2)}, u32[]{:S(2)}) collective-permute-start(f32[40,128]{1,0:T(8,128)S(1)} %get-tuple-element.101), channel_id=1, source_target_pairs={{8,16},{24,32},{40,48},{56,64},{72,80},{88,96},{104,112},{120,128}... | collective-permute-start | bytes 61448 | tf_op jit(solution)/shard_map/ppermute | solution.py:607
  59.0 7.3 %collective-permute-start.4 = (f32[32,256]{1,0:T(8,128)S(1)}, f32[32,256]{1,0:T(8,128)S(1)}, u32[]{:S(2)}, u32[]{:S(2)}) collective-permute-start(f32[32,256]{1,0:T(8,128)S(1)} %get-tuple-element.113), channel_id=1, source_target_pairs={{1,2},{3,4},{5,6},{7,8},{9,10},{11,12},{13,14},{15,16},{17,18},{19... | collective-permute-start | bytes 98312 | tf_op jit(solution)/shard_map/ppermute | solution.py:607
  64.5 1.8 %collective-permute-start.5 = (f32[32,256]{1,0:T(8,128)S(1)}, f32[32,256]{1,0:T(8,128)S(1)}, u32[]{:S(2)}, u32[]{:S(2)}) collective-permute-start(f32[32,256]{1,0:T(8,128)S(1)} %get-tuple-element.114), channel_id=1, source_target_pairs={{0,1},{1,0},{2,3},{3,2},{4,5},{5,4},{6,7},{7,6},{8,9},{9,8},{10,11... | collective-permute-start | bytes 98312 | tf_op jit(solution)/shard_map/ppermute | solution.py:608
  66.7 5.4 %collective-permute-start.6 = (f32[32,256]{1,0:T(8,128)S(1)}, f32[32,256]{1,0:T(8,128)S(1)}, u32[]{:S(2)}, u32[]{:S(2)}) collective-permute-start(f32[32,256]{1,0:T(8,128)S(1)} %get-tuple-element.119), channel_id=1, source_target_pairs={{1,2},{3,4},{5,6},{7,8},{9,10},{11,12},{13,14},{15,16},{17,18},{19... | collective-permute-start | bytes 98312 | tf_op jit(solution)/shard_map/ppermute | solution.py:607
  70.2 1.9 %collective-permute-start.7 = (f32[32,256]{1,0:T(8,128)S(1)}, f32[32,256]{1,0:T(8,128)S(1)}, u32[]{:S(2)}, u32[]{:S(2)}) collective-permute-start(f32[32,256]{1,0:T(8,128)S(1)} %get-tuple-element.120), channel_id=1, source_target_pairs={{0,1},{1,0},{2,3},{3,2},{4,5},{5,4},{6,7},{7,6},{8,9},{9,8},{10,11... | collective-permute-start | bytes 98312 | tf_op jit(solution)/shard_map/ppermute | solution.py:608
  72.6 5.2 %collective-permute-start.8 = (f32[32,256]{1,0:T(8,128)S(1)}, f32[32,256]{1,0:T(8,128)S(1)}, u32[]{:S(2)}, u32[]{:S(2)}) collective-permute-start(f32[32,256]{1,0:T(8,128)S(1)} %get-tuple-element.123), channel_id=1, source_target_pairs={{1,2},{3,4},{5,6},{7,8},{9,10},{11,12},{13,14},{15,16},{17,18},{19... | collective-permute-start | bytes 98312 | tf_op jit(solution)/shard_map/ppermute | solution.py:607
  75.9 2.0 %collective-permute-start.9 = (f32[32,256]{1,0:T(8,128)S(1)}, f32[32,256]{1,0:T(8,128)S(1)}, u32[]{:S(2)}, u32[]{:S(2)}) collective-permute-start(f32[32,256]{1,0:T(8,128)S(1)} %get-tuple-element.124), channel_id=1, source_target_pairs={{0,1},{1,0},{2,3},{3,2},{4,5},{5,4},{6,7},{7,6},{8,9},{9,8},{10,11... | collective-permute-start | bytes 98312 | tf_op jit(solution)/shard_map/ppermute | solution.py:608
  92.7 6.6 %collective-permute-start.10 = (f32[32,128]{1,0:T(8,128)S(1)}, f32[32,128]{1,0:T(8,128)S(1)}, u32[]{:S(2)}, u32[]{:S(2)}) collective-permute-start(f32[32,128]{1,0:T(8,128)S(1)} %get-tuple-element.127), channel_id=1, source_target_pairs={{8,16},{24,32},{40,48},{56,64},{72,80},{88,96},{104,112},{120,128}... | collective-permute-start | bytes 49160 | tf_op jit(solution)/shard_map/ppermute | solution.py:607
  93.4 6.0 %collective-permute-start.11 = (f32[32,128]{1,0:T(8,128)S(1)}, f32[32,128]{1,0:T(8,128)S(1)}, u32[]{:S(2)}, u32[]{:S(2)}) collective-permute-start(f32[32,128]{1,0:T(8,128)S(1)} %get-tuple-element.128), channel_id=1, source_target_pairs={{0,8},{8,0},{16,24},{24,16},{32,40},{40,32},{48,56},{56,48},{64,72... | collective-permute-start | bytes 49160 | tf_op jit(solution)/shard_map/ppermute | solution.py:608
  127.4 7.6 %collective-permute-start.12 = (f32[32,256]{1,0:T(8,128)S(1)}, f32[32,256]{1,0:T(8,128)S(1)}, u32[]{:S(2)}, u32[]{:S(2)}) collective-permute-start(f32[32,256]{1,0:T(8,128)S(1)} %get-tuple-element.132), channel_id=1, source_target_pairs={{1,2},{3,4},{5,6},{7,8},{9,10},{11,12},{13,14},{15,16},{17,18},{19... | collective-permute-start | bytes 98312 | tf_op jit(solution)/shard_map/ppermute | solution.py:607
  133.3 1.8 %collective-permute-start.13 = (f32[32,256]{1,0:T(8,128)S(1)}, f32[32,256]{1,0:T(8,128)S(1)}, u32[]{:S(2)}, u32[]{:S(2)}) collective-permute-start(f32[32,256]{1,0:T(8,128)S(1)} %get-tuple-element.133), channel_id=1, source_target_pairs={{0,1},{1,0},{2,3},{3,2},{4,5},{5,4},{6,7},{7,6},{8,9},{9,8},{10,11... | collective-permute-start | bytes 98312 | tf_op jit(solution)/shard_map/ppermute | solution.py:608
  135.5 5.2 %collective-permute-start.14 = (f32[32,256]{1,0:T(8,128)S(1)}, f32[32,256]{1,0:T(8,128)S(1)}, u32[]{:S(2)}, u32[]{:S(2)}) collective-permute-start(f32[32,256]{1,0:T(8,128)S(1)} %get-tuple-element.138), channel_id=1, source_target_pairs={{1,2},{3,4},{5,6},{7,8},{9,10},{11,12},{13,14},{15,16},{17,18},{19... | collective-permute-start | bytes 98312 | tf_op jit(solution)/shard_map/ppermute | solution.py:607
  139.0 1.8 %collective-permute-start.15 = (f32[32,256]{1,0:T(8,128)S(1)}, f32[32,256]{1,0:T(8,128)S(1)}, u32[]{:S(2)}, u32[]{:S(2)}) collective-permute-start(f32[32,256]{1,0:T(8,128)S(1)} %get-tuple-element.139), channel_id=1, source_target_pairs={{0,1},{1,0},{2,3},{3,2},{4,5},{5,4},{6,7},{7,6},{8,9},{9,8},{10,11... | collective-permute-start | bytes 98312 | tf_op jit(solution)/shard_map/ppermute | solution.py:608
